TPU v7x, 32 devices: a whole 2x2x4 slice. The times are simulated.
32 devices in a mesh: fsdp: 8 (over y, x, core), tp: 4 (over z).
Axes of the slice: x: 2, y: 2, z: 4, core: 2. Of those that a mesh axis runs over, the one named last changes fastest.
Arguments:
- tokens: bfloat16 [4096, 2048], P(('fsdp', 'tp')), may hold values from -6 to 6
- attention_norm_gain: bfloat16 [2048], P(('fsdp', 'tp')), may hold values from 0.5 to 1.5
- feedforward_norm_gain: bfloat16 [2048], P(('fsdp', 'tp')), may hold values from 0.5 to 1.5
- query_shared_weight: bfloat16 [2048, 2048], P('fsdp', 'tp'), may hold values from -0.125 to 0.125
- key_value_shared_weight: bfloat16 [2048, 512], P(('fsdp', 'tp')), may hold values from -0.125 to 0.125
- output_shared_weight: bfloat16 [2048, 2048], P('tp', 'fsdp'), may hold values from -0.75 to 0.75
- gate_shared_weight: bfloat16 [2048, 16384], P('fsdp', 'tp'), may hold values from -0.125 to 0.125
- up_shared_weight: bfloat16 [2048, 16384], P('fsdp', 'tp'), may hold values from -0.125 to 0.125
- down_shared_weight: bfloat16 [16384, 2048], P('tp', 'fsdp'), may hold values from -0.046875 to 0.046875
- attention_delta_input: bfloat16 [2048, 256], P(('fsdp', 'tp')), may hold values from -0.125 to 0.125
- query_delta_output: bfloat16 [256, 2048], P('fsdp', 'tp'), may hold values from -0.375 to 0.375
- key_value_delta_output: bfloat16 [256, 512], P(('fsdp', 'tp')), may hold values from -0.375 to 0.375
- output_delta_input: bfloat16 [2048, 256], P('tp', 'fsdp'), may hold values from -0.125 to 0.125
- output_delta_output: bfloat16 [256, 2048], P(('fsdp', 'tp')), may hold values from -2 to 2
- feedforward_delta_input: bfloat16 [2048, 256], P(('fsdp', 'tp')), may hold values from -0.125 to 0.125
- gate_delta_output: bfloat16 [256, 16384], P('fsdp', 'tp'), may hold values from -0.375 to 0.375
- up_delta_output: bfloat16 [256, 16384], P('fsdp', 'tp'), may hold values from -0.375 to 0.375
- down_delta_input: bfloat16 [16384, 256], P('tp', 'fsdp'), may hold values from -0.046875 to 0.046875
- down_delta_output: bfloat16 [256, 2048], P(('fsdp', 'tp')), may hold values from -0.375 to 0.375
- picture_begin_index: int32 [4], replicated, may hold values from 257 to 511
- cotangent: bfloat16 [4096, 2048], P(('fsdp', 'tp')), may hold values from -6 to 6
Outputs:
- result: bfloat16 [4096, 2048], P(('fsdp', 'tp'))
- tokens_grad: float32 [4096, 2048], P(('fsdp', 'tp'))
- attn_gain_grad: float32 [2048], P(('fsdp', 'tp'))
- mlp_gain_grad: float32 [2048], P(('fsdp', 'tp'))
- query_weight_grad: float32 [2048, 2048], P('fsdp', 'tp')
- keyval_weight_grad: float32 [2048, 512], P(('fsdp', 'tp'))
- out_weight_grad: float32 [2048, 2048], P('tp', 'fsdp')
- gate_weight_grad: float32 [2048, 16384], P('fsdp', 'tp')
- up_weight_grad: float32 [2048, 16384], P('fsdp', 'tp')
- down_weight_grad: float32 [16384, 2048], P('tp', 'fsdp')
- attn_lora_in_grad: float32 [2048, 256], P(('fsdp', 'tp'))
- query_lora_out_grad: float32 [256, 2048], P('fsdp', 'tp')
- keyval_lora_out_grad: float32 [256, 512], P(('fsdp', 'tp'))
- out_lora_in_grad: float32 [2048, 256], P('tp', 'fsdp')
- out_lora_out_grad: float32 [256, 2048], P(('fsdp', 'tp'))
- mlp_lora_in_grad: float32 [2048, 256], P(('fsdp', 'tp'))
- gate_lora_out_grad: float32 [256, 16384], P('fsdp', 'tp')
- up_lora_out_grad: float32 [256, 16384], P('fsdp', 'tp')
- down_lora_in_grad: float32 [16384, 256], P('tp', 'fsdp')
- down_lora_out_grad: float32 [256, 2048], P(('fsdp', 'tp'))
All inputs are finite; a program needn't handle non-finite values.
Results may differ from a plain program's by a relative error of at most 0.017.
The roundings to bfloat16 on the way count: a program that leaves them out, or rounds other values in their place, can miss the bound.
Values may be sent and summed in bfloat16 or wider, within the bound.
A program may use at most 320 MiB of HBM per device.

v0:
```python
import jax
import jax.numpy as jnp
from jax import lax
from jax.sharding import PartitionSpec as P

HEAD_WIDTH = 256
PICTURE = 256


EPSILON = 1e-06
EXACT = lax.Precision.HIGHEST
BLOCK_ROWS = 512


def partner(value, axis, apart):
    mask = 2**apart
    pairs = [(source, source ^ mask) for source in range(lax.axis_size(axis))]
    return lax.ppermute(value, axis, pairs)


def matrix_multiply(left_mat, right_mat):
    return jnp.dot(left_mat, right_mat, preferred_element_type=jnp.float32)


def times_transposed(left_mat, right_mat):
    return lax.dot_general(
        left_mat, right_mat, (((1,), (1,)), ((), ())), preferred_element_type=jnp.float32
    )


def transposed_times(left_mat, right_mat):
    return lax.dot_general(
        left_mat, right_mat, (((0,), (0,)), ((), ())), preferred_element_type=jnp.float32
    )


def exact_times_transposed(left_mat, right_mat):
    return lax.dot_general(
        left_mat,
        right_mat.astype(jnp.float32),
        (((1,), (1,)), ((), ())),
        precision=EXACT,
        preferred_element_type=jnp.float32,
    )


def exact_transposed_times(left_mat, right_mat):
    return lax.dot_general(
        left_mat.astype(jnp.float32),
        right_mat,
        (((0,), (0,)), ((), ())),
        precision=EXACT,
        preferred_element_type=jnp.float32,
    )


def merged_weight(shared_base, delta_left_factor, delta_right_factor):
    return (
        shared_base.astype(jnp.float32) + matrix_multiply(delta_left_factor, delta_right_factor)
    ).astype(jnp.bfloat16)


def normalize(values, gain_vec):
    return (
        values * lax.rsqrt(jnp.mean(values * values, axis=-1, keepdims=True) + EPSILON) * gain_vec
    )


def rotate(values, positions, direction):
    half_dim = HEAD_WIDTH // 2
    frequency = 10000.0 ** (-2.0 * jnp.arange(half_dim, dtype=jnp.float32) / HEAD_WIDTH)
    angles = positions.astype(jnp.float32)[:, None] * frequency[None, :]
    cosine = jnp.cos(angles)[:, None, :]
    sine_part = direction * jnp.sin(angles)[:, None, :]
    first_half = values[..., :half_dim]
    second = values[..., half_dim:]
    return jnp.concatenate(
        [first_half * cosine - second * sine_part, second * cosine + first_half * sine_part],
        axis=-1,
    )


def allowed_mask(query_pos, key_pos, picture_at):
    inside_query = (query_pos >= picture_at) & (query_pos < picture_at + PICTURE)
    inside_key = (key_pos >= picture_at) & (key_pos < picture_at + PICTURE)
    return (key_pos[None, :] <= query_pos[:, None]) | inside_query[:, None] & inside_key[None, :]


def spread_rows(values):
    return lax.all_gather(values, "tp", axis=0, tiled=True)


def spread_sum(term, row_count):
    return lax.psum_scatter(
        term(jnp.int32(0), row_count * lax.axis_size("tp")), "tp", scatter_dimension=0, tiled=True
    )


def attention_combined(
    pieces_list, delta_attention, key_value_complete, key_value_delta_product, output_delta_product
):
    query_complete, out_full, query_delta_product, out_down = pieces_list
    return (
        merged_weight(query_complete, delta_attention, query_delta_product),
        merged_weight(key_value_complete, delta_attention, key_value_delta_product),
        merged_weight(out_full, out_down, output_delta_product),
    )


def feedforward_combined(pieces_list, delta_feedforward, down_delta_product):
    gate_complete, up_complete, down_full, gate_delta_product, up_delta_product, down_in = (
        pieces_list
    )
    return (
        merged_weight(gate_complete, delta_feedforward, gate_delta_product),
        merged_weight(up_complete, delta_feedforward, up_delta_product),
        merged_weight(down_full, down_in, down_delta_product),
    )


def shards(
    tokens,
    attention_norm_gain,
    feedforward_norm_gain,
    query_shared_weight,
    key_value_shared_weight,
    output_shared_weight,
    gate_shared_weight,
    up_shared_weight,
    down_shared_weight,
    attention_delta_input,
    query_delta_output,
    key_value_delta_output,
    output_delta_input,
    output_delta_output,
    feedforward_delta_input,
    gate_delta_output,
    up_delta_output,
    down_delta_input,
    down_delta_output,
    picture_begin_index,
    cotangent,
):
    own_rows = tokens.shape[0]
    span_rows = own_rows * lax.axis_size("tp")
    key_rows = 2 * span_rows
    block_rows = min(BLOCK_ROWS, span_rows)
    block_count = span_rows // block_rows
    placed = lax.axis_index("fsdp")
    second_half = placed % 2
    picture_at = lax.dynamic_slice_in_dim(picture_begin_index, placed // 2, 1)[0]
    offset_rows = second_half * span_rows
    own_positions = (
        offset_rows + lax.axis_index("tp") * own_rows + jnp.arange(own_rows, dtype=jnp.int32)
    )
    span_positions = offset_rows + jnp.arange(span_rows, dtype=jnp.int32)
    key_positions = jnp.arange(key_rows, dtype=jnp.int32)
    scaling = HEAD_WIDTH ** (-0.5)
    shared = (
        lax.all_gather(attention_norm_gain, ("fsdp", "tp"), axis=0, tiled=True),
        lax.all_gather(feedforward_norm_gain, ("fsdp", "tp"), axis=0, tiled=True),
        lax.all_gather(key_value_shared_weight, ("fsdp", "tp"), axis=0, tiled=True),
        lax.all_gather(attention_delta_input, ("fsdp", "tp"), axis=0, tiled=True),
        lax.all_gather(key_value_delta_output, ("fsdp", "tp"), axis=0, tiled=True),
        lax.all_gather(output_delta_output, ("fsdp", "tp"), axis=0, tiled=True),
        lax.all_gather(feedforward_delta_input, ("fsdp", "tp"), axis=0, tiled=True),
        lax.all_gather(down_delta_output, ("fsdp", "tp"), axis=0, tiled=True),
    )
    gain_attn = shared[0].astype(jnp.float32)
    gain_mlp = shared[1].astype(jnp.float32)
    (
        key_value_complete,
        delta_attention,
        key_value_delta_product,
        output_delta_product,
        delta_feedforward,
        down_delta_product,
    ) = (shared[2], shared[3], shared[4], shared[5], shared[6], shared[7])
    attention_pieces_list = (
        lax.all_gather(query_shared_weight, "fsdp", axis=0, tiled=True),
        lax.all_gather(output_shared_weight, "fsdp", axis=1, tiled=True),
        lax.all_gather(query_delta_output, "fsdp", axis=0, tiled=True),
        lax.all_gather(output_delta_input, "fsdp", axis=1, tiled=True),
    )
    query_eff, keyval_eff, out_eff = attention_combined(
        attention_pieces_list,
        delta_attention,
        key_value_complete,
        key_value_delta_product,
        output_delta_product,
    )
    inputs = tokens.astype(jnp.float32)
    normed_own = normalize(inputs, gain_attn).astype(jnp.bfloat16)
    keyval_own = matrix_multiply(normed_own, keyval_eff)
    keys_own = rotate(keyval_own[:, None, :HEAD_WIDTH], own_positions, 1.0)[:, 0, :].astype(
        jnp.bfloat16
    )
    values_own = keyval_own[:, HEAD_WIDTH:].astype(jnp.bfloat16)
    normed_span, keys_span, values_span = (
        lax.all_gather(normed_own, "tp", axis=0, tiled=True),
        lax.all_gather(keys_own, "tp", axis=0, tiled=True),
        lax.all_gather(values_own, "tp", axis=0, tiled=True),
    )
    keys_other, values_other = partner((keys_span, values_span), "fsdp", 0)
    keys_all = jnp.where(
        second_half == 1,
        jnp.concatenate([keys_other, keys_span], axis=0),
        jnp.concatenate([keys_span, keys_other], axis=0),
    )
    values_all = jnp.where(
        second_half == 1,
        jnp.concatenate([values_other, values_span], axis=0),
        jnp.concatenate([values_span, values_other], axis=0),
    )
    query_lin = matrix_multiply(normed_span, query_eff)
    local_heads = query_lin.shape[1] // HEAD_WIDTH
    query_rot = (
        rotate(query_lin.reshape(span_rows, local_heads, HEAD_WIDTH), span_positions, 1.0) * scaling
    )
    query_blocks = (
        query_rot.astype(jnp.bfloat16)
        .transpose(1, 0, 2)
        .reshape(local_heads * block_count, block_rows, HEAD_WIDTH)
    )

    def block_mask(block_index):
        query_pos = (
            offset_rows
            + block_index % block_count * block_rows
            + jnp.arange(block_rows, dtype=jnp.int32)
        )
        return allowed_mask(query_pos, key_positions, picture_at)

    def attend(block_index):
        query_rows = query_blocks[block_index]
        scores = jnp.where(block_mask(block_index), times_transposed(query_rows, keys_all), -1e30)
        maximum = jnp.max(scores, axis=-1, keepdims=True)
        exponent = jnp.exp(scores - maximum)
        normalizer = jnp.sum(exponent, axis=-1, keepdims=True)
        probabilities = (exponent / normalizer).astype(jnp.bfloat16)
        return (matrix_multiply(probabilities, values_all), (maximum + jnp.log(normalizer))[:, 0])

    block_ids = jnp.arange(local_heads * block_count, dtype=jnp.int32)
    mixed_blocks, log_totals = lax.map(attend, block_ids)
    mixed_heads = (
        mixed_blocks.reshape(local_heads, span_rows, HEAD_WIDTH)
        .transpose(1, 0, 2)
        .reshape(span_rows, local_heads * HEAD_WIDTH)
        .astype(jnp.bfloat16)
    )
    attn_result = spread_sum(
        lambda first_row, row_count: matrix_multiply(mixed_heads, out_eff), own_rows
    )
    hidden = inputs + attn_result
    normed_mlp = spread_rows(normalize(hidden, gain_mlp).astype(jnp.bfloat16))
    feedforward_pieces = (
        lax.all_gather(gate_shared_weight, "fsdp", axis=0, tiled=True),
        lax.all_gather(up_shared_weight, "fsdp", axis=0, tiled=True),
        lax.all_gather(down_shared_weight, "fsdp", axis=1, tiled=True),
        lax.all_gather(gate_delta_output, "fsdp", axis=0, tiled=True),
        lax.all_gather(up_delta_output, "fsdp", axis=0, tiled=True),
        lax.all_gather(down_delta_input, "fsdp", axis=1, tiled=True),
    )
    gate_combined, up_combined, down_combined = feedforward_combined(
        feedforward_pieces, delta_feedforward, down_delta_product
    )
    gate_lin = matrix_multiply(normed_mlp, gate_combined)
    up_lin = matrix_multiply(normed_mlp, up_combined)
    activation = (jax.nn.gelu(gate_lin, approximate=True) * up_lin).astype(jnp.bfloat16)
    mlp_result = spread_sum(
        lambda first_row, row_count: matrix_multiply(activation, down_combined), own_rows
    )
    result = (hidden + mlp_result).astype(jnp.bfloat16)
    gate_delta_product, up_delta_product, down_in = (
        feedforward_pieces[3],
        feedforward_pieces[4],
        feedforward_pieces[5],
    )
    grad_span = spread_rows(cotangent)
    grad_activation = times_transposed(grad_span, down_combined)
    down_grad_eff = transposed_times(activation, grad_span)
    _, gelu_pull = jax.vjp(
        lambda gate_vals, up_vals: jax.nn.gelu(gate_vals, approximate=True) * up_vals,
        gate_lin,
        up_lin,
    )
    grad_gate, grad_up = gelu_pull(grad_activation)
    grad_gate = grad_gate.astype(jnp.bfloat16)
    grad_up = grad_up.astype(jnp.bfloat16)
    gate_combined_gradient = transposed_times(normed_mlp, grad_gate)
    up_combined_gradient = transposed_times(normed_mlp, grad_up)
    grad_normed_mlp = spread_sum(
        lambda first_row, row_count: times_transposed(grad_gate, gate_combined)
        + times_transposed(grad_up, up_combined),
        own_rows,
    )
    _, mlp_norm_pull = jax.vjp(normalize, hidden, gain_mlp)
    grad_hidden_norm, mlp_gain_part = mlp_norm_pull(grad_normed_mlp)
    grad_hidden = cotangent.astype(jnp.float32) + grad_hidden_norm
    query_delta_product, out_down = (attention_pieces_list[2], attention_pieces_list[3])
    grad_hidden_span = spread_rows(grad_hidden.astype(jnp.bfloat16))
    grad_mixed = times_transposed(grad_hidden_span, out_eff).astype(jnp.bfloat16)
    out_grad_eff = transposed_times(mixed_heads, grad_hidden_span)
    grad_blocks = (
        grad_mixed.reshape(span_rows, local_heads, HEAD_WIDTH)
        .transpose(1, 0, 2)
        .reshape(local_heads * block_count, block_rows, HEAD_WIDTH)
    )

    def revisit(totals, block_index):
        key_totals, value_totals = totals
        query_rows = query_blocks[block_index]
        grad_rows = grad_blocks[block_index]
        scores = jnp.where(block_mask(block_index), times_transposed(query_rows, keys_all), -1e30)
        probabilities = jnp.exp(scores - log_totals[block_index][:, None])
        grad_probs = times_transposed(grad_rows, values_all)
        inner_sum = jnp.sum(probabilities * grad_probs, axis=-1, keepdims=True)
        grad_scores = (probabilities * (grad_probs - inner_sum)).astype(jnp.bfloat16)
        key_totals = key_totals + transposed_times(grad_scores, query_rows)
        value_totals = value_totals + transposed_times(
            probabilities.astype(jnp.bfloat16), grad_rows
        )
        return ((key_totals, value_totals), matrix_multiply(grad_scores, keys_all))

    zero_rows = jnp.zeros((key_rows, HEAD_WIDTH), jnp.float32)
    (key_totals, value_totals), grad_query_blocks = lax.scan(
        revisit, (zero_rows, zero_rows), block_ids
    )
    grad_queries = (
        grad_query_blocks.reshape(local_heads, span_rows, HEAD_WIDTH).transpose(1, 0, 2) * scaling
    )
    grad_query_lin = (
        rotate(grad_queries, span_positions, -1.0)
        .reshape(span_rows, local_heads * HEAD_WIDTH)
        .astype(jnp.bfloat16)
    )
    keyval_totals = jnp.concatenate([key_totals, value_totals], axis=1)
    lower_rows = keyval_totals[:span_rows]
    upper_rows = keyval_totals[span_rows:]
    mine = jnp.where(second_half == 1, upper_rows, lower_rows)
    theirs = jnp.where(second_half == 1, lower_rows, upper_rows)
    returned = partner(theirs, "fsdp", 0)
    keyval_own_grad = lax.psum_scatter(mine + returned, "tp", scatter_dimension=0, tiled=True)
    grad_keys_own = rotate(keyval_own_grad[:, None, :HEAD_WIDTH], own_positions, -1.0)[:, 0, :]
    grad_keyval = jnp.concatenate([grad_keys_own, keyval_own_grad[:, HEAD_WIDTH:]], axis=1).astype(
        jnp.bfloat16
    )
    grad_normed_attn = spread_sum(
        lambda first_row, row_count: times_transposed(grad_query_lin, query_eff), own_rows
    ) + times_transposed(grad_keyval, keyval_eff)
    query_combined_gradient = transposed_times(normed_span, grad_query_lin)
    key_value_combined_gradient = transposed_times(normed_own, grad_keyval)
    _, attn_norm_pull = jax.vjp(normalize, inputs, gain_attn)
    grad_inputs_norm, attn_gain_part = attn_norm_pull(grad_normed_attn)
    tokens_grad = grad_hidden + grad_inputs_norm
    key_value_input_piece = exact_times_transposed(
        key_value_combined_gradient, key_value_delta_product
    )
    key_value_delta_piece = exact_transposed_times(delta_attention, key_value_combined_gradient)
    out_up_part = exact_transposed_times(out_down, out_grad_eff)
    down_up_part = exact_transposed_times(down_in, down_grad_eff)
    delta_attention_piece = (
        exact_times_transposed(query_combined_gradient, query_delta_product) + key_value_input_piece
    )
    query_delta_piece = exact_transposed_times(delta_attention, query_combined_gradient)
    out_down_part = exact_times_transposed(out_grad_eff, output_delta_product)
    delta_feedforward_piece = exact_times_transposed(
        gate_combined_gradient, gate_delta_product
    ) + exact_times_transposed(up_combined_gradient, up_delta_product)
    gate_delta_piece = exact_transposed_times(delta_feedforward, gate_combined_gradient)
    up_delta_piece = exact_transposed_times(delta_feedforward, up_combined_gradient)
    down_in_part = exact_times_transposed(down_grad_eff, down_delta_product)
    split_sums = (
        lax.psum_scatter(query_combined_gradient, "fsdp", scatter_dimension=0, tiled=True),
        lax.psum_scatter(out_grad_eff, "fsdp", scatter_dimension=1, tiled=True),
        lax.psum_scatter(query_delta_piece, "fsdp", scatter_dimension=0, tiled=True),
        lax.psum_scatter(out_down_part, "fsdp", scatter_dimension=1, tiled=True),
        lax.psum_scatter(gate_combined_gradient, "fsdp", scatter_dimension=0, tiled=True),
        lax.psum_scatter(up_combined_gradient, "fsdp", scatter_dimension=0, tiled=True),
        lax.psum_scatter(down_grad_eff, "fsdp", scatter_dimension=1, tiled=True),
        lax.psum_scatter(gate_delta_piece, "fsdp", scatter_dimension=0, tiled=True),
        lax.psum_scatter(up_delta_piece, "fsdp", scatter_dimension=0, tiled=True),
        lax.psum_scatter(down_in_part, "fsdp", scatter_dimension=1, tiled=True),
    )
    shared_sums = (
        lax.psum_scatter(attn_gain_part, ("fsdp", "tp"), scatter_dimension=0, tiled=True),
        lax.psum_scatter(mlp_gain_part, ("fsdp", "tp"), scatter_dimension=0, tiled=True),
        lax.psum_scatter(
            key_value_combined_gradient, ("fsdp", "tp"), scatter_dimension=0, tiled=True
        ),
        lax.psum_scatter(delta_attention_piece, ("fsdp", "tp"), scatter_dimension=0, tiled=True),
        lax.psum_scatter(key_value_delta_piece, ("fsdp", "tp"), scatter_dimension=0, tiled=True),
        lax.psum_scatter(out_up_part, ("fsdp", "tp"), scatter_dimension=0, tiled=True),
        lax.psum_scatter(delta_feedforward_piece, ("fsdp", "tp"), scatter_dimension=0, tiled=True),
        lax.psum_scatter(down_up_part, ("fsdp", "tp"), scatter_dimension=0, tiled=True),
    )
    return (
        result,
        tokens_grad,
        shared_sums[0],
        shared_sums[1],
        split_sums[0],
        shared_sums[2],
        split_sums[1],
        split_sums[4],
        split_sums[5],
        split_sums[6],
        shared_sums[3],
        split_sums[2],
        shared_sums[4],
        split_sums[3],
        shared_sums[5],
        shared_sums[6],
        split_sums[7],
        split_sums[8],
        split_sums[9],
        shared_sums[7],
    )


def solution(mesh):
    in_specs = (
        P(("fsdp", "tp"), None),
        P(("fsdp", "tp")),
        P(("fsdp", "tp")),
        P("fsdp", "tp"),
        P(("fsdp", "tp"), None),
        P("tp", "fsdp"),
        P("fsdp", "tp"),
        P("fsdp", "tp"),
        P("tp", "fsdp"),
        P(("fsdp", "tp"), None),
        P("fsdp", "tp"),
        P(("fsdp", "tp"), None),
        P("tp", "fsdp"),
        P(("fsdp", "tp"), None),
        P(("fsdp", "tp"), None),
        P("fsdp", "tp"),
        P("fsdp", "tp"),
        P("tp", "fsdp"),
        P(("fsdp", "tp"), None),
        P(),
        P(("fsdp", "tp"), None),
    )
    out_specs = (
        P(("fsdp", "tp"), None),
        P(("fsdp", "tp"), None),
        P(("fsdp", "tp")),
        P(("fsdp", "tp")),
        P("fsdp", "tp"),
        P(("fsdp", "tp"), None),
        P("tp", "fsdp"),
        P("fsdp", "tp"),
        P("fsdp", "tp"),
        P("tp", "fsdp"),
        P(("fsdp", "tp"), None),
        P("fsdp", "tp"),
        P(("fsdp", "tp"), None),
        P("tp", "fsdp"),
        P(("fsdp", "tp"), None),
        P(("fsdp", "tp"), None),
        P("fsdp", "tp"),
        P("fsdp", "tp"),
        P("tp", "fsdp"),
        P(("fsdp", "tp"), None),
    )
    return jax.shard_map(shards, mesh=mesh, in_specs=in_specs, out_specs=out_specs, check_vma=False)
```

profile of v0, /device:TPU:0, one launch (start us, length us, event | category | flops | bytes accessed | tf_op | source)
XLA Modules:
  0.0 3222.9 jit_solution(2667571070756240200)
XLA Ops:
  11.7 42.1 %all-reduce.5 = (bf16[2048]{0:T(1024)(128)(2,1)S(1)}, bf16[2048]{0:T(1024)(128)(2,1)S(1)}) all-reduce(bf16[2048]{0:T(1024)(128)(2,1)S(1)} %dynamic-update-slice, bf16[2048]{0:T(1024)(128)(2,1)S(1)} %dynamic-update-slice.1), channel_id=1, replica_groups=mesh['fsdp'=8,'tp'=4] {'fsdp','tp'}, use_global_device_ids=true, to_apply=%add | all-reduce | flops 4096 | bytes 16384
  80.4 74.0 %all_gather.78 = bf16[256,512]{1,0:T(8,128)(2,1)} all-gather(bf16[8,512]{1,0:T(8,128)(2,1)} %param.36), channel_id=1, replica_groups=mesh['fsdp'=8,'tp'=4] {'fsdp','tp'}, dimensions={0}, use_global_device_ids=true | all-gather | bytes 270336 | tf_op jit(solution)/shard_map/all_gather | solution.py:164
  184.8 45.0 %all-gather.19.cloned.1.call-done = bf16[512,2048]{1,0:T(8,128)(2,1)} async-done(((bf16[128,2048]{1,0:T(8,128)(2,1)}), bf16[512,2048]{1,0:T(8,128)(2,1)}) %all-gather.19.cloned.1.call-update) | async-done | bytes 2097168 | tf_op jit(solution)/shard_map/all_gather | solution.py:200
  234.3 53.5 %all-gather.25.cloned.1.call-done = bf16[2048,512]{1,0:T(8,128)(2,1)} async-done(((bf16[64,512]{1,0:T(8,128)(2,1)}), bf16[2048,512]{1,0:T(8,128)(2,1)}) %all-gather.25.cloned.1.call-update) | async-done | bytes 2097168 | tf_op jit(solution)/shard_map/all_gather | solution.py:162
  347.3 73.9 %reduce-scatter.34.cloned.1.call-done = f32[128,2048]{1,0:T(8,128)} async-done(((f32[512,2048]{1,0:T(8,128)}), f32[128,2048]{1,0:T(8,128)}) %reduce-scatter.34.cloned.1.call-update) | async-done | bytes 1048592 | tf_op jit(solution)/shard_map/reduce_scatter | solution.py:94
  428.4 50.1 %all-gather.35.cloned.1.call-done = bf16[2048,256]{1,0:T(8,128)(2,1)} async-done(((bf16[64,256]{1,0:T(8,128)(2,1)}), bf16[2048,256]{1,0:T(8,128)(2,1)}) %all-gather.35.cloned.1.call-update) | async-done | bytes 1048592 | tf_op jit(solution)/shard_map/all_gather | solution.py:166
  507.2 91.5 %all-gather.39.cloned.1.call-done = bf16[2048,4096]{1,0:T(8,128)(2,1)} async-done(((bf16[256,4096]{1,0:T(8,128)(2,1)}), bf16[2048,4096]{1,0:T(8,128)(2,1)}) %all-gather.39.cloned.1.call-update) | async-done | bytes 16777232 | tf_op jit(solution)/shard_map/all_gather | solution.py:258
  610.9 35.6 %all-gather.31.cloned.1.call-done = bf16[512,2048]{1,0:T(8,128)(2,1)} async-done(((bf16[128,2048]{1,0:T(8,128)(2,1)}), bf16[512,2048]{1,0:T(8,128)(2,1)}) %all-gather.31.cloned.1.call-update) | async-done | bytes 2097168 | tf_op jit(solution)/shard_map/all_gather | solution.py:90
  661.5 40.5 %all-gather.47.cloned.1.call-done = bf16[256,2048]{1,0:T(8,128)(2,1)} async-done(((bf16[8,2048]{1,0:T(8,128)(2,1)}), bf16[256,2048]{1,0:T(8,128)(2,1)}) %all-gather.47.cloned.1.call-update) | async-done | bytes 1048592 | tf_op jit(solution)/shard_map/all_gather | solution.py:167
  730.7 94.8 %all-gather.43.cloned.1.call-done = bf16[4096,2048]{1,0:T(8,128)(2,1)} async-done(((bf16[4096,256]{1,0:T(8,128)(2,1)}), bf16[4096,2048]{1,0:T(8,128)(2,1)}) %all-gather.43.cloned.1.call-update) | async-done | bytes 16777232 | tf_op jit(solution)/shard_map/all_gather | solution.py:259
  855.0 91.5 %all-gather.33.cloned.1.call-done = bf16[2048,4096]{1,0:T(8,128)(2,1)} async-done(((bf16[256,4096]{1,0:T(8,128)(2,1)}), bf16[2048,4096]{1,0:T(8,128)(2,1)}) %all-gather.33.cloned.1.call-update) | async-done | bytes 16777232 | tf_op jit(solution)/shard_map/all_gather | solution.py:257
  1045.8 75.7 %reduce-scatter.38.cloned.1.call-done = f32[128,2048]{1,0:T(8,128)} async-done(((f32[512,2048]{1,0:T(8,128)}), f32[128,2048]{1,0:T(8,128)}) %reduce-scatter.38.cloned.1.call-update) | async-done | bytes 1048592 | tf_op jit(solution)/shard_map/reduce_scatter | solution.py:94
  1126.6 46.2 %all-gather.51.cloned.1.call-done = bf16[512,2048]{1,0:T(8,128)(2,1)} async-done(((bf16[128,2048]{1,0:T(8,128)(2,1)}), bf16[512,2048]{1,0:T(8,128)(2,1)}) %all-gather.51.cloned.1.call-update) | async-done | bytes 2097168 | tf_op jit(solution)/shard_map/all_gather | solution.py:90
  1322.1 31.5 convolution_bitcast_fusion.4
  1356.7 32.5 %convolution_bitcast_fusion.2 = f32[256,4096]{0,1:T(8,128)} fusion(f32[2048,4096]{1,0:T(8,128)} %fusion.82, bf16[2048,256]{1,0:T(8,128)(2,1)S(1)} %copy-done.5), kind=kOutput, calls=%fused_computation.65 | convolution fusion | flops 25769803776 | bytes 38797312 | tf_op jit(solution)/shard_map/dot_general | solution.py:48
  1394.9 32.7 %convolution_bitcast_fusion.3 = f32[256,4096]{0,1:T(8,128)} fusion(f32[2048,4096]{1,0:T(8,128)} %fusion.81, bf16[2048,256]{1,0:T(8,128)(2,1)S(1)} %copy-done.5), kind=kOutput, calls=%fused_computation.66 | convolution fusion | flops 25769803776 | bytes 38797312 | tf_op jit(solution)/shard_map/dot_general | solution.py:48
  1517.1 39.7 %all-reduce.4 = (f32[2048]{0:T(1024)S(1)}, f32[2048]{0:T(1024)S(1)}) all-reduce(f32[2048]{0:T(1024)S(1)} %get-tuple-element.572, f32[2048]{0:T(1024)S(1)} %copy-done.43), channel_id=8, replica_groups=mesh['fsdp'=8,'tp'=4] {'fsdp','tp'}, use_global_device_ids=true, to_apply=%region_17.18.clone | all-reduce | flops 4096 | bytes 32768
  1561.8 110.2 %reduce-scatter.74.cloned.1.call-done = f32[8,2048]{1,0:T(8,128)} async-done(((f32[256,2048]{1,0:T(8,128)}), f32[8,2048]{1,0:T(8,128)}) %reduce-scatter.74.cloned.1.call-update) | async-done | bytes 65552
  1672.0 53.0 %reduce-scatter.72.cloned.1.call-done = f32[32,4096]{1,0:T(8,128)} async-done(((f32[256,4096]{1,0:T(8,128)}), f32[32,4096]{1,0:T(8,128)}) %reduce-scatter.72.cloned.1.call-update) | async-done | bytes 524304
  1725.0 55.0 %reduce-scatter.70.cloned.1.call-done = f32[32,4096]{1,0:T(8,128)} async-done(((f32[256,4096]{1,0:T(8,128)}), f32[32,4096]{1,0:T(8,128)}) %reduce-scatter.70.cloned.1.call-update) | async-done | bytes 524304
  1780.0 55.0 %reduce-scatter.62.cloned.1.call-done = f32[4096,32]{0,1:T(8,128)} async-done(((f32[4096,256]{0,1:T(8,128)}), f32[4096,32]{0,1:T(8,128)}) %reduce-scatter.62.cloned.1.call-update) | async-done | bytes 524304 | tf_op jit(solution)/shard_map/reduce_scatter | solution.py:383
  1834.9 37.8 %reduce-scatter.58.cloned.1.call-done = f32[512,32]{0,1:T(8,128)} async-done(((f32[512,256]{0,1:T(8,128)}), f32[512,32]{0,1:T(8,128)}) %reduce-scatter.58.cloned.1.call-update) | async-done | bytes 65552 | tf_op jit(solution)/shard_map/reduce_scatter | solution.py:377
  1872.8 37.8 %reduce-scatter.64.cloned.1.call-done = f32[32,512]{1,0:T(8,128)} async-done(((f32[256,512]{1,0:T(8,128)}), f32[32,512]{1,0:T(8,128)}) %reduce-scatter.64.cloned.1.call-update) | async-done | bytes 65552
  1910.6 142.5 %reduce-scatter.68.cloned.1.call-done = f32[8,2048]{1,0:T(8,128)} async-done(((f32[256,2048]{1,0:T(8,128)}), f32[8,2048]{1,0:T(8,128)}) %reduce-scatter.68.cloned.1.call-update) | async-done | bytes 65552
  2053.1 136.5 %reduce-scatter.66.cloned.1.call-done = f32[8,512]{1,0:T(8,128)} async-done(((f32[256,512]{1,0:T(8,128)}), f32[8,512]{1,0:T(8,128)}) %reduce-scatter.66.cloned.1.call-update) | async-done | bytes 16400
  2189.6 51.7 %reduce-scatter.48.cloned.1.call-done = f32[512,256]{1,0:T(8,128)} async-done(((f32[512,2048]{1,0:T(8,128)}), f32[512,256]{1,0:T(8,128)}) %reduce-scatter.48.cloned.1.call-update) | async-done | bytes 524304 | tf_op jit(solution)/shard_map/reduce_scatter | solution.py:375
  2241.3 55.0 %reduce-scatter.44.cloned.1.call-done = f32[256,512]{1,0:T(8,128)} async-done(((f32[2048,512]{1,0:T(8,128)}), f32[256,512]{1,0:T(8,128)}) %reduce-scatter.44.cloned.1.call-update) | async-done | bytes 524304 | tf_op jit(solution)/shard_map/reduce_scatter | solution.py:374
  2296.3 142.9 %reduce-scatter.56.cloned.1.call-done = f32[64,256]{1,0:T(8,128)} async-done(((f32[2048,256]{1,0:T(8,128)}), f32[64,256]{1,0:T(8,128)}) %reduce-scatter.56.cloned.1.call-update) | async-done | bytes 65552 | tf_op jit(solution)/shard_map/reduce_scatter | solution.py:391
  2439.2 149.6 %reduce-scatter.46.cloned.1.call-done = f32[64,512]{1,0:T(8,128)} async-done(((f32[2048,512]{1,0:T(8,128)}), f32[64,512]{1,0:T(8,128)}) %reduce-scatter.46.cloned.1.call-update) | async-done | bytes 131088 | tf_op jit(solution)/shard_map/reduce_scatter | solution.py:388
  2588.8 208.3 %reduce-scatter.52.cloned.1.call-done = f32[256,4096]{1,0:T(8,128)} async-done(((f32[2048,4096]{1,0:T(8,128)}), f32[256,4096]{1,0:T(8,128)}) %reduce-scatter.52.cloned.1.call-update) | async-done | bytes 4194320 | tf_op jit(solution)/shard_map/reduce_scatter | solution.py:379
  2797.2 209.5 %reduce-scatter.50.cloned.1.call-done = f32[256,4096]{1,0:T(8,128)} async-done(((f32[2048,4096]{1,0:T(8,128)}), f32[256,4096]{1,0:T(8,128)}) %reduce-scatter.50.cloned.1.call-update) | async-done | bytes 4194320 | tf_op jit(solution)/shard_map/reduce_scatter | solution.py:378
  3006.7 209.4 %reduce-scatter.54.cloned.1.call-done = f32[4096,256]{1,0:T(8,128)} async-done(((f32[4096,2048]{1,0:T(8,128)}), f32[4096,256]{1,0:T(8,128)}) %reduce-scatter.54.cloned.1.call-update) | async-done | bytes 4194320 | tf_op jit(solution)/shard_map/reduce_scatter | solution.py:380
  (369 shorter events, 630.8 us)
Async XLA Ops:
  9.4 172.7 %all-gather.27.cloned.1.call-start = ((), (), s32[]{:S(2)}) async-start(), calls=%async_computation.25 | async-start | bytes 2359296 | tf_op jit(solution)/shard_map/all_gather | solution.py:181
  10.0 219.8 %all-gather.19.cloned.1.call-start = ((), (), s32[]{:S(2)}) async-start(), calls=%async_computation.21 | async-start | bytes 2621440 | tf_op jit(solution)/shard_map/all_gather | solution.py:200
  58.2 229.6 %all-gather.25.cloned.1.call-start = ((), (), s32[]{:S(2)}) async-start(), calls=%async_computation.24 | async-start | bytes 2162688 | tf_op jit(solution)/shard_map/all_gather | solution.py:162
  58.8 362.4 %reduce-scatter.34.cloned.1.call-start = ((), (), s32[]{:S(2)}) async-start(), calls=%async_computation.27 | async-start | bytes 5242880 | tf_op jit(solution)/shard_map/reduce_scatter | solution.py:94
  346.6 252.0 %all-gather.39.cloned.1.call-start = ((), (), s32[]{:S(2)}) async-start(), calls=%async_computation.32 | async-start | bytes 18874368 | tf_op jit(solution)/shard_map/all_gather | solution.py:258
  347.2 299.3 %all-gather.31.cloned.1.call-start = ((), (), s32[]{:S(2)}) async-start(), calls=%async_computation.28 | async-start | bytes 2621440 | tf_op jit(solution)/shard_map/all_gather | solution.py:90
  424.6 277.3 %all-gather.47.cloned.1.call-start = ((), (), s32[]{:S(2)}) async-start(), calls=%async_computation.36 | async-start | bytes 1081344 | tf_op jit(solution)/shard_map/all_gather | solution.py:167
  425.2 305.4 %all-gather.45.cloned.1.call-start = ((), (), s32[]{:S(2)}) async-start(), calls=%async_computation.35 | async-start | bytes 2359296 | tf_op jit(solution)/shard_map/all_gather | solution.py:262
  426.0 399.5 %all-gather.43.cloned.1.call-start = ((), (), s32[]{:S(2)}) async-start(), calls=%async_computation.34 | async-start | bytes 18874368 | tf_op jit(solution)/shard_map/all_gather | solution.py:259
  426.6 428.4 %all-gather.37.cloned.1.call-start = ((), (), s32[]{:S(2)}) async-start(), calls=%async_computation.31 | async-start | bytes 2359296 | tf_op jit(solution)/shard_map/all_gather | solution.py:260
  427.1 519.4 %all-gather.33.cloned.1.call-start = ((), (), s32[]{:S(2)}) async-start(), calls=%async_computation.29 | async-start | bytes 18874368 | tf_op jit(solution)/shard_map/all_gather | solution.py:257
  427.7 565.9 %all-gather.49.cloned.1.call-start = ((), (), s32[]{:S(2)}) async-start(), calls=%async_computation.38 | async-start | bytes 2621440 | tf_op jit(solution)/shard_map/all_gather | solution.py:90
  428.3 693.2 %reduce-scatter.38.cloned.1.call-start = ((), (), s32[]{:S(2)}) async-start(), calls=%async_computation.39 | async-start | bytes 5242880 | tf_op jit(solution)/shard_map/reduce_scatter | solution.py:94
  1126.5 361.8 %reduce-scatter.42.cloned.1.call-start = ((), (), s32[]{:S(2)}) async-start(), calls=%async_computation.42 | async-start | bytes 1310720 | tf_op jit(solution)/shard_map/reduce_scatter | solution.py:343
  1204.9 308.2 %reduce-scatter.40.cloned.1.call-start = ((), (), s32[]{:S(2)}) async-start(), calls=%async_computation.41 | async-start | bytes 5242880 | tf_op jit(solution)/shard_map/reduce_scatter | solution.py:94
  1210.0 347.9 %reduce-scatter.36.cloned.1.call-start = ((), (), s32[]{:S(2)}) async-start(), calls=%async_computation.37 | async-start | bytes 5242880 | tf_op jit(solution)/shard_map/reduce_scatter | solution.py:94
  1225.0 336.8 %reduce-scatter.60.cloned.1.call-start = ((), (), s32[]{:S(2)}) async-start(), calls=%async_computation.51 | async-start | bytes 2162688 | tf_op jit(solution)/shard_map/reduce_scatter | solution.py:394
  1303.3 368.7 %reduce-scatter.74.cloned.1.call-start = ((), (), s32[]{:S(2)}) async-start(), calls=%async_computation.58 | async-start | bytes 2162688
  1356.6 368.3 %reduce-scatter.72.cloned.1.call-start = ((), (), s32[]{:S(2)}) async-start(), calls=%async_computation.57 | async-start | bytes 4718592
  1394.9 385.1 %reduce-scatter.70.cloned.1.call-start = ((), (), s32[]{:S(2)}) async-start(), calls=%async_computation.56 | async-start | bytes 4718592
  1433.3 401.7 %reduce-scatter.62.cloned.1.call-start = ((), (), s32[]{:S(2)}) async-start(), calls=%async_computation.52 | async-start | bytes 4718592 | tf_op jit(solution)/shard_map/reduce_scatter | solution.py:383
  1457.7 415.1 %reduce-scatter.58.cloned.1.call-start = ((), (), s32[]{:S(2)}) async-start(), calls=%async_computation.50 | async-start | bytes 589824 | tf_op jit(solution)/shard_map/reduce_scatter | solution.py:377
  1468.7 441.9 %reduce-scatter.64.cloned.1.call-start = ((), (), s32[]{:S(2)}) async-start(), calls=%async_computation.53 | async-start | bytes 589824
  1480.4 572.7 %reduce-scatter.68.cloned.1.call-start = ((), (), s32[]{:S(2)}) async-start(), calls=%async_computation.55 | async-start | bytes 2162688
  1488.0 701.6 %reduce-scatter.66.cloned.1.call-start = ((), (), s32[]{:S(2)}) async-start(), calls=%async_computation.54 | async-start | bytes 540672
  1500.9 740.4 %reduce-scatter.48.cloned.1.call-start = ((), (), s32[]{:S(2)}) async-start(), calls=%async_computation.45 | async-start | bytes 4718592 | tf_op jit(solution)/shard_map/reduce_scatter | solution.py:375
  1501.7 794.6 %reduce-scatter.44.cloned.1.call-start = ((), (), s32[]{:S(2)}) async-start(), calls=%async_computation.43 | async-start | bytes 4718592 | tf_op jit(solution)/shard_map/reduce_scatter | solution.py:374
  1502.3 936.9 %reduce-scatter.56.cloned.1.call-start = ((), (), s32[]{:S(2)}) async-start(), calls=%async_computation.49 | async-start | bytes 2162688 | tf_op jit(solution)/shard_map/reduce_scatter | solution.py:391
  1510.3 1078.5 %reduce-scatter.46.cloned.1.call-start = ((), (), s32[]{:S(2)}) async-start(), calls=%async_computation.44 | async-start | bytes 4325376 | tf_op jit(solution)/shard_map/reduce_scatter | solution.py:388
  1511.1 1286.1 %reduce-scatter.52.cloned.1.call-start = ((), (), s32[]{:S(2)}) async-start(), calls=%async_computation.47 | async-start | bytes 37748736 | tf_op jit(solution)/shard_map/reduce_scatter | solution.py:379
  1511.7 1495.0 %reduce-scatter.50.cloned.1.call-start = ((), (), s32[]{:S(2)}) async-start(), calls=%async_computation.46 | async-start | bytes 37748736 | tf_op jit(solution)/shard_map/reduce_scatter | solution.py:378
  1512.3 1703.8 %reduce-scatter.54.cloned.1.call-start = ((), (), s32[]{:S(2)}) async-start(), calls=%async_computation.48 | async-start | bytes 37748736 | tf_op jit(solution)/shard_map/reduce_scatter | solution.py:380
  (78 other events, 3651.1 us)
Sparse Core Ops, SparseCore 0:
  11.0 56.5 all-gather.22
  99.3 53.9 all-gather.28
  184.1 45.6 all-gather.18
  232.6 55.1 all-gather.24
  345.2 75.9 reduce-scatter.33
  424.2 54.2 all-gather.34
  508.9 89.7 all-gather.38
  600.8 45.6 all-gather.30
  649.4 52.5 all-gather.46
  732.4 93.0 all-gather.42
  856.7 89.7 all-gather.32
  947.9 45.6 all-gather.48
  1045.8 75.5 reduce-scatter.37
  1126.6 46.1 all-gather.50
  1233.4 75.3 reduce-scatter.39
  1311.0 77.2 reduce-scatter.35
  1391.2 140.6 reduce-scatter.59
  1534.6 137.3 reduce-scatter.73
  1675.9 48.9 reduce-scatter.71
  1728.8 51.1 reduce-scatter.69
  1783.7 51.1 reduce-scatter.61
  1838.6 34.1 reduce-scatter.57
  1876.4 34.1 reduce-scatter.63
  1913.3 139.8 reduce-scatter.67
  2055.9 133.6 reduce-scatter.65
  2193.6 47.7 reduce-scatter.47
  2245.1 51.1 reduce-scatter.43
  2299.2 140.0 reduce-scatter.55
  2442.1 146.7 reduce-scatter.45
  2592.8 204.3 reduce-scatter.51
  2801.2 205.4 reduce-scatter.49
  3010.8 205.2 reduce-scatter.53
  (6 shorter events, 161.0 us)
where the time goes:
time: 3230 us; the launch traced here: 3220 us
  waiting for transfers between devices  2480 us (77%)
  matrix products  438 us (14%)
  blocking collectives  202 us (6%)
  local copies, waits for them, and re-layouts  40.9 us (1%)
    unnamed x44, waiting for transfers between devices  547 us
    reduce_scatter x1, waiting for transfers between devices, shards(): lax.psum_scatter(gate_combined_gradient, 'fsdp', scatter_dimension=0, til...  209 us
    reduce_scatter x1, waiting for transfers between devices, shards(): lax.psum_scatter(down_grad_eff, 'fsdp', scatter_dimension=1, tiled=True)  209 us
    reduce_scatter x1, waiting for transfers between devices, shards(): lax.psum_scatter(up_combined_gradient, 'fsdp', scatter_dimension=0, tiled...  208 us
    reduce_scatter x4, waiting for transfers between devices, spread_sum(): lax.psum_scatter(term(jnp.int32(0), row_count * lax.axis_size('tp')), 'tp...  150 us
    reduce_scatter x1, waiting for transfers between devices, shards(): lax.psum_scatter(key_value_combined_gradient, ('fsdp', 'tp'), scatter_dim...  150 us
    reduce_scatter x1, waiting for transfers between devices, shards(): lax.psum_scatter(delta_attention_piece, ('fsdp', 'tp'), scatter_dimension...  143 us
    dot_general x6, matrix products, exact_transposed_times(): lax.dot_general(left_mat.astype(jnp.float32), right_mat, (((0,), (0,)), (...  114 us
  transfers between devices with their start and end apart: 41, of which 32 were waited for; matrix products, arithmetic and copies ran while one was open for 12% of the time, Pallas kernels for 0%

commit v1 on v0

v1 whole, which is shorter than its diff:
```python
import jax
import jax.numpy as jnp
from jax import lax
from jax.sharding import PartitionSpec as P

HEAD_WIDTH = 256
PICTURE = 256


EPSILON = 1e-06
BLOCK_ROWS = 512


def partner(value, axis, apart):
    mask = 2**apart
    pairs = [(source, source ^ mask) for source in range(lax.axis_size(axis))]
    return lax.ppermute(value, axis, pairs)


def matrix_multiply(left_mat, right_mat):
    return jnp.dot(left_mat, right_mat, preferred_element_type=jnp.float32)


def times_transposed(left_mat, right_mat):
    return lax.dot_general(
        left_mat, right_mat, (((1,), (1,)), ((), ())), preferred_element_type=jnp.float32
    )


def transposed_times(left_mat, right_mat):
    return lax.dot_general(
        left_mat, right_mat, (((0,), (0,)), ((), ())), preferred_element_type=jnp.float32
    )


def merged_weight(shared_base, delta_left_factor, delta_right_factor):
    return (
        shared_base.astype(jnp.float32) + matrix_multiply(delta_left_factor, delta_right_factor)
    ).astype(jnp.bfloat16)


def normalize(values, gain_vec):
    return (
        values * lax.rsqrt(jnp.mean(values * values, axis=-1, keepdims=True) + EPSILON) * gain_vec
    )


def rotate(values, positions, direction):
    half_dim = HEAD_WIDTH // 2
    frequency = 10000.0 ** (-2.0 * jnp.arange(half_dim, dtype=jnp.float32) / HEAD_WIDTH)
    angles = positions.astype(jnp.float32)[:, None] * frequency[None, :]
    cosine = jnp.cos(angles)[:, None, :]
    sine_part = direction * jnp.sin(angles)[:, None, :]
    first_half = values[..., :half_dim]
    second = values[..., half_dim:]
    return jnp.concatenate(
        [first_half * cosine - second * sine_part, second * cosine + first_half * sine_part],
        axis=-1,
    )


def allowed_mask(query_pos, key_pos, picture_at):
    inside_query = (query_pos >= picture_at) & (query_pos < picture_at + PICTURE)
    inside_key = (key_pos >= picture_at) & (key_pos < picture_at + PICTURE)
    return (key_pos[None, :] <= query_pos[:, None]) | inside_query[:, None] & inside_key[None, :]


def joined(axis_names, value, axis=0):
    return lax.all_gather(value, axis_names, axis=axis, tiled=True)


def scattered(axis_names, value):
    return lax.psum_scatter(value, axis_names, scatter_dimension=0, tiled=True)


def low(value):
    return value.astype(jnp.bfloat16)


def to_lanes(value, width):
    return jnp.concatenate(
        [value[:, at : at + width] for at in range(0, value.shape[1], width)], axis=0
    )


class Packed:
    def __init__(self, width):
        self.width, self.pieces, self.shapes = width, [], []

    def add(self, value):
        self.shapes.append(value.shape)
        self.pieces.append(to_lanes(value, self.width))

    def gather(self, axis_names):
        whole = lax.all_gather(jnp.concatenate(self.pieces, axis=0), axis_names, axis=0)
        results, at = [], 0
        for rows, columns in self.shapes:
            parts = []
            for _ in range(columns // self.width):
                parts.append(whole[:, at : at + rows].reshape(-1, self.width))
                at += rows
            results.append(jnp.concatenate(parts, axis=1))
        return results


def blocked(main_cols, extra_cols, parts):
    rows = main_cols.shape[0]
    return jnp.concatenate(
        [main_cols.reshape(rows, parts, -1), extra_cols.reshape(rows, parts, -1)], axis=2
    ).reshape(rows, -1)


def shards(
    tokens,
    attention_norm_gain,
    feedforward_norm_gain,
    query_shared_weight,
    key_value_shared_weight,
    output_shared_weight,
    gate_shared_weight,
    up_shared_weight,
    down_shared_weight,
    attention_delta_input,
    query_delta_output,
    key_value_delta_output,
    output_delta_input,
    output_delta_output,
    feedforward_delta_input,
    gate_delta_output,
    up_delta_output,
    down_delta_input,
    down_delta_output,
    picture_begin_index,
    cotangent,
):
    both = ("fsdp", "tp")
    tp_size = lax.axis_size("tp")
    fsdp_size = lax.axis_size("fsdp")
    parts = tp_size * fsdp_size
    own_rows, model_width = tokens.shape
    span_rows = own_rows * tp_size
    key_rows = 2 * span_rows
    block_rows = min(BLOCK_ROWS, span_rows)
    block_count = span_rows // block_rows
    placed = lax.axis_index("fsdp")
    tp_at = lax.axis_index("tp")
    second_half = placed % 2
    picture_at = lax.dynamic_slice_in_dim(picture_begin_index, placed // 2, 1)[0]
    offset_rows = second_half * span_rows
    span_positions = offset_rows + jnp.arange(span_rows, dtype=jnp.int32)
    key_positions = jnp.arange(key_rows, dtype=jnp.int32)
    scaling = HEAD_WIDTH ** (-0.5)

    rank = gate_delta_output.shape[0] * fsdp_size
    common = Packed(rank)
    gain_rows = jnp.concatenate([attention_norm_gain[None], feedforward_norm_gain[None]], axis=0)
    common.add(jnp.pad(gain_rows, ((0, 6), (0, rank - gain_rows.shape[1]))))
    common.add(key_value_shared_weight)
    common.add(attention_delta_input)
    common.add(key_value_delta_output)
    common.add(output_delta_output)
    common.add(feedforward_delta_input)
    common.add(down_delta_output)
    (
        gains,
        key_value_complete,
        delta_attention,
        key_value_delta_product,
        output_delta_product,
        delta_feedforward,
        down_delta_product,
    ) = common.gather(both)
    gains = gains.reshape(parts, 8, rank)[:, :2, : gain_rows.shape[1]].astype(jnp.float32)
    gain_attn = gains[:, 0].reshape(-1)
    gain_mlp = gains[:, 1].reshape(-1)

    rows_both = joined("tp", jnp.concatenate([tokens, cotangent], axis=1))
    tokens_span = rows_both[:, :model_width]
    grad_span = rows_both[:, model_width:]

    width = output_shared_weight.shape[1]
    heads_pack = Packed(width)
    heads_pack.add(query_shared_weight)
    heads_pack.add(query_delta_output)
    heads_pack.add(output_delta_input.T)
    heads_pack.add(output_shared_weight)
    query_complete, query_delta_product, out_down_t, out_stack = heads_pack.gather("fsdp")
    out_rows = output_shared_weight.shape[0]
    out_full = (
        out_stack.reshape(fsdp_size, out_rows, width).transpose(1, 0, 2).reshape(out_rows, -1)
    )
    query_eff = merged_weight(query_complete, delta_attention, query_delta_product)
    keyval_eff = merged_weight(key_value_complete, delta_attention, key_value_delta_product)
    out_eff = low(out_full.astype(jnp.float32) + transposed_times(out_down_t, output_delta_product))

    delta_rows = gate_delta_output.shape[0]
    delta_stack = lax.all_gather(
        jnp.concatenate([gate_delta_output, up_delta_output, down_delta_input.T], axis=0),
        "fsdp",
        axis=0,
    )
    gate_delta_product, up_delta_product, down_in_t = (
        delta_stack[:, at * delta_rows : (at + 1) * delta_rows].reshape(rank, -1) for at in range(3)
    )
    shard_rows = gate_shared_weight.shape[0]
    delta_feedforward_rows = lax.dynamic_slice_in_dim(
        delta_feedforward, placed * shard_rows, shard_rows
    )
    down_delta_cols = lax.dynamic_slice_in_dim(
        down_delta_product, placed * shard_rows, shard_rows, axis=1
    )
    down_eff = joined(
        "fsdp",
        low(
            down_shared_weight.astype(jnp.float32) + transposed_times(down_in_t, down_delta_cols)
        ),
        axis=1,
    )
    gate_eff = joined(
        "fsdp", merged_weight(gate_shared_weight, delta_feedforward_rows, gate_delta_product)
    )
    up_eff = joined(
        "fsdp", merged_weight(up_shared_weight, delta_feedforward_rows, up_delta_product)
    )

    inputs = tokens.astype(jnp.float32)
    inputs_span = tokens_span.astype(jnp.float32)
    normed_span = low(normalize(inputs_span, gain_attn))
    keyval_span = matrix_multiply(normed_span, keyval_eff)
    keys_span = rotate(keyval_span[:, None, :HEAD_WIDTH], span_positions, 1.0)[:, 0, :]
    keyval_low = low(jnp.concatenate([keys_span, keyval_span[:, HEAD_WIDTH:]], axis=1))
    keyval_other = partner(keyval_low, "fsdp", 0)
    keyval_all = jnp.where(
        second_half == 1,
        jnp.concatenate([keyval_other, keyval_low], axis=0),
        jnp.concatenate([keyval_low, keyval_other], axis=0),
    )
    keys_all = keyval_all[:, :HEAD_WIDTH]
    values_all = keyval_all[:, HEAD_WIDTH:]
    query_lin = matrix_multiply(normed_span, query_eff)
    local_heads = query_lin.shape[1] // HEAD_WIDTH
    query_rot = (
        rotate(query_lin.reshape(span_rows, local_heads, HEAD_WIDTH), span_positions, 1.0) * scaling
    )
    query_blocks = (
        low(query_rot)
        .transpose(1, 0, 2)
        .reshape(local_heads * block_count, block_rows, HEAD_WIDTH)
    )

    def block_mask(block_index):
        query_pos = (
            offset_rows
            + block_index % block_count * block_rows
            + jnp.arange(block_rows, dtype=jnp.int32)
        )
        return allowed_mask(query_pos, key_positions, picture_at)

    def attend(block_index):
        query_rows = query_blocks[block_index]
        scores = jnp.where(block_mask(block_index), times_transposed(query_rows, keys_all), -1e30)
        maximum = jnp.max(scores, axis=-1, keepdims=True)
        exponent = jnp.exp(scores - maximum)
        normalizer = jnp.sum(exponent, axis=-1, keepdims=True)
        probabilities = low(exponent / normalizer)
        return (matrix_multiply(probabilities, values_all), (maximum + jnp.log(normalizer))[:, 0])

    block_ids = jnp.arange(local_heads * block_count, dtype=jnp.int32)
    mixed_blocks, log_totals = lax.map(attend, block_ids)
    mixed_heads = low(
        mixed_blocks.reshape(local_heads, span_rows, HEAD_WIDTH)
        .transpose(1, 0, 2)
        .reshape(span_rows, local_heads * HEAD_WIDTH)
    )
    attn_result = scattered("tp", low(matrix_multiply(mixed_heads, out_eff)))
    hidden = inputs + attn_result.astype(jnp.float32)
    normed_mlp = joined("tp", low(normalize(hidden, gain_mlp)))

    grad_activation = times_transposed(grad_span, down_eff)
    gate_lin = matrix_multiply(normed_mlp, gate_eff)
    up_lin = matrix_multiply(normed_mlp, up_eff)
    activation, gelu_pull = jax.vjp(
        lambda gate_vals, up_vals: jax.nn.gelu(gate_vals, approximate=True) * up_vals,
        gate_lin,
        up_lin,
    )
    activation = low(activation)
    grad_gate, grad_up = gelu_pull(grad_activation)
    grad_gate, grad_up = low(grad_gate), low(grad_up)
    grad_normed_mlp = scattered(
        "tp",
        low(times_transposed(grad_gate, gate_eff) + times_transposed(grad_up, up_eff)),
    ).astype(jnp.float32)
    _, mlp_norm_pull = jax.vjp(normalize, hidden, gain_mlp)
    grad_hidden_norm, mlp_gain_part = mlp_norm_pull(grad_normed_mlp)
    grad_hidden = cotangent.astype(jnp.float32) + grad_hidden_norm
    grad_hidden_span = joined("tp", low(grad_hidden))
    mlp_result = scattered("tp", low(matrix_multiply(activation, down_eff)))
    result = low(hidden + mlp_result.astype(jnp.float32))

    normed_delta = low(matrix_multiply(normed_mlp, delta_feedforward))
    normed_wide = blocked(normed_mlp, normed_delta, fsdp_size)
    grad_delta = low(times_transposed(grad_span, down_delta_product))
    grad_wide = blocked(grad_span, grad_delta, fsdp_size)
    down_sum = scattered("fsdp", low(transposed_times(grad_wide, activation)))
    gate_sum = scattered("fsdp", low(transposed_times(normed_wide, grad_gate)))
    up_sum = scattered("fsdp", low(transposed_times(normed_wide, grad_up)))
    mlp_inner = low(
        times_transposed(grad_gate, gate_delta_product)
        + times_transposed(grad_up, up_delta_product)
    )
    mlp_lora_in = low(transposed_times(normed_mlp, mlp_inner))
    active_delta = low(times_transposed(activation, down_in_t))
    down_lora_out = low(transposed_times(active_delta, grad_span))

    grad_mixed = low(times_transposed(grad_hidden_span, out_eff))
    grad_blocks = (
        grad_mixed.reshape(span_rows, local_heads, HEAD_WIDTH)
        .transpose(1, 0, 2)
        .reshape(local_heads * block_count, block_rows, HEAD_WIDTH)
    )

    def revisit(totals, block_index):
        key_totals, value_totals = totals
        query_rows = query_blocks[block_index]
        grad_rows = grad_blocks[block_index]
        scores = jnp.where(block_mask(block_index), times_transposed(query_rows, keys_all), -1e30)
        probabilities = jnp.exp(scores - log_totals[block_index][:, None])
        grad_probs = times_transposed(grad_rows, values_all)
        inner_sum = jnp.sum(probabilities * grad_probs, axis=-1, keepdims=True)
        grad_scores = low(probabilities * (grad_probs - inner_sum))
        key_totals = key_totals + transposed_times(grad_scores, query_rows)
        value_totals = value_totals + transposed_times(low(probabilities), grad_rows)
        return ((key_totals, value_totals), matrix_multiply(grad_scores, keys_all))

    zero_rows = jnp.zeros((key_rows, HEAD_WIDTH), jnp.float32)
    (key_totals, value_totals), grad_query_blocks = lax.scan(
        revisit, (zero_rows, zero_rows), block_ids
    )
    grad_queries = (
        grad_query_blocks.reshape(local_heads, span_rows, HEAD_WIDTH).transpose(1, 0, 2) * scaling
    )
    grad_query_lin = low(
        rotate(grad_queries, span_positions, -1.0).reshape(span_rows, local_heads * HEAD_WIDTH)
    )
    keyval_totals = jnp.concatenate([key_totals, value_totals], axis=1)
    lower_rows = keyval_totals[:span_rows]
    upper_rows = keyval_totals[span_rows:]
    mine = jnp.where(second_half == 1, upper_rows, lower_rows)
    theirs = jnp.where(second_half == 1, lower_rows, upper_rows)
    keyval_part = mine + partner(theirs, "fsdp", 0)
    grad_keys = rotate(keyval_part[:, None, :HEAD_WIDTH], span_positions, -1.0)[:, 0, :]
    grad_keyval = low(jnp.concatenate([grad_keys, keyval_part[:, HEAD_WIDTH:]], axis=1))
    grad_normed_part = times_transposed(grad_query_lin, query_eff) + times_transposed(
        grad_keyval, keyval_eff
    )
    grad_normed_attn = scattered("tp", low(grad_normed_part)).astype(jnp.float32)
    unit_span = inputs_span * lax.rsqrt(
        jnp.mean(inputs_span * inputs_span, axis=-1, keepdims=True) + EPSILON
    )
    attn_gain_part = jnp.sum(grad_normed_part * unit_span, axis=0)
    _, attn_norm_pull = jax.vjp(normalize, inputs, gain_attn)
    tokens_grad = grad_hidden + attn_norm_pull(grad_normed_attn)[0]

    mixed_delta = low(times_transposed(mixed_heads, out_down_t))
    out_lora_out = low(transposed_times(mixed_delta, grad_hidden_span))
    hidden_delta = low(times_transposed(grad_hidden_span, output_delta_product))
    out_grads = low(
        transposed_times(blocked(grad_hidden_span, hidden_delta, parts), mixed_heads)
    )
    attn_delta = low(matrix_multiply(normed_span, delta_attention))
    attn_inner = low(
        times_transposed(grad_query_lin, query_delta_product)
        + times_transposed(grad_keyval, key_value_delta_product)
    )
    attn_grads = low(
        transposed_times(
            blocked(normed_span, attn_delta, parts),
            jnp.concatenate([grad_query_lin, grad_keyval, attn_inner], axis=1),
        )
    )

    def per_device(value):
        rows = value.shape[0] // parts
        return jnp.concatenate(
            [
                value[:, at : at + rank].reshape(parts, rows, rank)
                for at in range(0, value.shape[1], rank)
            ],
            axis=1,
        )

    def from_device(value, rows):
        return jnp.concatenate(
            [value[..., at : at + rows, :] for at in range(0, value.shape[-2], rows)], axis=-1
        )

    main = model_width // parts
    extra = rank // parts
    wide = main + extra
    gain_lines = jnp.stack(
        [mlp_gain_part.reshape(parts, main), attn_gain_part.reshape(parts, main)], axis=1
    )
    gain_lines = low(jnp.pad(gain_lines, ((0, 0), (0, 6), (0, rank - main))))
    head_cols = query_eff.shape[1]
    split_rows = 2 * (head_cols // rank) * wide
    first = jnp.concatenate(
        [
            per_device(out_grads),
            per_device(attn_grads),
            per_device(mlp_lora_in),
            per_device(down_lora_out),
            per_device(out_lora_out),
            gain_lines,
        ],
        axis=1,
    )
    first_sum = scattered("fsdp", first)
    split_part = first_sum[:, :split_rows]
    second_sum = scattered("tp", first_sum[:, split_rows:])[0].astype(jnp.float32)
    split_part = split_part.astype(jnp.float32)
    out_part = from_device(split_part[:, : split_rows // 2], wide)
    query_part = from_device(split_part[:, split_rows // 2 :], wide)
    sizes = [
        (keyval_eff.shape[1] // rank) * wide,
        wide,
        main,
        model_width // rank * extra,
        model_width // rank * extra,
        8,
    ]
    starts = [sum(sizes[:at]) for at in range(len(sizes))]
    pieces = [second_sum[at : at + size] for at, size in zip(starts, sizes)]
    keyval_part = from_device(pieces[0], wide)

    def rows_of(value, first_row, row_count):
        return value[:, first_row : first_row + row_count].reshape(-1, value.shape[-1])

    down_sum, gate_sum, up_sum = (
        value.astype(jnp.float32) for value in (down_sum, gate_sum, up_sum)
    )
    return (
        result,
        tokens_grad,
        pieces[5][1, :main],
        pieces[5][0, :main],
        rows_of(query_part, 0, main),
        keyval_part[:main],
        rows_of(out_part, 0, main).T,
        gate_sum[:shard_rows],
        up_sum[:shard_rows],
        down_sum[:shard_rows].T,
        pieces[1][:main],
        rows_of(query_part, main, extra),
        keyval_part[main:],
        rows_of(out_part, main, extra).T,
        from_device(pieces[4], extra),
        pieces[2],
        gate_sum[shard_rows:],
        up_sum[shard_rows:],
        down_sum[shard_rows:].T,
        from_device(pieces[3], extra),
    )


def solution(mesh):
    in_specs = (
        P(("fsdp", "tp"), None),
        P(("fsdp", "tp")),
        P(("fsdp", "tp")),
        P("fsdp", "tp"),
        P(("fsdp", "tp"), None),
        P("tp", "fsdp"),
        P("fsdp", "tp"),
        P("fsdp", "tp"),
        P("tp", "fsdp"),
        P(("fsdp", "tp"), None),
        P("fsdp", "tp"),
        P(("fsdp", "tp"), None),
        P("tp", "fsdp"),
        P(("fsdp", "tp"), None),
        P(("fsdp", "tp"), None),
        P("fsdp", "tp"),
        P("fsdp", "tp"),
        P("tp", "fsdp"),
        P(("fsdp", "tp"), None),
        P(),
        P(("fsdp", "tp"), None),
    )
    out_specs = (
        P(("fsdp", "tp"), None),
        P(("fsdp", "tp"), None),
        P(("fsdp", "tp")),
        P(("fsdp", "tp")),
        P("fsdp", "tp"),
        P(("fsdp", "tp"), None),
        P("tp", "fsdp"),
        P("fsdp", "tp"),
        P("fsdp", "tp"),
        P("tp", "fsdp"),
        P(("fsdp", "tp"), None),
        P("fsdp", "tp"),
        P(("fsdp", "tp"), None),
        P("tp", "fsdp"),
        P(("fsdp", "tp"), None),
        P(("fsdp", "tp"), None),
        P("fsdp", "tp"),
        P("fsdp", "tp"),
        P("tp", "fsdp"),
        P(("fsdp", "tp"), None),
    )
    return jax.shard_map(shards, mesh=mesh, in_specs=in_specs, out_specs=out_specs, check_vma=False)
```

time: 3230 us -> 1540 us (0.48)
  waiting for transfers between devices: 2480 us -> 1090 us
  blocking collectives: 202 us -> 0 us
  matrix products: 438 us -> 242 us
  local copies, waits for them, and re-layouts: 40.9 us -> 117 us
    reduce_scatter x15 -> x9, waiting for transfers between devices: 1270 us -> 566 us  [scattered(): return lax.psum_scatter(value, axis_names, scatter_dimension=0, tiled=True)]
    unnamed x44 -> x18, waiting for transfers between devices: 547 us -> 0.97 us
    dot_general x12 -> x0, matrix products: 190 us -> none  [the longest x6 114 us: exact_transposed_times(): lax.dot_general(left_mat.astype(jnp.float32), right_mat, (((0,), (0,)), (...]
    all_gather x17 -> x9, waiting for transfers between devices: 665 us -> 518 us  [the longest x6 370 us: joined(): return lax.all_gather(value, axis_names, axis=axis, tiled=True)]
    all_gather x5 -> x0, blocking collectives: 121 us -> none  [the longest x1 74 us: shards(): lax.all_gather(key_value_delta_output, ('fsdp', 'tp'), axis=0, tiled=True)]
    unnamed x2 -> x0, blocking collectives: 81.8 us -> none
    dot_general x10 -> x14, matrix products: 72.3 us -> 85.3 us  [transposed_times(): lax.dot_general(left_mat, right_mat, (((0,), (0,)), ((), ())), preferred_...]
    dot_general x12 -> x17, matrix products: 73.5 us -> 79.7 us  [times_transposed(): lax.dot_general(left_mat, right_mat, (((1,), (1,)), ((), ())), preferred_...]
  transfers between devices with their start and end apart: 41 -> 20, of which waited for: 32 -> 17; matrix products, arithmetic and copies ran while one was open for 12% -> 15% of each run, Pallas kernels for 0% -> 0%
where the time goes in v1:
time: 1540 us; the launch traced here: 1530 us
  waiting for transfers between devices  1090 us (71%)
  matrix products  242 us (16%)
  local copies, waits for them, and re-layouts  117 us (8%)
  other arithmetic  53.4 us (3%)
  loops' own time  19.3 us (1%)
  between operations  16.8 us (1%)
    reduce_scatter x9, waiting for transfers between devices, scattered(): return lax.psum_scatter(value, axis_names, scatter_dimension=0, tiled=True)  566 us
    all_gather x6, waiting for transfers between devices, joined(): return lax.all_gather(value, axis_names, axis=axis, tiled=True)  370 us
    all_gather x2, waiting for transfers between devices, gather(): lax.all_gather(jnp.concatenate(self.pieces, axis=0), axis_names, axis=0)  105 us
    dot_general x14, matrix products, transposed_times(): lax.dot_general(left_mat, right_mat, (((0,), (0,)), ((), ())), preferred_...  85.3 us
    dot_general x17, matrix products, times_transposed(): lax.dot_general(left_mat, right_mat, (((1,), (1,)), ((), ())), preferred_...  79.7 us
    dot_general x16, matrix products, matrix_multiply(): return jnp.dot(left_mat, right_mat, preferred_element_type=jnp.float32)  76.7 us
    unnamed x244, local copies, waits for them, and re-layouts  53 us
    all_gather x1, waiting for transfers between devices, shards(): lax.all_gather(jnp.concatenate([gate_delta_output, up_delta_output, down_...  43.5 us
  transfers between devices with their start and end apart: 20, of which 17 were waited for; matrix products, arithmetic and copies ran while one was open for 15% of the time, Pallas kernels for 0%

profile of v1, /device:TPU:0, one launch (start us, length us, event | category | flops | bytes accessed | tf_op | source)
XLA Modules:
  0.0 1534.5 jit_solution(13558420954706123454)
XLA Ops:
  21.3 72.4 %all-gather.13.cloned.1.call-done = bf16[512,4096]{1,0:T(8,128)(2,1)} async-done(((bf16[128,4096]{1,0:T(8,128)(2,1)}), bf16[512,4096]{1,0:T(8,128)(2,1)}) %all-gather.13.cloned.1.call-update) | async-done | bytes 4194320 | tf_op jit(solution)/shard_map/all_gather | solution.py:69
  95.8 37.7 %all-gather.27.cloned.1.call-done = bf16[9216,256]{1,0:T(8,128)(2,1)} async-done(((bf16[1152,256]{1,0:T(8,128)(2,1)}), bf16[9216,256]{1,0:T(8,128)(2,1)}) %all-gather.27.cloned.1.call-update) | async-done | bytes 4718608 | tf_op jit(solution)/shard_map/all_gather | solution.py:95
  140.1 67.4 %all-gather.25.cloned.1.call-done = bf16[13056,256]{1,0:T(8,128)(2,1)} async-done(((bf16[408,256]{1,0:T(8,128)(2,1)}), bf16[13056,256]{1,0:T(8,128)(2,1)}) %all-gather.25.cloned.1.call-update) | async-done | bytes 6684688 | tf_op jit(solution)/shard_map/all_gather | solution.py:95
  243.0 29.8 %while.36 = (s32[]{:T(128)}, bf16[2,512,256]{1,2,0:T(8,128)(2,1)S(1)}, f32[2,512]{1,0:T(2,128)}, s32[]{:T(128)}, s32[]{:T(128)}, /*index=5*/s32[]{:T(128)}, s32[...) while((s32[]{:T(128)}, ...), condition=%wide.region_4.5_spmd.clone.clone.clone, body=%wide.region_1.4_spmd.clone.clone.sunk.clone | while | flops 542118912 | bytes 8154295 | solution.py:269
  278.5 41.1 %reduce-scatter.10.cloned.1.call-done = bf16[128,2048]{1,0:T(8,128)(2,1)} async-done(((bf16[512,2048]{1,0:T(8,128)(2,1)}), bf16[128,2048]{1,0:T(8,128)(2,1)}) %reduce-scatter.10.cloned.1.call-update) | async-done | bytes 524304 | tf_op jit(solution)/shard_map/reduce_scatter | solution.py:73
  323.0 43.5 %all-gather.29.cloned.1.call-done = bf16[768,4096]{1,0:T(8,128)(2,1)} async-done(((bf16[96,4096]{1,0:T(8,128)(2,1)}), bf16[768,4096]{1,0:T(8,128)(2,1)}) %all-gather.29.cloned.1.call-update) | async-done | bytes 6291472 | tf_op jit(solution)/shard_map/all_gather | solution.py:197
  366.6 5.0 fusion.119
  384.3 29.9 %all-gather.15.cloned.1.call-done = bf16[512,2048]{1,0:T(8,128)(2,1)} async-done(((bf16[128,2048]{1,0:T(8,128)(2,1)}), bf16[512,2048]{1,0:T(8,128)(2,1)}) %all-gather.15.cloned.1.call-update) | async-done | bytes 2097168 | tf_op jit(solution)/shard_map/all_gather | solution.py:69
  414.2 91.0 %all-gather.19.cloned.1.call-done = bf16[2048,4096]{1,0:T(8,128)(2,1)} async-done(((bf16[256,4096]{1,0:T(8,128)(2,1)}), bf16[2048,4096]{1,0:T(8,128)(2,1)}) %all-gather.19.cloned.1.call-update) | async-done | bytes 16777232 | tf_op jit(solution)/shard_map/all_gather | solution.py:69
  505.3 14.9 fusion.130
  520.2 77.3 %all-gather.17.cloned.1.call-done = bf16[2048,4096]{1,0:T(8,128)(2,1)} async-done(((bf16[256,4096]{1,0:T(8,128)(2,1)}), bf16[2048,4096]{1,0:T(8,128)(2,1)}) %all-gather.17.cloned.1.call-update) | async-done | bytes 16777232 | tf_op jit(solution)/shard_map/all_gather | solution.py:69
  597.5 15.0 fusion.129
  612.5 80.5 %all-gather.21.cloned.1.call-done = bf16[4096,2048]{1,0:T(8,128)(2,1)} async-done(((bf16[4096,256]{1,0:T(8,128)(2,1)}), bf16[4096,2048]{1,0:T(8,128)(2,1)}) %all-gather.21.cloned.1.call-update) | async-done | bytes 16777232 | tf_op jit(solution)/shard_map/all_gather | solution.py:69
  693.0 23.1 %multiply_convert_fusion.1 = (bf16[512,4096]{1,0:T(8,128)(2,1)}, bf16[512,4096]{1,0:T(8,128)(2,1)}, bf16[512,4096]{1,0:T(8,128)(2,1)}) fusion(f32[512,4096]{1,0:T(8,128)} %fusion.129, f32[512,4096]{1,0:T(8,128)} %fusion.130, bf16[4096,2048]{1,0:T(8,128)(2,1)} %all-gather.21.cloned.1.call-done, bf16[512,4096]{1,0:T(8,128)(2,1)} %all-gather.13.cloned.1.call-done), kind=kOutput, calls=%fused_computation.61 | convolution fusion | flops 8644460544 | bytes 48234496 | tf_op jit(solution)/shard_map/dot_general | solution.py:25
  716.1 15.5 %fusion.131 = f32[512,2048]{1,0:T(8,128)} fusion(bf16[512,4096]{1,0:T(8,128)(2,1)} %get-tuple-element.606, bf16[2048,4096]{1,0:T(8,128)(2,1)} %all-gather.17.cloned.1.call-done), kind=kOutput, calls=%fused_computation.401 | convolution fusion | flops 8589934592 | bytes 25165824 | tf_op jit(solution)/shard_map/dot_general | solution.py:25
  731.6 14.2 add_convert_fusion
  745.9 43.7 %reduce-scatter.14.cloned.1.call-done = bf16[128,2048]{1,0:T(8,128)(2,1)} async-done(((bf16[512,2048]{1,0:T(8,128)(2,1)}), bf16[128,2048]{1,0:T(8,128)(2,1)}) %reduce-scatter.14.cloned.1.call-update) | async-done | bytes 524304 | tf_op jit(solution)/shard_map/reduce_scatter | solution.py:73
  806.9 6.9 convolution_convert_fusion.8
  813.7 7.6 convolution_convert_fusion.9
  821.4 18.5 %all-gather.23.cloned.1.call-done = bf16[512,2048]{1,0:T(8,128)(2,1)} async-done(((bf16[128,2048]{1,0:T(8,128)(2,1)}), bf16[512,2048]{1,0:T(8,128)(2,1)}) %all-gather.23.cloned.1.call-update) | async-done | bytes 2097168 | tf_op jit(solution)/shard_map/all_gather | solution.py:69
  843.8 31.1 %while.37 = (s32[]{:T(128)}, f32[1024,256]{1,0:T(8,128)}, f32[1024,256]{1,0:T(8,128)}, f32[2,512,256]{1,2,0:T(8,128)}, s32[]{:T(128)}, /*index=5*/s32[]{:T(128)}...) while((s32[]{:T(128)}, f32[1024,256]{1,0:T(8,128)}, ...), condition=%wide.region_12.13_spmd.clone.clone.clone, body=%wide.region_10.12_spmd.clone.clone.sunk.clone | while | flops 1348998144 | bytes 23086816 | solution.py:337
  930.6 15.5 %convolution_convert_fusion.6 = bf16[512,2048]{1,0:T(8,128)(2,1)} fusion(bf16[512,4096]{1,0:T(8,128)(2,1)} %get-tuple-element.607, bf16[4096,2048]{1,0:T(8,128)(2,1)} %all-gather.21.cloned.1.call-done), kind=kOutput, calls=%fused_computation.86 | convolution fusion | flops 8590983168 | bytes 23068672 | tf_op jit(solution)/shard_map/dot_general | solution.py:21
  953.0 63.0 %reduce-scatter.18.cloned.1.call-done = bf16[4,704,256]{2,1,0:T(8,128)(2,1)} async-done(((bf16[32,704,256]{2,1,0:T(8,128)(2,1)}), bf16[4,704,256]{2,1,0:T(8,128)(2,1)}) %reduce-scatter.18.cloned.1.call-update) | async-done | bytes 1441808 | tf_op jit(solution)/shard_map/reduce_scatter | solution.py:73
  1018.2 15.1 convolution_convert_fusion
  1040.7 12.9 convolution_convert_fusion.2
  1055.2 15.1 convolution_convert_fusion.1
  1072.7 34.3 %reduce-scatter.12.cloned.1.call-done = bf16[128,2048]{1,0:T(8,128)(2,1)} async-done(((bf16[512,2048]{1,0:T(8,128)(2,1)}), bf16[128,2048]{1,0:T(8,128)(2,1)}) %reduce-scatter.12.cloned.1.call-update) | async-done | bytes 524304 | tf_op jit(solution)/shard_map/reduce_scatter | solution.py:73
  1114.0 18.5 %reduce-scatter.20.cloned.1.call-done = bf16[1,416,256]{2,1,0:T(8,128)(2,1)} async-done(((bf16[4,416,256]{2,1,0:T(8,128)(2,1)}), bf16[1,416,256]{2,1,0:T(8,128)(2,1)}) %reduce-scatter.20.cloned.1.call-update) | async-done | bytes 213008 | tf_op jit(solution)/shard_map/reduce_scatter | solution.py:73
  1136.1 125.6 %reduce-scatter.26.cloned.1.call-done = bf16[288,4096]{1,0:T(8,128)(2,1)} async-done(((bf16[2304,4096]{1,0:T(8,128)(2,1)}), bf16[288,4096]{1,0:T(8,128)(2,1)}) %reduce-scatter.26.cloned.1.call-update) | async-done | bytes 2359312 | tf_op jit(solution)/shard_map/reduce_scatter | solution.py:73
  1268.4 5.7 copy.77
  1274.1 117.6 %reduce-scatter.22.cloned.1.call-done = bf16[288,4096]{1,0:T(8,128)(2,1)} async-done(((bf16[2304,4096]{1,0:T(8,128)(2,1)}), bf16[288,4096]{1,0:T(8,128)(2,1)}) %reduce-scatter.22.cloned.1.call-update) | async-done | bytes 2359312 | tf_op jit(solution)/shard_map/reduce_scatter | solution.py:73
  1399.4 122.2 %reduce-scatter.24.cloned.1.call-done = bf16[288,4096]{1,0:T(8,128)(2,1)} async-done(((bf16[2304,4096]{1,0:T(8,128)(2,1)}), bf16[288,4096]{1,0:T(8,128)(2,1)}) %reduce-scatter.24.cloned.1.call-update) | async-done | bytes 2359312 | tf_op jit(solution)/shard_map/reduce_scatter | solution.py:73
  (444 shorter events, 247.9 us)
Async XLA Ops:
  7.3 86.4 %all-gather.13.cloned.1.call-start = ((), (), s32[]{:S(2)}) async-start(), calls=%async_computation.9 | async-start | bytes 5242880 | tf_op jit(solution)/shard_map/all_gather | solution.py:69
  9.6 123.9 %all-gather.27.cloned.1.call-start = ((), (), s32[]{:S(2)}) async-start(), calls=%async_computation.25 | async-start | bytes 5308416 | tf_op jit(solution)/shard_map/all_gather | solution.py:95
  16.2 191.3 %all-gather.25.cloned.1.call-start = ((), (), s32[]{:S(2)}) async-start(), calls=%async_computation.24 | async-start | bytes 6893568 | tf_op jit(solution)/shard_map/all_gather | solution.py:95
  17.3 302.3 %reduce-scatter.10.cloned.1.call-start = ((), (), s32[]{:S(2)}) async-start(), calls=%async_computation.10 | async-start | bytes 2621440 | tf_op jit(solution)/shard_map/reduce_scatter | solution.py:73
  18.7 202.1 %copy-start.70 = (f32[128]{0:T(128)}, f32[128]{0:T(128)S(1)}, u32[]{:S(2)}) copy-start(f32[128]{0:T(128)S(1)} %multiply_power_fusion) | copy-start | bytes 1540
  18.7 202.1 %copy-start.58 = (f32[512]{0:T(512)}, f32[512]{0:T(512)S(1)}, u32[]{:S(2)}) copy-start(f32[512]{0:T(512)S(1)} %add_convert_fusion.6) | copy-start | bytes 6148
  21.3 211.6 %copy-start.16 = (f32[512,128]{0,1:T(8,128)}, f32[512,128]{0,1:T(8,128)S(1)}, u32[]{:S(2)}) copy-start(f32[512,128]{0,1:T(8,128)S(1)} %get-tuple-element.690) | copy-start | bytes 786436
  95.8 122.6 %copy-start.67 = (f32[512]{0:T(512)}, f32[512]{0:T(512)S(1)}, u32[]{:S(2)}) copy-start(f32[512]{0:T(512)S(1)} %add_rsqrt_fusion) | copy-start | bytes 6148
  139.0 84.1 %copy-start.34 = (bf16[8,32,256]{2,1,0:T(8,128)(2,1)}, bf16[8,32,256]{2,1,0:T(8,128)(2,1)S(1)}, u32[]{:S(2)}) copy-start(bf16[8,32,256]{2,1,0:T(8,128)(2,1)S(1)} %get-tuple-element.640) | copy-start | bytes 393220
  139.0 84.1 %copy-start.36 = (bf16[8,32,256]{2,1,0:T(8,128)(2,1)}, bf16[8,32,256]{2,1,0:T(8,128)(2,1)S(1)}, u32[]{:S(2)}) copy-start(bf16[8,32,256]{2,1,0:T(8,128)(2,1)S(1)} %get-tuple-element.641) | copy-start | bytes 393220
  139.0 96.1 %copy-start.38 = (bf16[8,32,256]{2,1,0:T(8,128)(2,1)}, bf16[8,32,256]{2,1,0:T(8,128)(2,1)S(1)}, u32[]{:S(2)}) copy-start(bf16[8,32,256]{2,1,0:T(8,128)(2,1)S(1)} %get-tuple-element.638) | copy-start | bytes 393220
  222.9 16.5 %collective-permute-start = (bf16[512,512]{0,1:T(8,128)(2,1)}, bf16[512,512]{0,1:T(8,128)(2,1)}, u32[]{:S(2)}, u32[]{:S(2)}) collective-permute-start(bf16[512,512]{0,1:T(8,128)(2,1)} %pad_maximum_fusion.7), channel_id=1, source_target_pairs={{0,4},{4,0},{8,12},{12,8},{16,20},{20,16},{24,28},{28,24},{1,5},{5... | collective-permute-start | bytes 1572872 | tf_op jit(solution)/shard_map/ppermute | solution.py:17
  277.3 89.3 %all-gather.29.cloned.1.call-start = ((), (), s32[]{:S(2)}) async-start(), calls=%async_computation.26 | async-start | bytes 7077888 | tf_op jit(solution)/shard_map/all_gather | solution.py:197
  278.3 135.9 %all-gather.15.cloned.1.call-start = ((), (), s32[]{:S(2)}) async-start(), calls=%async_computation.11 | async-start | bytes 2621440 | tf_op jit(solution)/shard_map/all_gather | solution.py:69
  278.5 513.3 %copy-start.46 = (f32[2048]{0:T(1024)}, f32[2048]{0:T(1024)S(1)}, u32[]{:S(2)}) copy-start(f32[2048]{0:T(1024)S(1)} %mul.399) | copy-start | bytes 24580
  320.9 470.9 %copy-start.65 = (f32[128]{0:T(128)}, f32[128]{0:T(128)S(1)}, u32[]{:S(2)}) copy-start(f32[128]{0:T(128)S(1)} %fusion.101) | copy-start | bytes 1540
  323.0 182.3 %all-gather.19.cloned.1.call-start = ((), (), s32[]{:S(2)}) async-start(), calls=%async_computation.13 | async-start | bytes 18874368 | tf_op jit(solution)/shard_map/all_gather | solution.py:69
  375.9 221.6 %all-gather.17.cloned.1.call-start = ((), (), s32[]{:S(2)}) async-start(), calls=%async_computation.12 | async-start | bytes 18874368 | tf_op jit(solution)/shard_map/all_gather | solution.py:69
  380.4 312.6 %all-gather.21.cloned.1.call-start = ((), (), s32[]{:S(2)}) async-start(), calls=%async_computation.14 | async-start | bytes 18874368 | tf_op jit(solution)/shard_map/all_gather | solution.py:69
  384.3 405.3 %reduce-scatter.14.cloned.1.call-start = ((), (), s32[]{:S(2)}) async-start(), calls=%async_computation.16 | async-start | bytes 2621440 | tf_op jit(solution)/shard_map/reduce_scatter | solution.py:73
  731.6 58.0 %copy-start.3 = (bf16[128,2048]{1,0:T(8,128)(2,1)S(1)}, bf16[128,2048]{1,0:T(8,128)(2,1)}, u32[]{:S(2)}) copy-start(bf16[128,2048]{1,0:T(8,128)(2,1)} %reduce-scatter.10.cloned.1.call-done) | copy-start | bytes 1572868
  745.8 94.0 %all-gather.23.cloned.1.call-start = ((), (), s32[]{:S(2)}) async-start(), calls=%async_computation.17 | async-start | bytes 2621440 | tf_op jit(solution)/shard_map/all_gather | solution.py:69
  794.9 221.2 %reduce-scatter.18.cloned.1.call-start = ((), (), s32[]{:S(2)}) async-start(), calls=%async_computation.19 | async-start | bytes 12976128 | tf_op jit(solution)/shard_map/reduce_scatter | solution.py:73
  879.2 20.8 %collective-permute-start.1 = (f32[512,512]{0,1:T(8,128)}, f32[512,512]{0,1:T(8,128)}, u32[]{:S(2)}, u32[]{:S(2)}) collective-permute-start(f32[512,512]{0,1:T(8,128)} %broadcast_select_fusion), channel_id=1, source_target_pairs={{0,4},{4,0},{8,12},{12,8},{16,20},{20,16},{24,28},{28,24},{1,5},{5... | collective-permute-start | bytes 3145736 | tf_op jit(solution)/shard_map/ppermute | solution.py:17
  929.8 140.7 %reduce-scatter.16.cloned.1.call-start = ((), (), s32[]{:S(2)}) async-start(), calls=%async_computation.18 | async-start | bytes 2621440 | tf_op jit(solution)/shard_map/reduce_scatter | solution.py:73
  930.5 176.5 %reduce-scatter.12.cloned.1.call-start = ((), (), s32[]{:S(2)}) async-start(), calls=%async_computation.15 | async-start | bytes 2621440 | tf_op jit(solution)/shard_map/reduce_scatter | solution.py:73
  946.1 186.5 %reduce-scatter.20.cloned.1.call-start = ((), (), s32[]{:S(2)}) async-start(), calls=%async_computation.20 | async-start | bytes 1064960 | tf_op jit(solution)/shard_map/reduce_scatter | solution.py:73
  1018.2 243.5 %reduce-scatter.26.cloned.1.call-start = ((), (), s32[]{:S(2)}) async-start(), calls=%async_computation.23 | async-start | bytes 21233664 | tf_op jit(solution)/shard_map/reduce_scatter | solution.py:73
  1033.4 358.3 %reduce-scatter.22.cloned.1.call-start = ((), (), s32[]{:S(2)}) async-start(), calls=%async_computation.21 | async-start | bytes 21233664 | tf_op jit(solution)/shard_map/reduce_scatter | solution.py:73
  1053.6 468.0 %reduce-scatter.24.cloned.1.call-start = ((), (), s32[]{:S(2)}) async-start(), calls=%async_computation.22 | async-start | bytes 21233664 | tf_op jit(solution)/shard_map/reduce_scatter | solution.py:73
  1135.4 133.0 %copy-start.75 = (f32[8,2048]{1,0:T(8,128)}, f32[8,2048]{1,0:T(8,128)S(1)}, u32[]{:S(2)}) copy-start(f32[8,2048]{1,0:T(8,128)S(1)} %get-tuple-element.664) | copy-start | bytes 196612
  1135.4 133.0 %copy-start.76 = (f32[8,2048]{1,0:T(8,128)}, f32[8,2048]{1,0:T(8,128)S(1)}, u32[]{:S(2)}) copy-start(f32[8,2048]{1,0:T(8,128)S(1)} %get-tuple-element.665) | copy-start | bytes 196612
  (76 other events, 631.2 us)
Sparse Core Ops, SparseCore 0:
  10.2 83.4 all-gather.12
  96.2 37.2 all-gather.26
  136.9 70.5 all-gather.24
  277.4 42.1 reduce-scatter.9
  321.9 44.5 all-gather.28
  368.5 45.6 all-gather.14
  416.7 88.5 all-gather.18
  507.7 89.7 all-gather.16
  599.9 93.0 all-gather.20
  745.9 43.6 reduce-scatter.13
  795.0 44.8 all-gather.22
  929.9 86.1 reduce-scatter.17
  1018.3 43.6 reduce-scatter.15
  1064.1 42.7 reduce-scatter.11
  1109.1 23.3 reduce-scatter.19
  1136.0 125.6 reduce-scatter.25
  1265.2 126.4 reduce-scatter.21
  1395.1 126.4 reduce-scatter.23

commit v2 on v1

--- a/solution.py
+++ b/solution.py
@@ -31,12 +31,6 @@
     return lax.dot_general(
         left_mat, right_mat, (((0,), (0,)), ((), ())), preferred_element_type=jnp.float32
     )
-
-
-def merged_weight(shared_base, delta_left_factor, delta_right_factor):
-    return (
-        shared_base.astype(jnp.float32) + matrix_multiply(delta_left_factor, delta_right_factor)
-    ).astype(jnp.bfloat16)
 
 
 def normalize(values, gain_vec):
@@ -103,11 +97,130 @@
         return results
 
 
-def blocked(main_cols, extra_cols, parts):
-    rows = main_cols.shape[0]
+def chip_groups(fsdp_size):
+    return [list(range(core, fsdp_size, 2)) for core in range(2)]
+
+
+def chip_gather(value):
+    fsdp_size = lax.axis_size("fsdp")
+    chips = fsdp_size // 2
+    if chips != 4:
+        whole = lax.all_gather(value, "fsdp", axis=0, axis_index_groups=chip_groups(fsdp_size))
+        return [whole[at] for at in range(chips)]
+    half = value.shape[0] // 2
+    along_x = partner(value, "fsdp", 1)
+    along_y = partner(value, "fsdp", 2)
+    far_low = partner(along_x[:half], "fsdp", 2)
+    far_high = partner(along_y[half:], "fsdp", 1)
+    return [value, along_x, along_y, jnp.concatenate([far_low, far_high], axis=0)]
+
+
+def chip_scatter(pieces):
+    fsdp_size = lax.axis_size("fsdp")
+    if fsdp_size // 2 != 4:
+        return lax.psum_scatter(
+            jnp.concatenate(pieces, axis=0),
+            "fsdp",
+            scatter_dimension=0,
+            tiled=True,
+            axis_index_groups=chip_groups(fsdp_size),
+        ).astype(jnp.float32)
+
+    half = pieces[0].shape[1] // 2
+    left = [piece[:, :half] for piece in pieces]
+    right = [piece[:, half:] for piece in pieces]
+    left_far = partner(left[3], "fsdp", 1)
+    right_far = partner(right[3], "fsdp", 2)
+    left_near = partner(left[1], "fsdp", 1)
+    right_near = partner(right[2], "fsdp", 2)
+
+    def total(*values):
+        return sum(value.astype(jnp.float32) for value in values)
+
+    left_last = partner(low(total(left[2], left_far)), "fsdp", 2)
+    right_last = partner(low(total(right[1], right_far)), "fsdp", 1)
     return jnp.concatenate(
-        [main_cols.reshape(rows, parts, -1), extra_cols.reshape(rows, parts, -1)], axis=2
-    ).reshape(rows, -1)
+        [total(left[0], left_near, left_last), total(right[0], right_near, right_last)], axis=1
+    )
+
+
+def chip_relative(value, axis):
+    if lax.axis_size("fsdp") // 2 != 4:
+        return value
+    placed = lax.axis_index("fsdp")
+    size = value.shape[axis] // 4
+    blocks = [lax.slice_in_dim(value, at * size, (at + 1) * size, axis=axis) for at in range(4)]
+    across_x = (placed // 2) % 2 == 1
+    across_y = placed // 4 == 1
+    blocks = [jnp.where(across_x, blocks[at ^ 1], blocks[at]) for at in range(4)]
+    blocks = [jnp.where(across_y, blocks[at ^ 2], blocks[at]) for at in range(4)]
+    return jnp.concatenate(blocks, axis=axis)
+
+
+def both_cores(value):
+    return jnp.concatenate([value, partner(value, "fsdp", 0)], axis=0)
+
+
+def core_sum(value):
+    rows = value.shape[0] // 2
+    return low(value[:rows] + partner(low(value[rows:]), "fsdp", 0).astype(jnp.float32))
+
+
+def own_half(second, value, other=False):
+    half = value.shape[1] // 2
+    return jnp.where(second != other, value[:, half:], value[:, :half])
+
+
+def in_order(second, mine, theirs, axis):
+    return jnp.where(
+        second,
+        jnp.concatenate([theirs, mine], axis=axis),
+        jnp.concatenate([mine, theirs], axis=axis),
+    )
+
+
+def tp_rows(value):
+    size = lax.axis_size("tp")
+    rows = value.shape[0]
+    arrived = [
+        lax.ppermute(value, "tp", [(at, (at + shift) % size) for at in range(size)])
+        for shift in range(1, size)
+    ]
+    cycle = arrived[::-1] + [value] + arrived[:0:-1]
+    first = (size - 1 - lax.axis_index("tp")) * rows
+    return lax.dynamic_slice_in_dim(
+        jnp.concatenate(cycle + [arrived[0]], axis=0), first, size * rows
+    )
+
+
+def gathered_wide(second, main, extra):
+    shard = jnp.concatenate([main, extra], axis=0)
+    theirs = partner(own_half(second, shard, True), "fsdp", 0)
+    pieces = chip_gather(in_order(second, own_half(second, shard), theirs, 0))
+    rows, wide = main.shape[0], shard.shape[0]
+    return jnp.concatenate(
+        [piece[at * wide : at * wide + rows] for piece in pieces for at in range(2)]
+        + [piece[at * wide + rows : (at + 1) * wide] for piece in pieces for at in range(2)],
+        axis=0,
+    )
+
+
+def scattered_wide(second, value, rows):
+    chips = lax.axis_size("fsdp") // 2
+    extra = (value.shape[0] - chips * 2 * rows) // (2 * chips)
+    main_end = chips * 2 * rows
+    pieces = []
+    for chip in range(chips):
+        for core in range(2):
+            at = 2 * chip + core
+            pieces.append(value[at * rows : (at + 1) * rows])
+            pieces.append(value[main_end + at * extra : main_end + (at + 1) * extra])
+    pieces = [jnp.concatenate(pieces[4 * at : 4 * at + 4], axis=0) for at in range(chips)]
+    summed = chip_scatter(pieces)
+    wide = rows + extra
+    mine = jnp.where(second, summed[wide:], summed[:wide])
+    theirs = partner(low(jnp.where(second, summed[:wide], summed[wide:])), "fsdp", 0)
+    return in_order(second, mine, theirs.astype(jnp.float32), 1)
 
 
 def shards(
@@ -151,6 +264,14 @@
     key_positions = jnp.arange(key_rows, dtype=jnp.int32)
     scaling = HEAD_WIDTH ** (-0.5)
 
+    second = second_half == 1
+
+    down_wide = gathered_wide(second, down_shared_weight.T, down_delta_input.T)
+    gate_wide = gathered_wide(second, gate_shared_weight, gate_delta_output)
+    up_wide = gathered_wide(second, up_shared_weight, up_delta_output)
+
+    tokens_span = tp_rows(tokens)
+
     rank = gate_delta_output.shape[0] * fsdp_size
     common = Packed(rank)
     gain_rows = jnp.concatenate([attention_norm_gain[None], feedforward_norm_gain[None]], axis=0)
@@ -173,60 +294,53 @@
     gains = gains.reshape(parts, 8, rank)[:, :2, : gain_rows.shape[1]].astype(jnp.float32)
     gain_attn = gains[:, 0].reshape(-1)
     gain_mlp = gains[:, 1].reshape(-1)
-
-    rows_both = joined("tp", jnp.concatenate([tokens, cotangent], axis=1))
-    tokens_span = rows_both[:, :model_width]
-    grad_span = rows_both[:, model_width:]
-
-    width = output_shared_weight.shape[1]
-    heads_pack = Packed(width)
-    heads_pack.add(query_shared_weight)
-    heads_pack.add(query_delta_output)
-    heads_pack.add(output_delta_input.T)
-    heads_pack.add(output_shared_weight)
-    query_complete, query_delta_product, out_down_t, out_stack = heads_pack.gather("fsdp")
-    out_rows = output_shared_weight.shape[0]
-    out_full = (
-        out_stack.reshape(fsdp_size, out_rows, width).transpose(1, 0, 2).reshape(out_rows, -1)
-    )
-    query_eff = merged_weight(query_complete, delta_attention, query_delta_product)
-    keyval_eff = merged_weight(key_value_complete, delta_attention, key_value_delta_product)
-    out_eff = low(out_full.astype(jnp.float32) + transposed_times(out_down_t, output_delta_product))
-
-    delta_rows = gate_delta_output.shape[0]
-    delta_stack = lax.all_gather(
-        jnp.concatenate([gate_delta_output, up_delta_output, down_delta_input.T], axis=0),
+    keyval_wide = jnp.concatenate([key_value_complete, key_value_delta_product], axis=0)
+
+    head_cols = query_shared_weight.shape[1]
+    shard_rows = query_shared_weight.shape[0]
+    heads_stack = lax.all_gather(
+        jnp.concatenate(
+            [
+                jnp.concatenate([query_shared_weight, output_shared_weight.T], axis=1),
+                jnp.concatenate([query_delta_output, output_delta_input.T], axis=1),
+            ],
+            axis=0,
+        ),
         "fsdp",
         axis=0,
     )
-    gate_delta_product, up_delta_product, down_in_t = (
-        delta_stack[:, at * delta_rows : (at + 1) * delta_rows].reshape(rank, -1) for at in range(3)
-    )
-    shard_rows = gate_shared_weight.shape[0]
-    delta_feedforward_rows = lax.dynamic_slice_in_dim(
-        delta_feedforward, placed * shard_rows, shard_rows
-    )
-    down_delta_cols = lax.dynamic_slice_in_dim(
-        down_delta_product, placed * shard_rows, shard_rows, axis=1
-    )
-    down_eff = joined(
-        "fsdp",
-        low(
-            down_shared_weight.astype(jnp.float32) + transposed_times(down_in_t, down_delta_cols)
-        ),
-        axis=1,
-    )
-    gate_eff = joined(
-        "fsdp", merged_weight(gate_shared_weight, delta_feedforward_rows, gate_delta_product)
-    )
-    up_eff = joined(
-        "fsdp", merged_weight(up_shared_weight, delta_feedforward_rows, up_delta_product)
-    )
+    heads_wide = jnp.concatenate(
+        [
+            heads_stack[:, :shard_rows].reshape(-1, 2 * head_cols),
+            heads_stack[:, shard_rows:].reshape(-1, 2 * head_cols),
+        ],
+        axis=0,
+    )
+    query_wide = heads_wide[:, :head_cols]
+    out_wide = heads_wide[:, head_cols:]
+
+    grad_span = joined("tp", cotangent)
+    down_delta_relative = chip_relative(down_delta_product, 0)
+    grad_wide = both_cores(
+        jnp.concatenate(
+            [
+                chip_relative(grad_span, 1),
+                low(times_transposed(grad_span, down_delta_relative)),
+            ],
+            axis=1,
+        )
+    )
+    down_delta_both = chip_relative(down_delta_relative, 1)
+    delta_relative = chip_relative(delta_feedforward, 1)
+    delta_both = chip_relative(delta_relative, 0)
 
     inputs = tokens.astype(jnp.float32)
     inputs_span = tokens_span.astype(jnp.float32)
     normed_span = low(normalize(inputs_span, gain_attn))
-    keyval_span = matrix_multiply(normed_span, keyval_eff)
+    normed_attn_wide = jnp.concatenate(
+        [normed_span, low(matrix_multiply(normed_span, delta_attention))], axis=1
+    )
+    keyval_span = matrix_multiply(normed_attn_wide, keyval_wide)
     keys_span = rotate(keyval_span[:, None, :HEAD_WIDTH], span_positions, 1.0)[:, 0, :]
     keyval_low = low(jnp.concatenate([keys_span, keyval_span[:, HEAD_WIDTH:]], axis=1))
     keyval_other = partner(keyval_low, "fsdp", 0)
@@ -237,7 +351,7 @@
     )
     keys_all = keyval_all[:, :HEAD_WIDTH]
     values_all = keyval_all[:, HEAD_WIDTH:]
-    query_lin = matrix_multiply(normed_span, query_eff)
+    query_lin = matrix_multiply(normed_attn_wide, query_wide)
     local_heads = query_lin.shape[1] // HEAD_WIDTH
     query_rot = (
         rotate(query_lin.reshape(span_rows, local_heads, HEAD_WIDTH), span_positions, 1.0) * scaling
@@ -272,13 +386,30 @@
         .transpose(1, 0, 2)
         .reshape(span_rows, local_heads * HEAD_WIDTH)
     )
-    attn_result = scattered("tp", low(matrix_multiply(mixed_heads, out_eff)))
+    mixed_out = times_transposed(mixed_heads, out_wide)
+    mixed_delta = low(mixed_out[:, model_width:])
+    attn_result = scattered(
+        "tp",
+        low(mixed_out[:, :model_width] + matrix_multiply(mixed_delta, output_delta_product)),
+    )
     hidden = inputs + attn_result.astype(jnp.float32)
-    normed_mlp = joined("tp", low(normalize(hidden, gain_mlp)))
-
-    grad_activation = times_transposed(grad_span, down_eff)
-    gate_lin = matrix_multiply(normed_mlp, gate_eff)
-    up_lin = matrix_multiply(normed_mlp, up_eff)
+    normed_own = low(normalize(hidden, gain_mlp))
+    normed_wide = both_cores(
+        joined(
+            "tp",
+            jnp.concatenate(
+                [
+                    chip_relative(normed_own, 1),
+                    low(matrix_multiply(normed_own, delta_relative)),
+                ],
+                axis=1,
+            ),
+        )
+    )
+
+    grad_activation = matrix_multiply(grad_wide, down_wide)
+    gate_lin = matrix_multiply(normed_wide, gate_wide)
+    up_lin = matrix_multiply(normed_wide, up_wide)
     activation, gelu_pull = jax.vjp(
         lambda gate_vals, up_vals: jax.nn.gelu(gate_vals, approximate=True) * up_vals,
         gate_lin,
@@ -287,33 +418,43 @@
     activation = low(activation)
     grad_gate, grad_up = gelu_pull(grad_activation)
     grad_gate, grad_up = low(grad_gate), low(grad_up)
+    grad_normed_wide = times_transposed(grad_gate, gate_wide) + times_transposed(grad_up, up_wide)
+    mlp_inner = low(grad_normed_wide[:, model_width:])
     grad_normed_mlp = scattered(
         "tp",
-        low(times_transposed(grad_gate, gate_eff) + times_transposed(grad_up, up_eff)),
-    ).astype(jnp.float32)
+        core_sum(
+            grad_normed_wide[:, :model_width]
+            + times_transposed(mlp_inner, delta_both)
+        ),
+    )
+    grad_normed_mlp = chip_relative(grad_normed_mlp, 1).astype(jnp.float32)
     _, mlp_norm_pull = jax.vjp(normalize, hidden, gain_mlp)
     grad_hidden_norm, mlp_gain_part = mlp_norm_pull(grad_normed_mlp)
     grad_hidden = cotangent.astype(jnp.float32) + grad_hidden_norm
     grad_hidden_span = joined("tp", low(grad_hidden))
-    mlp_result = scattered("tp", low(matrix_multiply(activation, down_eff)))
-    result = low(hidden + mlp_result.astype(jnp.float32))
-
-    normed_delta = low(matrix_multiply(normed_mlp, delta_feedforward))
-    normed_wide = blocked(normed_mlp, normed_delta, fsdp_size)
-    grad_delta = low(times_transposed(grad_span, down_delta_product))
-    grad_wide = blocked(grad_span, grad_delta, fsdp_size)
-    down_sum = scattered("fsdp", low(transposed_times(grad_wide, activation)))
-    gate_sum = scattered("fsdp", low(transposed_times(normed_wide, grad_gate)))
-    up_sum = scattered("fsdp", low(transposed_times(normed_wide, grad_up)))
-    mlp_inner = low(
-        times_transposed(grad_gate, gate_delta_product)
-        + times_transposed(grad_up, up_delta_product)
-    )
-    mlp_lora_in = low(transposed_times(normed_mlp, mlp_inner))
-    active_delta = low(times_transposed(activation, down_in_t))
-    down_lora_out = low(transposed_times(active_delta, grad_span))
-
-    grad_mixed = low(times_transposed(grad_hidden_span, out_eff))
+
+    down_sum = scattered_wide(second, low(transposed_times(grad_wide, activation)), shard_rows)
+    gate_sum = scattered_wide(second, low(transposed_times(normed_wide, grad_gate)), shard_rows)
+    up_sum = scattered_wide(second, low(transposed_times(normed_wide, grad_up)), shard_rows)
+    mlp_lora_in = low(transposed_times(normed_wide[:, :model_width], mlp_inner))
+    mlp_lora_in = chip_relative(chip_relative(mlp_lora_in, 0), 1)
+    active_wide = times_transposed(activation, down_wide)
+    active_delta = low(active_wide[:, model_width:])
+    down_lora_out = transposed_times(active_delta, grad_wide[:, :model_width])
+    down_lora_out = chip_relative(chip_relative(low(down_lora_out), 0), 1)
+    mlp_result = scattered(
+        "tp",
+        core_sum(
+            active_wide[:, :model_width]
+            + matrix_multiply(active_delta, down_delta_both)
+        ),
+    )
+    result = low(hidden + chip_relative(mlp_result, 1).astype(jnp.float32))
+
+    grad_hidden_wide = jnp.concatenate(
+        [grad_hidden_span, low(times_transposed(grad_hidden_span, output_delta_product))], axis=1
+    )
+    grad_mixed = low(matrix_multiply(grad_hidden_wide, out_wide))
     grad_blocks = (
         grad_mixed.reshape(span_rows, local_heads, HEAD_WIDTH)
         .transpose(1, 0, 2)
@@ -351,8 +492,12 @@
     keyval_part = mine + partner(theirs, "fsdp", 0)
     grad_keys = rotate(keyval_part[:, None, :HEAD_WIDTH], span_positions, -1.0)[:, 0, :]
     grad_keyval = low(jnp.concatenate([grad_keys, keyval_part[:, HEAD_WIDTH:]], axis=1))
-    grad_normed_part = times_transposed(grad_query_lin, query_eff) + times_transposed(
-        grad_keyval, keyval_eff
+    grad_normed_both = times_transposed(grad_query_lin, query_wide) + times_transposed(
+        grad_keyval, keyval_wide
+    )
+    attn_inner = low(grad_normed_both[:, model_width:])
+    grad_normed_part = grad_normed_both[:, :model_width] + times_transposed(
+        attn_inner, delta_attention
     )
     grad_normed_attn = scattered("tp", low(grad_normed_part)).astype(jnp.float32)
     unit_span = inputs_span * lax.rsqrt(
@@ -362,21 +507,11 @@
     _, attn_norm_pull = jax.vjp(normalize, inputs, gain_attn)
     tokens_grad = grad_hidden + attn_norm_pull(grad_normed_attn)[0]
 
-    mixed_delta = low(times_transposed(mixed_heads, out_down_t))
     out_lora_out = low(transposed_times(mixed_delta, grad_hidden_span))
-    hidden_delta = low(times_transposed(grad_hidden_span, output_delta_product))
-    out_grads = low(
-        transposed_times(blocked(grad_hidden_span, hidden_delta, parts), mixed_heads)
-    )
-    attn_delta = low(matrix_multiply(normed_span, delta_attention))
-    attn_inner = low(
-        times_transposed(grad_query_lin, query_delta_product)
-        + times_transposed(grad_keyval, key_value_delta_product)
-    )
+    out_grads = low(transposed_times(grad_hidden_wide, mixed_heads))
     attn_grads = low(
         transposed_times(
-            blocked(normed_span, attn_delta, parts),
-            jnp.concatenate([grad_query_lin, grad_keyval, attn_inner], axis=1),
+            normed_attn_wide, jnp.concatenate([grad_query_lin, grad_keyval, attn_inner], axis=1)
         )
     )
 
@@ -395,71 +530,84 @@
             [value[..., at : at + rows, :] for at in range(0, value.shape[-2], rows)], axis=-1
         )
 
+    def per_device_wide(value):
+        return jnp.concatenate(
+            [per_device(value[:model_width]), per_device(value[model_width:])], axis=1
+        )
+
     main = model_width // parts
     extra = rank // parts
-    wide = main + extra
-    gain_lines = jnp.stack(
-        [mlp_gain_part.reshape(parts, main), attn_gain_part.reshape(parts, main)], axis=1
-    )
-    gain_lines = low(jnp.pad(gain_lines, ((0, 0), (0, 6), (0, rank - main))))
-    head_cols = query_eff.shape[1]
-    split_rows = 2 * (head_cols // rank) * wide
-    first = jnp.concatenate(
+    gain_pad = ((0, 0), (0, 7), (0, rank - main))
+    early = jnp.concatenate(
         [
-            per_device(out_grads),
-            per_device(attn_grads),
+            per_device_wide(out_grads),
             per_device(mlp_lora_in),
             per_device(down_lora_out),
             per_device(out_lora_out),
-            gain_lines,
+            low(jnp.pad(mlp_gain_part.reshape(parts, 1, main), gain_pad)),
         ],
         axis=1,
     )
-    first_sum = scattered("fsdp", first)
-    split_part = first_sum[:, :split_rows]
-    second_sum = scattered("tp", first_sum[:, split_rows:])[0].astype(jnp.float32)
-    split_part = split_part.astype(jnp.float32)
-    out_part = from_device(split_part[:, : split_rows // 2], wide)
-    query_part = from_device(split_part[:, split_rows // 2 :], wide)
+    late = jnp.concatenate(
+        [
+            per_device_wide(attn_grads[:, :head_cols]),
+            per_device_wide(attn_grads[:, head_cols:-rank]),
+            per_device(attn_grads[:model_width, -rank:]),
+            low(jnp.pad(attn_gain_part.reshape(parts, 1, main), gain_pad)),
+        ],
+        axis=1,
+    )
+    early_sum = scattered("fsdp", early)
+    late_sum = scattered("fsdp", late)
+    head_blocks = head_cols // rank
+    keyval_blocks = keyval_wide.shape[1] // rank
+    model_blocks = model_width // rank
+    split_rows = head_blocks * (main + extra)
+    second_sum = scattered(
+        "tp", jnp.concatenate([early_sum[:, split_rows:], late_sum[:, split_rows:]], axis=1)
+    )[0].astype(jnp.float32)
+    out_split = early_sum[:, :split_rows].astype(jnp.float32)
+    query_split = late_sum[:, :split_rows].astype(jnp.float32)
     sizes = [
-        (keyval_eff.shape[1] // rank) * wide,
-        wide,
         main,
-        model_width // rank * extra,
-        model_width // rank * extra,
+        model_blocks * extra,
+        model_blocks * extra,
+        8,
+        keyval_blocks * main,
+        keyval_blocks * extra,
+        main,
         8,
     ]
     starts = [sum(sizes[:at]) for at in range(len(sizes))]
     pieces = [second_sum[at : at + size] for at, size in zip(starts, sizes)]
-    keyval_part = from_device(pieces[0], wide)
-
-    def rows_of(value, first_row, row_count):
-        return value[:, first_row : first_row + row_count].reshape(-1, value.shape[-1])
-
-    down_sum, gate_sum, up_sum = (
-        value.astype(jnp.float32) for value in (down_sum, gate_sum, up_sum)
-    )
+
+    def split_main(value):
+        return from_device(value[:, : head_blocks * main], main).reshape(-1, head_cols)
+
+    def split_extra(value):
+        return from_device(value[:, head_blocks * main :], extra).reshape(-1, head_cols)
+
     return (
         result,
         tokens_grad,
-        pieces[5][1, :main],
-        pieces[5][0, :main],
-        rows_of(query_part, 0, main),
-        keyval_part[:main],
-        rows_of(out_part, 0, main).T,
+        pieces[7][0, :main],
+        pieces[3][0, :main],
+        split_main(query_split),
+        from_device(pieces[4], main),
+        split_main(out_split).T,
         gate_sum[:shard_rows],
         up_sum[:shard_rows],
         down_sum[:shard_rows].T,
-        pieces[1][:main],
-        rows_of(query_part, main, extra),
-        keyval_part[main:],
-        rows_of(out_part, main, extra).T,
-        from_device(pieces[4], extra),
-        pieces[2],
+        pieces[6],
+        split_extra(query_split),
+        from_device(pieces[5], extra),
+        split_extra(out_split).T,
+        from_device(pieces[2], extra),
+        pieces[0],
         gate_sum[shard_rows:],
         up_sum[shard_rows:],
         down_sum[shard_rows:].T,
-        from_device(pieces[3], extra),
+        from_device(pieces[1], extra),
     )
 
 

time: 1540 us -> 1200 us (0.78)
  waiting for transfers between devices: 1090 us -> 532 us
  local copies, waits for them, and re-layouts: 117 us -> 247 us
  other arithmetic: 53.4 us -> 116 us
  starting transfers between devices: 1 us -> 43 us
  matrix products: 242 us -> 226 us
    reduce_scatter x9 -> x7, waiting for transfers between devices: 566 us -> 61.2 us  [scattered(): return lax.psum_scatter(value, axis_names, scatter_dimension=0, tiled=True)]
    ppermute x2 -> x42, waiting for transfers between devices: 0.01 us -> 352 us  [partner(): return lax.ppermute(value, axis, pairs)]
    all_gather x6 -> x3, waiting for transfers between devices: 370 us -> 58.3 us  [joined(): return lax.all_gather(value, axis_names, axis=axis, tiled=True)]
    unnamed x244 -> x463, local copies, waits for them, and re-layouts: 53 us -> 160 us
    all_gather x2 -> x1, waiting for transfers between devices: 105 us -> 0.02 us  [gather(): lax.all_gather(jnp.concatenate(self.pieces, axis=0), axis_names, axis=0)]
    ppermute x0 -> x3, waiting for transfers between devices: none -> 59.5 us  [tp_rows(): lax.ppermute(value, 'tp', [(at, (at + shift) % size) for at in range(size)])]
    all_gather x1, waiting for transfers between devices: 43.5 us -> 0.01 us  [shards(): lax.all_gather(jnp.concatenate([jnp.concatenate([query_shared_weight, out...]
    ppermute x2 -> x42, starting transfers between devices: 0.25 us -> 35.6 us  [partner(): return lax.ppermute(value, axis, pairs)]
  transfers between devices with their start and end apart: 20 -> 57, of which waited for: 17 -> 22; matrix products, arithmetic and copies ran while one was open for 15% -> 34% of each run, Pallas kernels for 0% -> 0%
where the time goes in v2:
time: 1200 us; the launch traced here: 1190 us
  waiting for transfers between devices  532 us (44%)
  local copies, waits for them, and re-layouts  247 us (21%)
  matrix products  226 us (19%)
  other arithmetic  116 us (10%)
  starting transfers between devices  43 us (4%)
  between operations  17.9 us (1%)
    ppermute x42, waiting for transfers between devices, partner(): return lax.ppermute(value, axis, pairs)  352 us
    unnamed x463, local copies, waits for them, and re-layouts  160 us
    dot_general x14, matrix products, matrix_multiply(): return jnp.dot(left_mat, right_mat, preferred_element_type=jnp.float32)  81 us
    dot_general x16, matrix products, times_transposed(): lax.dot_general(left_mat, right_mat, (((1,), (1,)), ((), ())), preferred_...  75.4 us
    dot_general x12, matrix products, transposed_times(): lax.dot_general(left_mat, right_mat, (((0,), (0,)), ((), ())), preferred_...  69.1 us
    reduce_scatter x7, waiting for transfers between devices, scattered(): return lax.psum_scatter(value, axis_names, scatter_dimension=0, tiled=True)  61.2 us
    ppermute x3, waiting for transfers between devices, tp_rows(): lax.ppermute(value, 'tp', [(at, (at + shift) % size) for at in range(size)])  59.5 us
    all_gather x3, waiting for transfers between devices, joined(): return lax.all_gather(value, axis_names, axis=axis, tiled=True)  58.3 us
  transfers between devices with their start and end apart: 57, of which 22 were waited for; matrix products, arithmetic and copies ran while one was open for 34% of the time, Pallas kernels for 0%

profile of v2, /device:TPU:0, one launch (start us, length us, event | category | flops | bytes accessed | tf_op | source)
XLA Modules:
  0.0 1189.1 jit_solution(13137132722113907558)
XLA Ops:
  37.6 56.0 %collective-permute-done.1 = bf16[128,2048]{1,0:T(8,128)(2,1)} collective-permute-done((bf16[128,2048]{1,0:T(8,128)(2,1)S(1)}, bf16[128,2048]{1,0:T(8,128)(2,1)}, u32[]{:S(2)}, u32[]{:S(2)}) %collective-permute-start.1) | collective-permute-done | bytes 524320 | tf_op jit(solution)/shard_map/ppermute | solution.py:186
  131.2 46.3 %collective-permute-done.6 = bf16[576,2048]{1,0:T(8,128)(2,1)} collective-permute-done((bf16[576,2048]{1,0:T(8,128)(2,1)S(1)}, bf16[576,2048]{1,0:T(8,128)(2,1)}, u32[]{:S(2)}, u32[]{:S(2)}) %collective-permute-start.6) | collective-permute-done | bytes 2359328 | tf_op jit(solution)/shard_map/ppermute | solution.py:17
  182.3 63.6 %collective-permute-done.11 = bf16[576,2048]{1,0:T(8,128)(2,1)} collective-permute-done((bf16[576,2048]{1,0:T(8,128)(2,1)}, bf16[576,2048]{1,0:T(8,128)(2,1)}, u32[]{:S(2)}, u32[]{:S(2)}) %collective-permute-start.11) | collective-permute-done | bytes 2359328 | tf_op jit(solution)/shard_map/ppermute | solution.py:17
  269.7 26.7 %collective-permute-done.16 = bf16[576,2048]{1,0:T(8,128)(2,1)} collective-permute-done((bf16[576,2048]{1,0:T(8,128)(2,1)}, bf16[576,2048]{1,0:T(8,128)(2,1)}, u32[]{:S(2)}, u32[]{:S(2)}) %collective-permute-start.16) | collective-permute-done | bytes 2359328 | tf_op jit(solution)/shard_map/ppermute | solution.py:17
  307.4 12.0 %collective-permute-done.8 = bf16[288,2048]{1,0:T(8,128)(2,1)S(1)} collective-permute-done((bf16[288,2048]{1,0:T(8,128)(2,1)S(1)}, bf16[288,2048]{1,0:T(8,128)(2,1)S(1)}, u32[]{:S(2)}, u32[]{:S(2)}) %collective-permute-start.8) | collective-permute-done | bytes 1179680 | tf_op jit(solution)/shard_map/ppermute | solution.py:17
  323.5 21.1 %collective-permute-done.13 = bf16[288,2048]{1,0:T(8,128)(2,1)S(1)} collective-permute-done((bf16[288,2048]{1,0:T(8,128)(2,1)S(1)}, bf16[288,2048]{1,0:T(8,128)(2,1)S(1)}, u32[]{:S(2)}, u32[]{:S(2)}) %collective-permute-start.13) | collective-permute-done | bytes 1179680 | tf_op jit(solution)/shard_map/ppermute | solution.py:17
  352.0 15.0 %collective-permute-done.18 = bf16[288,2048]{1,0:T(8,128)(2,1)S(1)} collective-permute-done((bf16[288,2048]{1,0:T(8,128)(2,1)S(1)}, bf16[288,2048]{1,0:T(8,128)(2,1)S(1)}, u32[]{:S(2)}, u32[]{:S(2)}) %collective-permute-start.18) | collective-permute-done | bytes 1179680 | tf_op jit(solution)/shard_map/ppermute | solution.py:17
  422.3 19.6 %while.36 = (s32[]{:T(128)}, bf16[2,512,256]{1,2,0:T(8,128)(2,1)}, f32[2,512]{1,0:T(2,128)}, s32[]{:T(128)}, s32[]{:T(128)}, /*index=5*/s32[]{:T(128)}, s32[2]{0...) while((s32[]{:T(128)}, bf16[2,512,256]{1,2,0:T(8,128)(2,1)}, ...), condition=%wide.region_4.5_spmd.clone.clone.clone, body=%wide.region_1.4_spmd.clone.clone.sunk.clone | while | flops 542118912 | bytes 8154803 | solution.py:383
  463.6 32.2 %reduce-scatter.8.cloned.1.call-done = bf16[128,2048]{1,0:T(8,128)(2,1)} async-done(((bf16[512,2048]{1,0:T(8,128)(2,1)}), bf16[128,2048]{1,0:T(8,128)(2,1)}) %reduce-scatter.8.cloned.1.call-update) | async-done | bytes 524304 | tf_op jit(solution)/shard_map/reduce_scatter | solution.py:67
  518.9 32.7 %all-gather.8.cloned.1.call-done = bf16[512,2304]{1,0:T(8,128)(2,1)} async-done(((bf16[128,2304]{1,0:T(8,128)(2,1)}), bf16[512,2304]{1,0:T(8,128)(2,1)}) %all-gather.8.cloned.1.call-update) | async-done | bytes 2359312 | tf_op jit(solution)/shard_map/all_gather | solution.py:63
  551.6 16.1 %fusion.50 = f32[1024,2048]{1,0:T(8,128)} fusion(bf16[2304,2048]{1,0:T(8,128)(2,1)} %constant_dynamic-update-slice_fusion.64, bf16[512,2304]{1,0:T(8,128)(2,1)} %collective-permute-done.21, bf16[512,2304]{1,0:T(8,128)(2,1)} %constant_dynamic-update-slice_fusion.80), kind=kOutput, calls=%fused_computation.104 | convolution fusion | flops 9673113600 | bytes 22544384 | tf_op jit(solution)/shard_map/dot_general | solution.py:21
  568.0 16.1 %fusion.171 = f32[1024,2048]{1,0:T(8,128)} fusion(bf16[1024,2304]{1,0:T(8,128)(2,1)S(1)} %constant_dynamic-update-slice_fusion.42, bf16[2304,2048]{1,0:T(8,128)(2,1)} %constant_dynamic-update-slice_fusion.56), kind=kOutput, calls=%fused_computation.650 | convolution fusion | flops 9663676416 | bytes 22544384 | tf_op jit(solution)/shard_map/dot_general | solution.py:21
  584.2 23.9 %fusion.35 = (bf16[1024,2048]{1,0:T(8,128)(2,1)}, bf16[1024,2048]{1,0:T(8,128)(2,1)}, bf16[1024,2048]{1,0:T(8,128)(2,1)}) fusion(f32[1024,2048]{1,0:T(8,128)} %fusion.50, f32[1024,2048]{1,0:T(8,128)} %fusion.171, bf16[1024,2304]{1,0:T(8,128)(2,1)S(1)} %constant_dynamic-update-slice_fusion.42, bf16[2304,2048]{1,0:T(8,128)(2,1)} %constant_dynamic-update-slice_fusion.46), kind=kOutput, calls=%fused_computation.60 | convolution fusion | flops 9718202368 | bytes 43515904 | tf_op jit(solution)/shard_map/dot_general | solution.py:21
  608.1 13.4 %convolution_convert_fusion = bf16[2304,2048]{1,0:T(8,128)(2,1)S(1)} fusion(bf16[1024,2048]{1,0:T(8,128)(2,1)} %get-tuple-element.607, bf16[512,2304]{1,0:T(8,128)(2,1)} %collective-permute-done.21, bf16[512,2304]{1,0:T(8,128)(2,1)} %constant_dynamic-update-slice_fusion.80), kind=kOutput, calls=%fused_computation.50 | convolution fusion | flops 9677832192 | bytes 18350080 | tf_op jit(solution)/shard_map/dot_general | solution.py:31
  625.5 13.9 %fusion.173 = f32[1024,2304]{1,0:T(8,128)} fusion(bf16[1024,2048]{1,0:T(8,128)(2,1)S(1)} %copy-done.167, bf16[2304,2048]{1,0:T(8,128)(2,1)} %constant_dynamic-update-slice_fusion.56), kind=kOutput, calls=%fused_computation.652 | convolution fusion | flops 9663676416 | bytes 23068672 | tf_op jit(solution)/shard_map/dot_general | solution.py:25
  639.4 18.4 %convolution_add_fusion.2 = f32[1024,2304]{1,0:T(8,128)} fusion(f32[1024,2304]{1,0:T(8,128)} %fusion.173, bf16[1024,2048]{1,0:T(8,128)(2,1)} %get-tuple-element.605, bf16[2304,2048]{1,0:T(8,128)(2,1)} %constant_dynamic-update-slice_fusion.46), kind=kOutput, calls=%fused_computation.66 | convolution fusion | flops 9666035712 | bytes 32505856 | tf_op jit(solution)/shard_map/dot_general | solution.py:25
  673.5 13.5 %fusion.172 = f32[1024,2304]{1,0:T(8,128)S(1)} fusion(bf16[1024,2048]{1,0:T(8,128)(2,1)} %get-tuple-element.607, bf16[2304,2048]{1,0:T(8,128)(2,1)} %constant_dynamic-update-slice_fusion.64), kind=kOutput, calls=%fused_computation.651 | convolution fusion | flops 9663676416 | bytes 23068672 | tf_op jit(solution)/shard_map/dot_general | solution.py:25
  687.1 6.7 fusion.51
  704.0 5.8 fusion.54
  716.1 12.3 %convolution_convert_fusion.1 = bf16[2304,2048]{1,0:T(8,128)(2,1)} fusion(bf16[1024,2304]{1,0:T(8,128)(2,1)S(1)} %bitcast.455, bf16[1024,2048]{1,0:T(8,128)(2,1)S(1)} %copy-done.168), kind=kOutput, calls=%fused_computation.51 | convolution fusion | flops 9668395008 | bytes 18350080 | tf_op jit(solution)/shard_map/dot_general | solution.py:31
  728.4 10.9 reduce-scatter.12.cloned.1.call-done
  749.2 6.2 fusion.154
  763.0 25.6 %all-gather.12.cloned.1.call-done = bf16[512,2048]{1,0:T(8,128)(2,1)} async-done(((bf16[128,2048]{1,0:T(8,128)(2,1)}), bf16[512,2048]{1,0:T(8,128)(2,1)}) %all-gather.12.cloned.1.call-update) | async-done | bytes 2097168 | tf_op jit(solution)/shard_map/all_gather | solution.py:63
  795.3 33.1 %while.37 = (s32[]{:T(128)}, f32[1024,256]{1,0:T(8,128)}, f32[1024,256]{1,0:T(8,128)}, f32[2,512,256]{1,2,0:T(8,128)}, s32[]{:T(128)}, /*index=5*/s32[]{:T(128)}...) while((s32[]{:T(128)}, f32[1024,256]{1,0:T(8,128)}, ...), condition=%wide.region_12.13_spmd.clone.clone.clone, body=%wide.region_10.12_spmd.clone.clone.sunk.clone | while | flops 1348998144 | bytes 33572280 | solution.py:478
  872.5 11.9 %convolution_convert_fusion.2 = bf16[2304,2048]{1,0:T(8,128)(2,1)S(1)} fusion(bf16[1024,2304]{1,0:T(8,128)(2,1)} %copy-done.74, bf16[1024,2048]{1,0:T(8,128)(2,1)S(1)} %copy-done.169), kind=kOutput, calls=%fused_computation.52 | convolution fusion | flops 9668395008 | bytes 18350080 | tf_op jit(solution)/shard_map/dot_general | solution.py:31
  931.3 38.9 %collective-permute-done.32 = bf16[576,1024]{1,0:T(8,128)(2,1)} collective-permute-done((bf16[576,1024]{1,0:T(8,128)(2,1)}, bf16[576,1024]{1,0:T(8,128)(2,1)}, u32[]{:S(2)}, u32[]{:S(2)}) %collective-permute-start.32) | collective-permute-done | bytes 1179680 | tf_op jit(solution)/shard_map/ppermute | solution.py:17
  977.7 19.9 %collective-permute-done.25 = bf16[576,1024]{1,0:T(8,128)(2,1)} collective-permute-done((bf16[576,1024]{1,0:T(8,128)(2,1)}, bf16[576,1024]{1,0:T(8,128)(2,1)}, u32[]{:S(2)}, u32[]{:S(2)}) %collective-permute-start.25) | collective-permute-done | bytes 1179680 | tf_op jit(solution)/shard_map/ppermute | solution.py:17
  1003.3 35.2 %collective-permute-done.43 = bf16[576,1024]{1,0:T(8,128)(2,1)S(1)} collective-permute-done((bf16[576,1024]{1,0:T(8,128)(2,1)}, bf16[576,1024]{1,0:T(8,128)(2,1)S(1)}, u32[]{:S(2)}, u32[]{:S(2)}) %collective-permute-start.43) | collective-permute-done | bytes 1179680 | tf_op jit(solution)/shard_map/ppermute | solution.py:17
  1040.6 31.1 %collective-permute-done.36 = bf16[576,1024]{1,0:T(8,128)(2,1)S(1)} collective-permute-done((bf16[576,1024]{1,0:T(8,128)(2,1)}, bf16[576,1024]{1,0:T(8,128)(2,1)S(1)}, u32[]{:S(2)}, u32[]{:S(2)}) %collective-permute-start.36) | collective-permute-done | bytes 1179680 | tf_op jit(solution)/shard_map/ppermute | solution.py:17
  1081.4 15.6 %collective-permute-done.24 = bf16[576,1024]{1,0:T(8,128)(2,1)S(1)} collective-permute-done((bf16[576,1024]{1,0:T(8,128)(2,1)S(1)}, bf16[576,1024]{1,0:T(8,128)(2,1)S(1)}, u32[]{:S(2)}, u32[]{:S(2)}) %collective-permute-start.24) | collective-permute-done | bytes 1179680 | tf_op jit(solution)/shard_map/ppermute | solution.py:17
  1097.0 23.7 %collective-permute-done.29 = bf16[576,1024]{1,0:T(8,128)(2,1)S(1)} collective-permute-done((bf16[576,1024]{1,0:T(8,128)(2,1)S(1)}, bf16[576,1024]{1,0:T(8,128)(2,1)S(1)}, u32[]{:S(2)}, u32[]{:S(2)}) %collective-permute-start.29) | collective-permute-done | bytes 1179680 | tf_op jit(solution)/shard_map/ppermute | solution.py:17
  1160.4 18.1 %reduce-scatter.20.cloned.1.call-done = bf16[1,416,256]{2,1,0:T(8,128)(2,1)} async-done(((bf16[4,416,256]{2,1,0:T(8,128)(2,1)}), bf16[1,416,256]{2,1,0:T(8,128)(2,1)}) %reduce-scatter.20.cloned.1.call-update) | async-done | bytes 213008 | tf_op jit(solution)/shard_map/reduce_scatter | solution.py:67
  (835 shorter events, 480.2 us)
Async XLA Ops:
  7.2 119.5 %all-gather.10.cloned.1.call-start = ((), (), s32[]{:S(2)}) async-start(), calls=%async_computation.10 | async-start | bytes 2621440 | tf_op jit(solution)/shard_map/all_gather | solution.py:63
  7.9 372.0 %all-gather.16.cloned.1.call-start = ((), (), s32[]{:S(2)}) async-start(), calls=%async_computation.18 | async-start | bytes 5308416 | tf_op jit(solution)/shard_map/all_gather | solution.py:301
  11.0 374.7 %all-gather.14.cloned.1.call-start = ((), (), s32[]{:S(2)}) async-start(), calls=%async_computation.17 | async-start | bytes 6893568 | tf_op jit(solution)/shard_map/all_gather | solution.py:89
  16.2 77.4 %collective-permute-start.1 = (bf16[128,2048]{1,0:T(8,128)(2,1)S(1)}, bf16[128,2048]{1,0:T(8,128)(2,1)}, u32[]{:S(2)}, u32[]{:S(2)}) collective-permute-start(bf16[128,2048]{1,0:T(8,128)(2,1)S(1)} %copy-done.5), channel_id=1, source_target_pairs={{0,2},{1,3},{2,0},{3,1},{4,6},{5,7},{6,4},{7,5},{8,10},{9,11},{10,... | collective-permute-start | bytes 1572872 | tf_op jit(solution)/shard_map/ppermute | solution.py:186
  16.2 78.4 %collective-permute-start.2 = (bf16[128,2048]{1,0:T(8,128)(2,1)S(1)}, bf16[128,2048]{1,0:T(8,128)(2,1)}, u32[]{:S(2)}, u32[]{:S(2)}) collective-permute-start(bf16[128,2048]{1,0:T(8,128)(2,1)S(1)} %copy-done.5), channel_id=1, source_target_pairs={{0,1},{1,2},{2,3},{3,0},{4,5},{5,6},{6,7},{7,4},{8,9},{9,10},{10,1... | collective-permute-start | bytes 1572872 | tf_op jit(solution)/shard_map/ppermute | solution.py:186
  19.0 80.7 %collective-permute-start.5 = (bf16[288,2048]{1,0:T(8,128)(2,1)}, bf16[288,2048]{1,0:T(8,128)(2,1)}, u32[]{:S(2)}, u32[]{:S(2)}) collective-permute-start(bf16[288,2048]{1,0:T(8,128)(2,1)} %get-tuple-element.701), channel_id=1, source_target_pairs={{0,4},{4,0},{8,12},{12,8},{16,20},{20,16},{24,28},{28,24},{1,5},{5... | collective-permute-start | bytes 3538952 | tf_op jit(solution)/shard_map/ppermute | solution.py:17
  21.8 84.8 %collective-permute-start.10 = (bf16[288,2048]{1,0:T(8,128)(2,1)}, bf16[288,2048]{1,0:T(8,128)(2,1)}, u32[]{:S(2)}, u32[]{:S(2)}) collective-permute-start(bf16[288,2048]{1,0:T(8,128)(2,1)} %get-tuple-element.703), channel_id=1, source_target_pairs={{0,4},{4,0},{8,12},{12,8},{16,20},{20,16},{24,28},{28,24},{1,5},{5... | collective-permute-start | bytes 3538952 | tf_op jit(solution)/shard_map/ppermute | solution.py:17
  22.9 473.0 %reduce-scatter.8.cloned.1.call-start = ((), (), s32[]{:S(2)}) async-start(), calls=%async_computation.7 | async-start | bytes 2621440 | tf_op jit(solution)/shard_map/reduce_scatter | solution.py:67
  36.5 77.9 %collective-permute-start.15 = (bf16[288,2048]{1,0:T(8,128)(2,1)}, bf16[288,2048]{1,0:T(8,128)(2,1)S(1)}, u32[]{:S(2)}, u32[]{:S(2)}) collective-permute-start(bf16[288,2048]{1,0:T(8,128)(2,1)} %get-tuple-element.699), channel_id=1, source_target_pairs={{0,4},{4,0},{8,12},{12,8},{16,20},{20,16},{24,28},{28,24},{1,5},{5... | collective-permute-start | bytes 3538952 | tf_op jit(solution)/shard_map/ppermute | solution.py:17
  110.0 135.9 %collective-permute-start.11 = (bf16[576,2048]{1,0:T(8,128)(2,1)}, bf16[576,2048]{1,0:T(8,128)(2,1)}, u32[]{:S(2)}, u32[]{:S(2)}) collective-permute-start(bf16[576,2048]{1,0:T(8,128)(2,1)} %maximum_select_fusion.4), channel_id=1, source_target_pairs={{0,8},{4,12},{8,0},{12,4},{16,24},{20,28},{24,16},{28,20},{1,9},{5... | collective-permute-start | bytes 7077896 | tf_op jit(solution)/shard_map/ppermute | solution.py:17
  110.5 142.2 %collective-permute-start.12 = (bf16[576,2048]{1,0:T(8,128)(2,1)}, bf16[576,2048]{1,0:T(8,128)(2,1)}, u32[]{:S(2)}, u32[]{:S(2)}) collective-permute-start(bf16[576,2048]{1,0:T(8,128)(2,1)} %maximum_select_fusion.4), channel_id=1, source_target_pairs={{0,16},{4,20},{8,24},{12,28},{16,0},{20,4},{24,8},{28,12},{1,17},{... | collective-permute-start | bytes 7077896 | tf_op jit(solution)/shard_map/ppermute | solution.py:17
  119.2 177.3 %collective-permute-start.16 = (bf16[576,2048]{1,0:T(8,128)(2,1)}, bf16[576,2048]{1,0:T(8,128)(2,1)}, u32[]{:S(2)}, u32[]{:S(2)}) collective-permute-start(bf16[576,2048]{1,0:T(8,128)(2,1)} %maximum_select_fusion.5), channel_id=1, source_target_pairs={{0,8},{4,12},{8,0},{12,4},{16,24},{20,28},{24,16},{28,20},{1,9},{5... | collective-permute-start | bytes 7077896 | tf_op jit(solution)/shard_map/ppermute | solution.py:17
  177.4 125.8 %collective-permute-start.17 = (bf16[576,2048]{1,0:T(8,128)(2,1)}, bf16[576,2048]{1,0:T(8,128)(2,1)S(1)}, u32[]{:S(2)}, u32[]{:S(2)}) collective-permute-start(bf16[576,2048]{1,0:T(8,128)(2,1)} %maximum_select_fusion.5), channel_id=1, source_target_pairs={{0,16},{4,20},{8,24},{12,28},{16,0},{20,4},{24,8},{28,12},{1,17},{... | collective-permute-start | bytes 7077896 | tf_op jit(solution)/shard_map/ppermute | solution.py:17
  180.3 139.1 %collective-permute-start.8 = (bf16[288,2048]{1,0:T(8,128)(2,1)S(1)}, bf16[288,2048]{1,0:T(8,128)(2,1)S(1)}, u32[]{:S(2)}, u32[]{:S(2)}) collective-permute-start(bf16[288,2048]{1,0:T(8,128)(2,1)S(1)} %slice.1565), channel_id=1, source_target_pairs={{0,16},{4,20},{8,24},{12,28},{16,0},{20,4},{24,8},{28,12},{1,17},{... | collective-permute-start | bytes 3538952 | tf_op jit(solution)/shard_map/ppermute | solution.py:17
  252.7 91.9 %collective-permute-start.13 = (bf16[288,2048]{1,0:T(8,128)(2,1)S(1)}, bf16[288,2048]{1,0:T(8,128)(2,1)S(1)}, u32[]{:S(2)}, u32[]{:S(2)}) collective-permute-start(bf16[288,2048]{1,0:T(8,128)(2,1)S(1)} %slice.1585), channel_id=1, source_target_pairs={{0,16},{4,20},{8,24},{12,28},{16,0},{20,4},{24,8},{28,12},{1,17},{... | collective-permute-start | bytes 3538952 | tf_op jit(solution)/shard_map/ppermute | solution.py:17
  449.7 101.9 %all-gather.8.cloned.1.call-start = ((), (), s32[]{:S(2)}) async-start(), calls=%async_computation.8 | async-start | bytes 2949120 | tf_op jit(solution)/shard_map/all_gather | solution.py:63
  502.3 237.0 %reduce-scatter.12.cloned.1.call-start = ((), (), s32[]{:S(2)}) async-start(), calls=%async_computation.11 | async-start | bytes 2621440 | tf_op jit(solution)/shard_map/reduce_scatter | solution.py:67
  666.4 228.8 %collective-permute-start.42 = (bf16[576,1024]{1,0:T(8,128)(2,1)}, bf16[576,1024]{1,0:T(8,128)(2,1)}, u32[]{:S(2)}, u32[]{:S(2)}) collective-permute-start(bf16[576,1024]{1,0:T(8,128)(2,1)} %get-tuple-element.688), channel_id=1, source_target_pairs={{0,16},{4,20},{8,24},{12,28},{16,0},{20,4},{24,8},{28,12},{1,17},{... | collective-permute-start | bytes 3538952 | tf_op jit(solution)/shard_map/ppermute | solution.py:17
  669.3 251.5 %collective-permute-start.38 = (bf16[576,1024]{1,0:T(8,128)(2,1)}, bf16[576,1024]{1,0:T(8,128)(2,1)}, u32[]{:S(2)}, u32[]{:S(2)}) collective-permute-start(bf16[576,1024]{1,0:T(8,128)(2,1)} %slice.1788), channel_id=1, source_target_pairs={{0,8},{4,12},{8,0},{12,4},{16,24},{20,28},{24,16},{28,20},{1,9},{5... | collective-permute-start | bytes 3538952 | tf_op jit(solution)/shard_map/ppermute | solution.py:17
  670.7 228.8 %collective-permute-start.39 = (bf16[576,1024]{1,0:T(8,128)(2,1)}, bf16[576,1024]{1,0:T(8,128)(2,1)}, u32[]{:S(2)}, u32[]{:S(2)}) collective-permute-start(bf16[576,1024]{1,0:T(8,128)(2,1)} %get-tuple-element.687), channel_id=1, source_target_pairs={{0,8},{4,12},{8,0},{12,4},{16,24},{20,28},{24,16},{28,20},{1,9},{5... | collective-permute-start | bytes 3538952 | tf_op jit(solution)/shard_map/ppermute | solution.py:17
  672.8 253.4 %collective-permute-start.41 = (bf16[576,1024]{1,0:T(8,128)(2,1)}, bf16[576,1024]{1,0:T(8,128)(2,1)}, u32[]{:S(2)}, u32[]{:S(2)}) collective-permute-start(bf16[576,1024]{1,0:T(8,128)(2,1)} %slice.1800), channel_id=1, source_target_pairs={{0,16},{4,20},{8,24},{12,28},{16,0},{20,4},{24,8},{28,12},{1,17},{... | collective-permute-start | bytes 3538952 | tf_op jit(solution)/shard_map/ppermute | solution.py:17
  696.9 91.6 %all-gather.12.cloned.1.call-start = ((), (), s32[]{:S(2)}) async-start(), calls=%async_computation.12 | async-start | bytes 2621440 | tf_op jit(solution)/shard_map/all_gather | solution.py:63
  743.6 403.3 %reduce-scatter.10.cloned.1.call-start = ((), (), s32[]{:S(2)}) async-start(), calls=%async_computation.9 | async-start | bytes 2621440 | tf_op jit(solution)/shard_map/reduce_scatter | solution.py:67
  762.8 385.3 %reduce-scatter.14.cloned.1.call-start = ((), (), s32[]{:S(2)}) async-start(), calls=%async_computation.13 | async-start | bytes 2621440 | tf_op jit(solution)/shard_map/reduce_scatter | solution.py:67
  850.3 302.2 %reduce-scatter.16.cloned.1.call-start = ((), (), s32[]{:S(2)}) async-start(), calls=%async_computation.14 | async-start | bytes 6340608 | tf_op jit(solution)/shard_map/reduce_scatter | solution.py:67
  867.9 285.7 %reduce-scatter.18.cloned.1.call-start = ((), (), s32[]{:S(2)}) async-start(), calls=%async_computation.15 | async-start | bytes 6635520 | tf_op jit(solution)/shard_map/reduce_scatter | solution.py:67
  926.0 252.5 %reduce-scatter.20.cloned.1.call-start = ((), (), s32[]{:S(2)}) async-start(), calls=%async_computation.16 | async-start | bytes 1064960 | tf_op jit(solution)/shard_map/reduce_scatter | solution.py:67
  928.9 109.7 %collective-permute-start.43 = (bf16[576,1024]{1,0:T(8,128)(2,1)}, bf16[576,1024]{1,0:T(8,128)(2,1)S(1)}, u32[]{:S(2)}, u32[]{:S(2)}) collective-permute-start(bf16[576,1024]{1,0:T(8,128)(2,1)} %add_convert_fusion), channel_id=1, source_target_pairs={{0,8},{4,12},{8,0},{12,4},{16,24},{20,28},{24,16},{28,20},{1,9},{5... | collective-permute-start | bytes 3538952 | tf_op jit(solution)/shard_map/ppermute | solution.py:17
  970.3 101.4 %collective-permute-start.36 = (bf16[576,1024]{1,0:T(8,128)(2,1)}, bf16[576,1024]{1,0:T(8,128)(2,1)S(1)}, u32[]{:S(2)}, u32[]{:S(2)}) collective-permute-start(bf16[576,1024]{1,0:T(8,128)(2,1)} %add_convert_fusion.2), channel_id=1, source_target_pairs={{0,8},{4,12},{8,0},{12,4},{16,24},{20,28},{24,16},{28,20},{1,9},{5... | collective-permute-start | bytes 3538952 | tf_op jit(solution)/shard_map/ppermute | solution.py:17
  997.6 78.3 %collective-permute-start.33 = (bf16[576,1024]{1,0:T(8,128)(2,1)S(1)}, bf16[576,1024]{1,0:T(8,128)(2,1)S(1)}, u32[]{:S(2)}, u32[]{:S(2)}) collective-permute-start(bf16[576,1024]{1,0:T(8,128)(2,1)S(1)} %add_convert_fusion.3), channel_id=1, source_target_pairs={{0,16},{4,20},{8,24},{12,28},{16,0},{20,4},{24,8},{28,12},{1,17},{... | collective-permute-start | bytes 3538952 | tf_op jit(solution)/shard_map/ppermute | solution.py:17
  1001.8 95.2 %collective-permute-start.24 = (bf16[576,1024]{1,0:T(8,128)(2,1)S(1)}, bf16[576,1024]{1,0:T(8,128)(2,1)S(1)}, u32[]{:S(2)}, u32[]{:S(2)}) collective-permute-start(bf16[576,1024]{1,0:T(8,128)(2,1)S(1)} %slice.1734), channel_id=1, source_target_pairs={{0,8},{4,12},{8,0},{12,4},{16,24},{20,28},{24,16},{28,20},{1,9},{5... | collective-permute-start | bytes 3538952 | tf_op jit(solution)/shard_map/ppermute | solution.py:17
  1039.1 81.6 %collective-permute-start.29 = (bf16[576,1024]{1,0:T(8,128)(2,1)S(1)}, bf16[576,1024]{1,0:T(8,128)(2,1)S(1)}, u32[]{:S(2)}, u32[]{:S(2)}) collective-permute-start(bf16[576,1024]{1,0:T(8,128)(2,1)S(1)} %add_convert_fusion.4), channel_id=1, source_target_pairs={{0,8},{4,12},{8,0},{12,4},{16,24},{20,28},{24,16},{28,20},{1,9},{5... | collective-permute-start | bytes 3538952 | tf_op jit(solution)/shard_map/ppermute | solution.py:17
  (204 other events, 3770.6 us)
Sparse Core Ops, SparseCore 0:
  9.6 85.3 all-gather.9
  97.5 56.1 all-gather.15
  157.0 88.9 all-gather.13
  449.8 45.9 reduce-scatter.7
  502.4 49.1 all-gather.7
  697.0 42.2 reduce-scatter.11
  743.7 44.8 all-gather.11
  790.8 42.4 reduce-scatter.9
  850.4 41.5 reduce-scatter.13
  895.3 80.4 reduce-scatter.15
  979.3 83.5 reduce-scatter.17
  1155.8 22.5 reduce-scatter.19

commit v3 on v2

--- a/solution.py
+++ b/solution.py
@@ -86,7 +86,8 @@
         self.pieces.append(to_lanes(value, self.width))
 
     def gather(self, axis_names):
-        whole = lax.all_gather(jnp.concatenate(self.pieces, axis=0), axis_names, axis=0)
+        stacked = jnp.concatenate(self.pieces, axis=0)
+        whole = lax.all_gather(stacked, axis_names, axis=0)
         results, at = [], 0
         for rows, columns in self.shapes:
             parts = []
@@ -256,7 +257,6 @@
     block_rows = min(BLOCK_ROWS, span_rows)
     block_count = span_rows // block_rows
     placed = lax.axis_index("fsdp")
-    tp_at = lax.axis_index("tp")
     second_half = placed % 2
     picture_at = lax.dynamic_slice_in_dim(picture_begin_index, placed // 2, 1)[0]
     offset_rows = second_half * span_rows
@@ -294,30 +294,32 @@
     gains = gains.reshape(parts, 8, rank)[:, :2, : gain_rows.shape[1]].astype(jnp.float32)
     gain_attn = gains[:, 0].reshape(-1)
     gain_mlp = gains[:, 1].reshape(-1)
-    keyval_wide = jnp.concatenate([key_value_complete, key_value_delta_product], axis=0)
 
     head_cols = query_shared_weight.shape[1]
     shard_rows = query_shared_weight.shape[0]
-    heads_stack = lax.all_gather(
-        jnp.concatenate(
-            [
-                jnp.concatenate([query_shared_weight, output_shared_weight.T], axis=1),
-                jnp.concatenate([query_delta_output, output_delta_input.T], axis=1),
-            ],
-            axis=0,
-        ),
-        "fsdp",
-        axis=0,
-    )
-    heads_wide = jnp.concatenate(
+    heads_own = jnp.concatenate(
         [
-            heads_stack[:, :shard_rows].reshape(-1, 2 * head_cols),
-            heads_stack[:, shard_rows:].reshape(-1, 2 * head_cols),
+            jnp.concatenate([query_shared_weight, output_shared_weight.T], axis=1),
+            jnp.concatenate([query_delta_output, output_delta_input.T], axis=1),
         ],
         axis=0,
     )
-    query_wide = heads_wide[:, :head_cols]
-    out_wide = heads_wide[:, head_cols:]
+    heads_stack = lax.all_gather(heads_own, "fsdp", axis=0)
+    heads_main = heads_stack[:, :shard_rows].reshape(-1, 2 * head_cols)
+    heads_delta = heads_stack[:, shard_rows:].reshape(-1, 2 * head_cols)
+    query_delta_product, out_delta_in = heads_delta[:, :head_cols], heads_delta[:, head_cols:]
+    query_eff = low(
+        heads_main[:, :head_cols].astype(jnp.float32)
+        + matrix_multiply(delta_attention, query_delta_product)
+    )
+    out_eff = low(
+        heads_main[:, head_cols:].astype(jnp.float32)
+        + transposed_times(output_delta_product, out_delta_in)
+    )
+    keyval_eff = low(
+        key_value_complete.astype(jnp.float32)
+        + matrix_multiply(delta_attention, key_value_delta_product)
+    )
 
     grad_span = joined("tp", cotangent)
     down_delta_relative = chip_relative(down_delta_product, 0)
@@ -337,10 +339,7 @@
     inputs = tokens.astype(jnp.float32)
     inputs_span = tokens_span.astype(jnp.float32)
     normed_span = low(normalize(inputs_span, gain_attn))
-    normed_attn_wide = jnp.concatenate(
-        [normed_span, low(matrix_multiply(normed_span, delta_attention))], axis=1
-    )
-    keyval_span = matrix_multiply(normed_attn_wide, keyval_wide)
+    keyval_span = matrix_multiply(normed_span, keyval_eff)
     keys_span = rotate(keyval_span[:, None, :HEAD_WIDTH], span_positions, 1.0)[:, 0, :]
     keyval_low = low(jnp.concatenate([keys_span, keyval_span[:, HEAD_WIDTH:]], axis=1))
     keyval_other = partner(keyval_low, "fsdp", 0)
@@ -351,7 +350,7 @@
     )
     keys_all = keyval_all[:, :HEAD_WIDTH]
     values_all = keyval_all[:, HEAD_WIDTH:]
-    query_lin = matrix_multiply(normed_attn_wide, query_wide)
+    query_lin = matrix_multiply(normed_span, query_eff)
     local_heads = query_lin.shape[1] // HEAD_WIDTH
     query_rot = (
         rotate(query_lin.reshape(span_rows, local_heads, HEAD_WIDTH), span_positions, 1.0) * scaling
@@ -386,26 +385,15 @@
         .transpose(1, 0, 2)
         .reshape(span_rows, local_heads * HEAD_WIDTH)
     )
-    mixed_out = times_transposed(mixed_heads, out_wide)
-    mixed_delta = low(mixed_out[:, model_width:])
-    attn_result = scattered(
-        "tp",
-        low(mixed_out[:, :model_width] + matrix_multiply(mixed_delta, output_delta_product)),
-    )
+    mixed_out = low(times_transposed(mixed_heads, out_eff))
+    attn_result = scattered("tp", mixed_out)
     hidden = inputs + attn_result.astype(jnp.float32)
     normed_own = low(normalize(hidden, gain_mlp))
-    normed_wide = both_cores(
-        joined(
-            "tp",
-            jnp.concatenate(
-                [
-                    chip_relative(normed_own, 1),
-                    low(matrix_multiply(normed_own, delta_relative)),
-                ],
-                axis=1,
-            ),
-        )
-    )
+    normed_wide = jnp.concatenate(
+        [chip_relative(normed_own, 1), low(matrix_multiply(normed_own, delta_relative))], axis=1
+    )
+    normed_wide = joined("tp", normed_wide)
+    normed_wide = both_cores(normed_wide)
 
     grad_activation = matrix_multiply(grad_wide, down_wide)
     gate_lin = matrix_multiply(normed_wide, gate_wide)
@@ -420,41 +408,38 @@
     grad_gate, grad_up = low(grad_gate), low(grad_up)
     grad_normed_wide = times_transposed(grad_gate, gate_wide) + times_transposed(grad_up, up_wide)
     mlp_inner = low(grad_normed_wide[:, model_width:])
-    grad_normed_mlp = scattered(
-        "tp",
-        core_sum(
-            grad_normed_wide[:, :model_width]
-            + times_transposed(mlp_inner, delta_both)
-        ),
-    )
+    grad_normed_mlp = core_sum(
+        grad_normed_wide[:, :model_width] + times_transposed(mlp_inner, delta_both)
+    )
+    grad_normed_mlp = scattered("tp", grad_normed_mlp)
     grad_normed_mlp = chip_relative(grad_normed_mlp, 1).astype(jnp.float32)
     _, mlp_norm_pull = jax.vjp(normalize, hidden, gain_mlp)
     grad_hidden_norm, mlp_gain_part = mlp_norm_pull(grad_normed_mlp)
     grad_hidden = cotangent.astype(jnp.float32) + grad_hidden_norm
     grad_hidden_span = joined("tp", low(grad_hidden))
 
-    down_sum = scattered_wide(second, low(transposed_times(grad_wide, activation)), shard_rows)
-    gate_sum = scattered_wide(second, low(transposed_times(normed_wide, grad_gate)), shard_rows)
-    up_sum = scattered_wide(second, low(transposed_times(normed_wide, grad_up)), shard_rows)
+    down_grads = low(transposed_times(grad_wide, activation))
+    gate_grads = low(transposed_times(normed_wide, grad_gate))
+    up_grads = low(transposed_times(normed_wide, grad_up))
+    down_sum = scattered_wide(second, down_grads, shard_rows)
+    gate_sum = scattered_wide(second, gate_grads, shard_rows)
+    up_sum = scattered_wide(second, up_grads, shard_rows)
     mlp_lora_in = low(transposed_times(normed_wide[:, :model_width], mlp_inner))
     mlp_lora_in = chip_relative(chip_relative(mlp_lora_in, 0), 1)
     active_wide = times_transposed(activation, down_wide)
     active_delta = low(active_wide[:, model_width:])
     down_lora_out = transposed_times(active_delta, grad_wide[:, :model_width])
     down_lora_out = chip_relative(chip_relative(low(down_lora_out), 0), 1)
-    mlp_result = scattered(
-        "tp",
-        core_sum(
-            active_wide[:, :model_width]
-            + matrix_multiply(active_delta, down_delta_both)
-        ),
-    )
+    mlp_result = core_sum(
+        active_wide[:, :model_width] + matrix_multiply(active_delta, down_delta_both)
+    )
+    mlp_result = scattered("tp", mlp_result)
     result = low(hidden + chip_relative(mlp_result, 1).astype(jnp.float32))
 
     grad_hidden_wide = jnp.concatenate(
         [grad_hidden_span, low(times_transposed(grad_hidden_span, output_delta_product))], axis=1
     )
-    grad_mixed = low(matrix_multiply(grad_hidden_wide, out_wide))
+    grad_mixed = low(matrix_multiply(grad_hidden_span, out_eff))
     grad_blocks = (
         grad_mixed.reshape(span_rows, local_heads, HEAD_WIDTH)
         .transpose(1, 0, 2)
@@ -492,12 +477,12 @@
     keyval_part = mine + partner(theirs, "fsdp", 0)
     grad_keys = rotate(keyval_part[:, None, :HEAD_WIDTH], span_positions, -1.0)[:, 0, :]
     grad_keyval = low(jnp.concatenate([grad_keys, keyval_part[:, HEAD_WIDTH:]], axis=1))
-    grad_normed_both = times_transposed(grad_query_lin, query_wide) + times_transposed(
-        grad_keyval, keyval_wide
-    )
-    attn_inner = low(grad_normed_both[:, model_width:])
-    grad_normed_part = grad_normed_both[:, :model_width] + times_transposed(
-        attn_inner, delta_attention
+    grad_normed_part = times_transposed(grad_query_lin, query_eff) + times_transposed(
+        grad_keyval, keyval_eff
+    )
+    attn_inner = low(
+        times_transposed(grad_query_lin, query_delta_product)
+        + times_transposed(grad_keyval, key_value_delta_product)
     )
     grad_normed_attn = scattered("tp", low(grad_normed_part)).astype(jnp.float32)
     unit_span = inputs_span * lax.rsqrt(
@@ -507,6 +492,10 @@
     _, attn_norm_pull = jax.vjp(normalize, inputs, gain_attn)
     tokens_grad = grad_hidden + attn_norm_pull(grad_normed_attn)[0]
 
+    normed_attn_wide = jnp.concatenate(
+        [normed_span, low(matrix_multiply(normed_span, delta_attention))], axis=1
+    )
+    mixed_delta = low(times_transposed(mixed_heads, out_delta_in))
     out_lora_out = low(transposed_times(mixed_delta, grad_hidden_span))
     out_grads = low(transposed_times(grad_hidden_wide, mixed_heads))
     attn_grads = low(
@@ -560,7 +549,7 @@
     early_sum = scattered("fsdp", early)
     late_sum = scattered("fsdp", late)
     head_blocks = head_cols // rank
-    keyval_blocks = keyval_wide.shape[1] // rank
+    keyval_blocks = keyval_eff.shape[1] // rank
     model_blocks = model_width // rank
     split_rows = head_blocks * (main + extra)
     second_sum = scattered(
@@ -657,4 +646,5 @@
         P("tp", "fsdp"),
         P(("fsdp", "tp"), None),
     )
+
     return jax.shard_map(shards, mesh=mesh, in_specs=in_specs, out_specs=out_specs, check_vma=False)

time: 1200 us -> 1190 us (level)
  local copies, waits for them, and re-layouts: 247 us -> 234 us
    unnamed x463 -> x439, local copies, waits for them, and re-layouts: 160 us -> 153 us
    dot_general x14 -> x15, matrix products: 81 us -> 78.4 us  [matrix_multiply(): return jnp.dot(left_mat, right_mat, preferred_element_type=jnp.float32)]
    dot_general x12 -> x13, matrix products: 69.1 us -> 68 us  [transposed_times(): lax.dot_general(left_mat, right_mat, (((0,), (0,)), ((), ())), preferred_...]
    dot_general x16 -> x17, matrix products: 75.4 us -> 76.2 us  [times_transposed(): lax.dot_general(left_mat, right_mat, (((1,), (1,)), ((), ())), preferred_...]
  transfers between devices with their start and end apart: 57 -> 57, of which waited for: 22 -> 22; matrix products, arithmetic and copies ran while one was open for 34% -> 33% of each run, Pallas kernels for 0% -> 0%
where the time goes in v3:
time: 1190 us; the launch traced here: 1180 us
  waiting for transfers between devices  542 us (46%)
  local copies, waits for them, and re-layouts  234 us (20%)
  matrix products  223 us (19%)
  other arithmetic  117 us (10%)
  starting transfers between devices  42.6 us (4%)
  between operations  17.8 us (1%)
    ppermute x42, waiting for transfers between devices, partner(): return lax.ppermute(value, axis, pairs)  354 us
    unnamed x439, local copies, waits for them, and re-layouts  153 us
    dot_general x15, matrix products, matrix_multiply(): return jnp.dot(left_mat, right_mat, preferred_element_type=jnp.float32)  78.4 us
    dot_general x17, matrix products, times_transposed(): lax.dot_general(left_mat, right_mat, (((1,), (1,)), ((), ())), preferred_...  76.2 us
    reduce_scatter x7, waiting for transfers between devices, scattered(): return lax.psum_scatter(value, axis_names, scatter_dimension=0, tiled=True)  69.3 us
    dot_general x13, matrix products, transposed_times(): lax.dot_general(left_mat, right_mat, (((0,), (0,)), ((), ())), preferred_...  68 us
    ppermute x3, waiting for transfers between devices, tp_rows(): lax.ppermute(value, 'tp', [(at, (at + shift) % size) for at in range(size)])  59.4 us
    all_gather x3, waiting for transfers between devices, joined(): return lax.all_gather(value, axis_names, axis=axis, tiled=True)  58.2 us
  transfers between devices with their start and end apart: 57, of which 22 were waited for; matrix products, arithmetic and copies ran while one was open for 33% of the time, Pallas kernels for 0%

profile of v3, /device:TPU:0, one launch (start us, length us, event | category | flops | bytes accessed | tf_op | source)
XLA Modules:
  0.0 1183.9 jit_solution(11538996310852434568)
XLA Ops:
  11.1 5.1 collective-permute-start
  37.6 56.0 %collective-permute-done.1 = bf16[128,2048]{1,0:T(8,128)(2,1)} collective-permute-done((bf16[128,2048]{1,0:T(8,128)(2,1)S(1)}, bf16[128,2048]{1,0:T(8,128)(2,1)}, u32[]{:S(2)}, u32[]{:S(2)}) %collective-permute-start.1) | collective-permute-done | bytes 524320 | tf_op jit(solution)/shard_map/ppermute | solution.py:187
  131.8 45.5 %collective-permute-done.6 = bf16[576,2048]{1,0:T(8,128)(2,1)} collective-permute-done((bf16[576,2048]{1,0:T(8,128)(2,1)S(1)}, bf16[576,2048]{1,0:T(8,128)(2,1)}, u32[]{:S(2)}, u32[]{:S(2)}) %collective-permute-start.6) | collective-permute-done | bytes 2359328 | tf_op jit(solution)/shard_map/ppermute | solution.py:17
  182.2 63.6 %collective-permute-done.11 = bf16[576,2048]{1,0:T(8,128)(2,1)} collective-permute-done((bf16[576,2048]{1,0:T(8,128)(2,1)}, bf16[576,2048]{1,0:T(8,128)(2,1)}, u32[]{:S(2)}, u32[]{:S(2)}) %collective-permute-start.11) | collective-permute-done | bytes 2359328 | tf_op jit(solution)/shard_map/ppermute | solution.py:17
  269.5 26.8 %collective-permute-done.16 = bf16[576,2048]{1,0:T(8,128)(2,1)} collective-permute-done((bf16[576,2048]{1,0:T(8,128)(2,1)}, bf16[576,2048]{1,0:T(8,128)(2,1)}, u32[]{:S(2)}, u32[]{:S(2)}) %collective-permute-start.16) | collective-permute-done | bytes 2359328 | tf_op jit(solution)/shard_map/ppermute | solution.py:17
  307.2 12.1 %collective-permute-done.8 = bf16[288,2048]{1,0:T(8,128)(2,1)S(1)} collective-permute-done((bf16[288,2048]{1,0:T(8,128)(2,1)S(1)}, bf16[288,2048]{1,0:T(8,128)(2,1)S(1)}, u32[]{:S(2)}, u32[]{:S(2)}) %collective-permute-start.8) | collective-permute-done | bytes 1179680 | tf_op jit(solution)/shard_map/ppermute | solution.py:17
  323.2 21.2 %collective-permute-done.13 = bf16[288,2048]{1,0:T(8,128)(2,1)S(1)} collective-permute-done((bf16[288,2048]{1,0:T(8,128)(2,1)S(1)}, bf16[288,2048]{1,0:T(8,128)(2,1)S(1)}, u32[]{:S(2)}, u32[]{:S(2)}) %collective-permute-start.13) | collective-permute-done | bytes 1179680 | tf_op jit(solution)/shard_map/ppermute | solution.py:17
  351.8 15.7 %collective-permute-done.18 = bf16[288,2048]{1,0:T(8,128)(2,1)S(1)} collective-permute-done((bf16[288,2048]{1,0:T(8,128)(2,1)S(1)}, bf16[288,2048]{1,0:T(8,128)(2,1)S(1)}, u32[]{:S(2)}, u32[]{:S(2)}) %collective-permute-start.18) | collective-permute-done | bytes 1179680 | tf_op jit(solution)/shard_map/ppermute | solution.py:17
  424.1 17.1 %while.36 = (s32[]{:T(128)}, bf16[2,512,256]{1,2,0:T(8,128)(2,1)}, f32[2,512]{1,0:T(2,128)S(1)}, s32[]{:T(128)}, s32[]{:T(128)}, /*index=5*/s32[]{:T(128)}, s32[...) while((s32[]{:T(128)}, bf16[2,512,256]{1,2,0:T(8,128)(2,1)}, ...), condition=%wide.region_4.5_spmd.clone.clone.clone, body=%wide.region_1.4_spmd.clone.clone.sunk.clone | while | flops 542118912 | bytes 8154803 | solution.py:382
  459.6 31.2 %reduce-scatter.8.cloned.1.call-done = bf16[128,2048]{1,0:T(8,128)(2,1)} async-done(((bf16[512,2048]{1,0:T(8,128)(2,1)}), bf16[128,2048]{1,0:T(8,128)(2,1)}) %reduce-scatter.8.cloned.1.call-update) | async-done | bytes 524304 | tf_op jit(solution)/shard_map/reduce_scatter | solution.py:67
  514.1 32.6 %all-gather.8.cloned.1.call-done = bf16[512,2304]{1,0:T(8,128)(2,1)} async-done(((bf16[128,2304]{1,0:T(8,128)(2,1)}), bf16[512,2304]{1,0:T(8,128)(2,1)}) %all-gather.8.cloned.1.call-update) | async-done | bytes 2359312 | tf_op jit(solution)/shard_map/all_gather | solution.py:63
  546.6 15.6 %fusion.49 = f32[1024,2048]{1,0:T(8,128)} fusion(bf16[2304,2048]{1,0:T(8,128)(2,1)} %constant_dynamic-update-slice_fusion.64, bf16[512,2304]{1,0:T(8,128)(2,1)} %collective-permute-done.21, bf16[512,2304]{1,0:T(8,128)(2,1)S(1)} %copy-done.119), kind=kOutput, calls=%fused_computation.102 | convolution fusion | flops 9673113600 | bytes 22544384 | tf_op jit(solution)/shard_map/dot_general | solution.py:21
  562.6 16.1 %fusion.170 = f32[1024,2048]{1,0:T(8,128)} fusion(bf16[1024,2304]{1,0:T(8,128)(2,1)S(1)} %constant_dynamic-update-slice_fusion.42, bf16[2304,2048]{1,0:T(8,128)(2,1)} %constant_dynamic-update-slice_fusion.56), kind=kOutput, calls=%fused_computation.649 | convolution fusion | flops 9663676416 | bytes 22544384 | tf_op jit(solution)/shard_map/dot_general | solution.py:21
  578.7 23.9 %fusion.35 = (bf16[1024,2048]{1,0:T(8,128)(2,1)}, bf16[1024,2048]{1,0:T(8,128)(2,1)}, bf16[1024,2048]{1,0:T(8,128)(2,1)}) fusion(f32[1024,2048]{1,0:T(8,128)} %fusion.49, f32[1024,2048]{1,0:T(8,128)} %fusion.170, bf16[1024,2304]{1,0:T(8,128)(2,1)S(1)} %constant_dynamic-update-slice_fusion.42, bf16[2304,2048]{1,0:T(8,128)(2,1)} %constant_dynamic-update-slice_fusion.46), kind=kOutput, calls=%fused_computation.60 | convolution fusion | flops 9718202368 | bytes 43515904 | tf_op jit(solution)/shard_map/dot_general | solution.py:21
  602.7 15.8 %fusion.171 = f32[1024,2304]{1,0:T(8,128)} fusion(bf16[1024,2048]{1,0:T(8,128)(2,1)} %get-tuple-element.607, bf16[2304,2048]{1,0:T(8,128)(2,1)} %constant_dynamic-update-slice_fusion.64), kind=kOutput, calls=%fused_computation.650 | convolution fusion | flops 9663676416 | bytes 23068672 | tf_op jit(solution)/shard_map/dot_general | solution.py:25
  618.5 11.7 convolution_convert_fusion
  634.2 13.9 %fusion.172 = f32[1024,2304]{1,0:T(8,128)} fusion(bf16[1024,2048]{1,0:T(8,128)(2,1)S(1)} %copy-done.153, bf16[2304,2048]{1,0:T(8,128)(2,1)} %constant_dynamic-update-slice_fusion.56), kind=kOutput, calls=%fused_computation.651 | convolution fusion | flops 9663676416 | bytes 23068672 | tf_op jit(solution)/shard_map/dot_general | solution.py:25
  648.1 18.2 %convolution_add_fusion.2 = f32[1024,2304]{1,0:T(8,128)} fusion(f32[1024,2304]{1,0:T(8,128)} %fusion.172, bf16[1024,2048]{1,0:T(8,128)(2,1)} %get-tuple-element.605, bf16[2304,2048]{1,0:T(8,128)(2,1)} %constant_dynamic-update-slice_fusion.46), kind=kOutput, calls=%fused_computation.66 | convolution fusion | flops 9666035712 | bytes 32505856 | tf_op jit(solution)/shard_map/dot_general | solution.py:25
  706.7 12.3 %convolution_convert_fusion.1 = bf16[2304,2048]{1,0:T(8,128)(2,1)} fusion(bf16[1024,2304]{1,0:T(8,128)(2,1)S(1)} %bitcast.470, bf16[1024,2048]{1,0:T(8,128)(2,1)S(1)} %copy-done.154), kind=kOutput, calls=%fused_computation.51 | convolution fusion | flops 9668395008 | bytes 18350080 | tf_op jit(solution)/shard_map/dot_general | solution.py:31
  719.0 20.4 %reduce-scatter.12.cloned.1.call-done = bf16[128,2048]{1,0:T(8,128)(2,1)} async-done(((bf16[512,2048]{1,0:T(8,128)(2,1)}), bf16[128,2048]{1,0:T(8,128)(2,1)}) %reduce-scatter.12.cloned.1.call-update) | async-done | bytes 524304 | tf_op jit(solution)/shard_map/reduce_scatter | solution.py:67
  747.5 5.4 fusion.152
  763.1 25.6 %all-gather.12.cloned.1.call-done = bf16[512,2048]{1,0:T(8,128)(2,1)} async-done(((bf16[128,2048]{1,0:T(8,128)(2,1)}), bf16[512,2048]{1,0:T(8,128)(2,1)}) %all-gather.12.cloned.1.call-update) | async-done | bytes 2097168 | tf_op jit(solution)/shard_map/all_gather | solution.py:63
  793.2 31.6 %while.37 = (s32[]{:T(128)}, f32[1024,256]{1,0:T(8,128)}, f32[1024,256]{1,0:T(8,128)}, f32[2,512,256]{1,2,0:T(8,128)}, s32[]{:T(128)}, /*index=5*/s32[]{:T(128)}...) while((s32[]{:T(128)}, f32[1024,256]{1,0:T(8,128)}, ...), condition=%wide.region_12.13_spmd.clone.clone.clone, body=%wide.region_10.12_spmd.clone.clone.sunk.clone | while | flops 1348998144 | bytes 33572160 | solution.py:463
  864.2 13.2 %convolution_convert_fusion.2 = bf16[2304,2048]{1,0:T(8,128)(2,1)S(1)} fusion(bf16[1024,2304]{1,0:T(8,128)(2,1)} %copy-done.68, bf16[1024,2048]{1,0:T(8,128)(2,1)} %get-tuple-element.605), kind=kOutput, calls=%fused_computation.52 | convolution fusion | flops 9668395008 | bytes 18350080 | tf_op jit(solution)/shard_map/dot_general | solution.py:31
  921.2 38.9 %collective-permute-done.32 = bf16[576,1024]{1,0:T(8,128)(2,1)} collective-permute-done((bf16[576,1024]{1,0:T(8,128)(2,1)}, bf16[576,1024]{1,0:T(8,128)(2,1)}, u32[]{:S(2)}, u32[]{:S(2)}) %collective-permute-start.32) | collective-permute-done | bytes 1179680 | tf_op jit(solution)/shard_map/ppermute | solution.py:17
  967.5 23.0 %collective-permute-done.25 = bf16[576,1024]{1,0:T(8,128)(2,1)} collective-permute-done((bf16[576,1024]{1,0:T(8,128)(2,1)}, bf16[576,1024]{1,0:T(8,128)(2,1)}, u32[]{:S(2)}, u32[]{:S(2)}) %collective-permute-start.25) | collective-permute-done | bytes 1179680 | tf_op jit(solution)/shard_map/ppermute | solution.py:17
  996.1 34.4 %collective-permute-done.43 = bf16[576,1024]{1,0:T(8,128)(2,1)S(1)} collective-permute-done((bf16[576,1024]{1,0:T(8,128)(2,1)}, bf16[576,1024]{1,0:T(8,128)(2,1)S(1)}, u32[]{:S(2)}, u32[]{:S(2)}) %collective-permute-start.43) | collective-permute-done | bytes 1179680 | tf_op jit(solution)/shard_map/ppermute | solution.py:17
  1032.9 31.7 %collective-permute-done.36 = bf16[576,1024]{1,0:T(8,128)(2,1)S(1)} collective-permute-done((bf16[576,1024]{1,0:T(8,128)(2,1)}, bf16[576,1024]{1,0:T(8,128)(2,1)S(1)}, u32[]{:S(2)}, u32[]{:S(2)}) %collective-permute-start.36) | collective-permute-done | bytes 1179680 | tf_op jit(solution)/shard_map/ppermute | solution.py:17
  1074.2 15.7 %collective-permute-done.24 = bf16[576,1024]{1,0:T(8,128)(2,1)S(1)} collective-permute-done((bf16[576,1024]{1,0:T(8,128)(2,1)S(1)}, bf16[576,1024]{1,0:T(8,128)(2,1)S(1)}, u32[]{:S(2)}, u32[]{:S(2)}) %collective-permute-start.24) | collective-permute-done | bytes 1179680 | tf_op jit(solution)/shard_map/ppermute | solution.py:17
  1089.9 23.8 %collective-permute-done.29 = bf16[576,1024]{1,0:T(8,128)(2,1)S(1)} collective-permute-done((bf16[576,1024]{1,0:T(8,128)(2,1)S(1)}, bf16[576,1024]{1,0:T(8,128)(2,1)S(1)}, u32[]{:S(2)}, u32[]{:S(2)}) %collective-permute-start.29) | collective-permute-done | bytes 1179680 | tf_op jit(solution)/shard_map/ppermute | solution.py:17
  1134.4 5.6 copy.76
  1155.5 17.7 %reduce-scatter.20.cloned.1.call-done = bf16[1,416,256]{2,1,0:T(8,128)(2,1)} async-done(((bf16[4,416,256]{2,1,0:T(8,128)(2,1)}), bf16[1,416,256]{2,1,0:T(8,128)(2,1)}) %reduce-scatter.20.cloned.1.call-update) | async-done | bytes 213008 | tf_op jit(solution)/shard_map/reduce_scatter | solution.py:67
  (803 shorter events, 465.1 us)
Async XLA Ops:
  7.2 120.1 %all-gather.10.cloned.1.call-start = ((), (), s32[]{:S(2)}) async-start(), calls=%async_computation.10 | async-start | bytes 2621440 | tf_op jit(solution)/shard_map/all_gather | solution.py:63
  7.9 373.1 %all-gather.16.cloned.1.call-start = ((), (), s32[]{:S(2)}) async-start(), calls=%async_computation.18 | async-start | bytes 5308416 | tf_op jit(solution)/shard_map/all_gather | solution.py:307
  11.0 376.0 %all-gather.14.cloned.1.call-start = ((), (), s32[]{:S(2)}) async-start(), calls=%async_computation.17 | async-start | bytes 6893568 | tf_op jit(solution)/shard_map/all_gather | solution.py:90
  16.2 78.4 %collective-permute-start.2 = (bf16[128,2048]{1,0:T(8,128)(2,1)S(1)}, bf16[128,2048]{1,0:T(8,128)(2,1)}, u32[]{:S(2)}, u32[]{:S(2)}) collective-permute-start(bf16[128,2048]{1,0:T(8,128)(2,1)S(1)} %copy-done.3), channel_id=1, source_target_pairs={{0,1},{1,2},{2,3},{3,0},{4,5},{5,6},{6,7},{7,4},{8,9},{9,10},{10,1... | collective-permute-start | bytes 1572872 | tf_op jit(solution)/shard_map/ppermute | solution.py:187
  19.0 82.4 %collective-permute-start.5 = (bf16[288,2048]{1,0:T(8,128)(2,1)}, bf16[288,2048]{1,0:T(8,128)(2,1)}, u32[]{:S(2)}, u32[]{:S(2)}) collective-permute-start(bf16[288,2048]{1,0:T(8,128)(2,1)} %get-tuple-element.701), channel_id=1, source_target_pairs={{0,4},{4,0},{8,12},{12,8},{16,20},{20,16},{24,28},{28,24},{1,5},{5... | collective-permute-start | bytes 3538952 | tf_op jit(solution)/shard_map/ppermute | solution.py:17
  21.9 85.3 %collective-permute-start.10 = (bf16[288,2048]{1,0:T(8,128)(2,1)}, bf16[288,2048]{1,0:T(8,128)(2,1)}, u32[]{:S(2)}, u32[]{:S(2)}) collective-permute-start(bf16[288,2048]{1,0:T(8,128)(2,1)} %get-tuple-element.703), channel_id=1, source_target_pairs={{0,4},{4,0},{8,12},{12,8},{16,20},{20,16},{24,28},{28,24},{1,5},{5... | collective-permute-start | bytes 3538952 | tf_op jit(solution)/shard_map/ppermute | solution.py:17
  22.9 467.9 %reduce-scatter.8.cloned.1.call-start = ((), (), s32[]{:S(2)}) async-start(), calls=%async_computation.7 | async-start | bytes 2621440 | tf_op jit(solution)/shard_map/reduce_scatter | solution.py:67
  36.5 78.5 %collective-permute-start.15 = (bf16[288,2048]{1,0:T(8,128)(2,1)}, bf16[288,2048]{1,0:T(8,128)(2,1)S(1)}, u32[]{:S(2)}, u32[]{:S(2)}) collective-permute-start(bf16[288,2048]{1,0:T(8,128)(2,1)} %get-tuple-element.699), channel_id=1, source_target_pairs={{0,4},{4,0},{8,12},{12,8},{16,20},{20,16},{24,28},{28,24},{1,5},{5... | collective-permute-start | bytes 3538952 | tf_op jit(solution)/shard_map/ppermute | solution.py:17
  110.7 135.1 %collective-permute-start.11 = (bf16[576,2048]{1,0:T(8,128)(2,1)}, bf16[576,2048]{1,0:T(8,128)(2,1)}, u32[]{:S(2)}, u32[]{:S(2)}) collective-permute-start(bf16[576,2048]{1,0:T(8,128)(2,1)} %maximum_select_fusion.4), channel_id=1, source_target_pairs={{0,8},{4,12},{8,0},{12,4},{16,24},{20,28},{24,16},{28,20},{1,9},{5... | collective-permute-start | bytes 7077896 | tf_op jit(solution)/shard_map/ppermute | solution.py:17
  111.2 143.7 %collective-permute-start.12 = (bf16[576,2048]{1,0:T(8,128)(2,1)}, bf16[576,2048]{1,0:T(8,128)(2,1)}, u32[]{:S(2)}, u32[]{:S(2)}) collective-permute-start(bf16[576,2048]{1,0:T(8,128)(2,1)} %maximum_select_fusion.4), channel_id=1, source_target_pairs={{0,16},{4,20},{8,24},{12,28},{16,0},{20,4},{24,8},{28,12},{1,17},{... | collective-permute-start | bytes 7077896 | tf_op jit(solution)/shard_map/ppermute | solution.py:17
  120.1 176.2 %collective-permute-start.16 = (bf16[576,2048]{1,0:T(8,128)(2,1)}, bf16[576,2048]{1,0:T(8,128)(2,1)}, u32[]{:S(2)}, u32[]{:S(2)}) collective-permute-start(bf16[576,2048]{1,0:T(8,128)(2,1)} %maximum_select_fusion.5), channel_id=1, source_target_pairs={{0,8},{4,12},{8,0},{12,4},{16,24},{20,28},{24,16},{28,20},{1,9},{5... | collective-permute-start | bytes 7077896 | tf_op jit(solution)/shard_map/ppermute | solution.py:17
  177.3 125.7 %collective-permute-start.17 = (bf16[576,2048]{1,0:T(8,128)(2,1)}, bf16[576,2048]{1,0:T(8,128)(2,1)S(1)}, u32[]{:S(2)}, u32[]{:S(2)}) collective-permute-start(bf16[576,2048]{1,0:T(8,128)(2,1)} %maximum_select_fusion.5), channel_id=1, source_target_pairs={{0,16},{4,20},{8,24},{12,28},{16,0},{20,4},{24,8},{28,12},{1,17},{... | collective-permute-start | bytes 7077896 | tf_op jit(solution)/shard_map/ppermute | solution.py:17
  180.2 139.0 %collective-permute-start.8 = (bf16[288,2048]{1,0:T(8,128)(2,1)S(1)}, bf16[288,2048]{1,0:T(8,128)(2,1)S(1)}, u32[]{:S(2)}, u32[]{:S(2)}) collective-permute-start(bf16[288,2048]{1,0:T(8,128)(2,1)S(1)} %slice.1555), channel_id=1, source_target_pairs={{0,16},{4,20},{8,24},{12,28},{16,0},{20,4},{24,8},{28,12},{1,17},{... | collective-permute-start | bytes 3538952 | tf_op jit(solution)/shard_map/ppermute | solution.py:17
  254.9 89.6 %collective-permute-start.13 = (bf16[288,2048]{1,0:T(8,128)(2,1)S(1)}, bf16[288,2048]{1,0:T(8,128)(2,1)S(1)}, u32[]{:S(2)}, u32[]{:S(2)}) collective-permute-start(bf16[288,2048]{1,0:T(8,128)(2,1)S(1)} %slice.1575), channel_id=1, source_target_pairs={{0,16},{4,20},{8,24},{12,28},{16,0},{20,4},{24,8},{28,12},{1,17},{... | collective-permute-start | bytes 3538952 | tf_op jit(solution)/shard_map/ppermute | solution.py:17
  445.8 100.8 %all-gather.8.cloned.1.call-start = ((), (), s32[]{:S(2)}) async-start(), calls=%async_computation.8 | async-start | bytes 2949120 | tf_op jit(solution)/shard_map/all_gather | solution.py:63
  497.3 242.1 %reduce-scatter.12.cloned.1.call-start = ((), (), s32[]{:S(2)}) async-start(), calls=%async_computation.11 | async-start | bytes 2621440 | tf_op jit(solution)/shard_map/reduce_scatter | solution.py:67
  674.9 213.1 %collective-permute-start.42 = (bf16[576,1024]{1,0:T(8,128)(2,1)}, bf16[576,1024]{1,0:T(8,128)(2,1)}, u32[]{:S(2)}, u32[]{:S(2)}) collective-permute-start(bf16[576,1024]{1,0:T(8,128)(2,1)} %get-tuple-element.688), channel_id=1, source_target_pairs={{0,16},{4,20},{8,24},{12,28},{16,0},{20,4},{24,8},{28,12},{1,17},{... | collective-permute-start | bytes 3538952 | tf_op jit(solution)/shard_map/ppermute | solution.py:17
  677.8 233.8 %collective-permute-start.38 = (bf16[576,1024]{1,0:T(8,128)(2,1)}, bf16[576,1024]{1,0:T(8,128)(2,1)}, u32[]{:S(2)}, u32[]{:S(2)}) collective-permute-start(bf16[576,1024]{1,0:T(8,128)(2,1)} %slice.1776), channel_id=1, source_target_pairs={{0,8},{4,12},{8,0},{12,4},{16,24},{20,28},{24,16},{28,20},{1,9},{5... | collective-permute-start | bytes 3538952 | tf_op jit(solution)/shard_map/ppermute | solution.py:17
  679.3 213.0 %collective-permute-start.39 = (bf16[576,1024]{1,0:T(8,128)(2,1)}, bf16[576,1024]{1,0:T(8,128)(2,1)}, u32[]{:S(2)}, u32[]{:S(2)}) collective-permute-start(bf16[576,1024]{1,0:T(8,128)(2,1)} %get-tuple-element.687), channel_id=1, source_target_pairs={{0,8},{4,12},{8,0},{12,4},{16,24},{20,28},{24,16},{28,20},{1,9},{5... | collective-permute-start | bytes 3538952 | tf_op jit(solution)/shard_map/ppermute | solution.py:17
  681.3 236.1 %collective-permute-start.41 = (bf16[576,1024]{1,0:T(8,128)(2,1)}, bf16[576,1024]{1,0:T(8,128)(2,1)}, u32[]{:S(2)}, u32[]{:S(2)}) collective-permute-start(bf16[576,1024]{1,0:T(8,128)(2,1)} %slice.1788), channel_id=1, source_target_pairs={{0,16},{4,20},{8,24},{12,28},{16,0},{20,4},{24,8},{28,12},{1,17},{... | collective-permute-start | bytes 3538952 | tf_op jit(solution)/shard_map/ppermute | solution.py:17
  697.0 91.8 %all-gather.12.cloned.1.call-start = ((), (), s32[]{:S(2)}) async-start(), calls=%async_computation.12 | async-start | bytes 2621440 | tf_op jit(solution)/shard_map/all_gather | solution.py:63
  743.7 398.4 %reduce-scatter.10.cloned.1.call-start = ((), (), s32[]{:S(2)}) async-start(), calls=%async_computation.9 | async-start | bytes 2621440 | tf_op jit(solution)/shard_map/reduce_scatter | solution.py:67
  762.9 380.3 %reduce-scatter.14.cloned.1.call-start = ((), (), s32[]{:S(2)}) async-start(), calls=%async_computation.13 | async-start | bytes 2621440 | tf_op jit(solution)/shard_map/reduce_scatter | solution.py:67
  846.1 301.6 %reduce-scatter.16.cloned.1.call-start = ((), (), s32[]{:S(2)}) async-start(), calls=%async_computation.14 | async-start | bytes 6340608 | tf_op jit(solution)/shard_map/reduce_scatter | solution.py:67
  864.0 284.8 %reduce-scatter.18.cloned.1.call-start = ((), (), s32[]{:S(2)}) async-start(), calls=%async_computation.15 | async-start | bytes 6635520 | tf_op jit(solution)/shard_map/reduce_scatter | solution.py:67
  911.7 78.8 %collective-permute-start.25 = (bf16[576,1024]{1,0:T(8,128)(2,1)}, bf16[576,1024]{1,0:T(8,128)(2,1)}, u32[]{:S(2)}, u32[]{:S(2)}) collective-permute-start(bf16[576,1024]{1,0:T(8,128)(2,1)} %get-tuple-element.695), channel_id=1, source_target_pairs={{0,8},{4,12},{8,0},{12,4},{16,24},{20,28},{24,16},{28,20},{1,9},{5... | collective-permute-start | bytes 3538952 | tf_op jit(solution)/shard_map/ppermute | solution.py:17
  917.1 256.1 %reduce-scatter.20.cloned.1.call-start = ((), (), s32[]{:S(2)}) async-start(), calls=%async_computation.16 | async-start | bytes 1064960 | tf_op jit(solution)/shard_map/reduce_scatter | solution.py:67
  919.0 111.5 %collective-permute-start.43 = (bf16[576,1024]{1,0:T(8,128)(2,1)}, bf16[576,1024]{1,0:T(8,128)(2,1)S(1)}, u32[]{:S(2)}, u32[]{:S(2)}) collective-permute-start(bf16[576,1024]{1,0:T(8,128)(2,1)} %add_convert_fusion.3), channel_id=1, source_target_pairs={{0,8},{4,12},{8,0},{12,4},{16,24},{20,28},{24,16},{28,20},{1,9},{5... | collective-permute-start | bytes 3538952 | tf_op jit(solution)/shard_map/ppermute | solution.py:17
  960.1 104.5 %collective-permute-start.36 = (bf16[576,1024]{1,0:T(8,128)(2,1)}, bf16[576,1024]{1,0:T(8,128)(2,1)S(1)}, u32[]{:S(2)}, u32[]{:S(2)}) collective-permute-start(bf16[576,1024]{1,0:T(8,128)(2,1)} %add_convert_fusion.5), channel_id=1, source_target_pairs={{0,8},{4,12},{8,0},{12,4},{16,24},{20,28},{24,16},{28,20},{1,9},{5... | collective-permute-start | bytes 3538952 | tf_op jit(solution)/shard_map/ppermute | solution.py:17
  990.4 78.2 %collective-permute-start.33 = (bf16[576,1024]{1,0:T(8,128)(2,1)S(1)}, bf16[576,1024]{1,0:T(8,128)(2,1)S(1)}, u32[]{:S(2)}, u32[]{:S(2)}) collective-permute-start(bf16[576,1024]{1,0:T(8,128)(2,1)S(1)} %add_convert_fusion.6), channel_id=1, source_target_pairs={{0,16},{4,20},{8,24},{12,28},{16,0},{20,4},{24,8},{28,12},{1,17},{... | collective-permute-start | bytes 3538952 | tf_op jit(solution)/shard_map/ppermute | solution.py:17
  994.6 95.3 %collective-permute-start.24 = (bf16[576,1024]{1,0:T(8,128)(2,1)S(1)}, bf16[576,1024]{1,0:T(8,128)(2,1)S(1)}, u32[]{:S(2)}, u32[]{:S(2)}) collective-permute-start(bf16[576,1024]{1,0:T(8,128)(2,1)S(1)} %slice.1722), channel_id=1, source_target_pairs={{0,8},{4,12},{8,0},{12,4},{16,24},{20,28},{24,16},{28,20},{1,9},{5... | collective-permute-start | bytes 3538952 | tf_op jit(solution)/shard_map/ppermute | solution.py:17
  1030.5 83.2 %collective-permute-start.29 = (bf16[576,1024]{1,0:T(8,128)(2,1)S(1)}, bf16[576,1024]{1,0:T(8,128)(2,1)S(1)}, u32[]{:S(2)}, u32[]{:S(2)}) collective-permute-start(bf16[576,1024]{1,0:T(8,128)(2,1)S(1)} %add_convert_fusion.7), channel_id=1, source_target_pairs={{0,8},{4,12},{8,0},{12,4},{16,24},{20,28},{24,16},{28,20},{1,9},{5... | collective-permute-start | bytes 3538952 | tf_op jit(solution)/shard_map/ppermute | solution.py:17
  (188 other events, 3763.2 us)
Sparse Core Ops, SparseCore 0:
  9.6 85.3 all-gather.9
  96.9 56.1 all-gather.15
  156.5 88.9 all-gather.13
  445.9 44.8 reduce-scatter.7
  497.4 49.1 all-gather.7
  697.1 42.2 reduce-scatter.11
  743.8 44.8 all-gather.11
  791.0 42.4 reduce-scatter.9
  846.2 41.6 reduce-scatter.13
  891.2 80.4 reduce-scatter.15
  975.1 83.4 reduce-scatter.17
  1150.9 22.2 reduce-scatter.19

commit v4 on v3

--- a/solution.py
+++ b/solution.py
@@ -107,13 +107,13 @@
     chips = fsdp_size // 2
     if chips != 4:
         whole = lax.all_gather(value, "fsdp", axis=0, axis_index_groups=chip_groups(fsdp_size))
-        return [whole[at] for at in range(chips)]
+        return [[whole[at]] for at in range(chips)]
     half = value.shape[0] // 2
     along_x = partner(value, "fsdp", 1)
     along_y = partner(value, "fsdp", 2)
     far_low = partner(along_x[:half], "fsdp", 2)
     far_high = partner(along_y[half:], "fsdp", 1)
-    return [value, along_x, along_y, jnp.concatenate([far_low, far_high], axis=0)]
+    return [[value], [along_x], [along_y], [far_low, far_high]]
 
 
 def chip_scatter(pieces):
@@ -194,34 +194,74 @@
     )
 
 
+def row_parts(pieces, first, last):
+    parts, start = [], 0
+    for piece in pieces:
+        low_row, high_row = max(first - start, 0), min(last - start, piece.shape[0])
+        if low_row < high_row:
+            parts.append(piece[low_row:high_row])
+        start += piece.shape[0]
+    return parts
+
+
 def gathered_wide(second, main, extra):
+    rows = main.shape[0]
     shard = jnp.concatenate([main, extra], axis=0)
+    mine = own_half(second, shard)
     theirs = partner(own_half(second, shard, True), "fsdp", 0)
-    pieces = chip_gather(in_order(second, own_half(second, shard), theirs, 0))
-    rows, wide = main.shape[0], shard.shape[0]
-    return jnp.concatenate(
-        [piece[at * wide : at * wide + rows] for piece in pieces for at in range(2)]
-        + [piece[at * wide + rows : (at + 1) * wide] for piece in pieces for at in range(2)],
-        axis=0,
-    )
+    block = jnp.where(
+        second,
+        jnp.concatenate([theirs[:rows], mine[:rows], theirs[rows:], mine[rows:]], axis=0),
+        jnp.concatenate([mine[:rows], theirs[:rows], mine[rows:], theirs[rows:]], axis=0),
+    )
+    pieces = chip_gather(block)
+    wide = []
+    for first, last in ((0, 2 * rows), (2 * rows, block.shape[0])):
+        for piece in pieces:
+            wide += row_parts(piece, first, last)
+    return jnp.concatenate(wide, axis=0)
 
 
 def scattered_wide(second, value, rows):
     chips = lax.axis_size("fsdp") // 2
-    extra = (value.shape[0] - chips * 2 * rows) // (2 * chips)
     main_end = chips * 2 * rows
-    pieces = []
-    for chip in range(chips):
-        for core in range(2):
-            at = 2 * chip + core
-            pieces.append(value[at * rows : (at + 1) * rows])
-            pieces.append(value[main_end + at * extra : main_end + (at + 1) * extra])
-    pieces = [jnp.concatenate(pieces[4 * at : 4 * at + 4], axis=0) for at in range(chips)]
+    extra = (value.shape[0] - main_end) // (2 * chips)
+    pieces = [
+        jnp.concatenate(
+            [
+                value[2 * at * rows : 2 * (at + 1) * rows],
+                value[main_end + 2 * at * extra : main_end + 2 * (at + 1) * extra],
+            ],
+            axis=0,
+        )
+        for at in range(chips)
+    ]
     summed = chip_scatter(pieces)
-    wide = rows + extra
-    mine = jnp.where(second, summed[wide:], summed[:wide])
-    theirs = partner(low(jnp.where(second, summed[:wide], summed[wide:])), "fsdp", 0)
-    return in_order(second, mine, theirs.astype(jnp.float32), 1)
+    first = jnp.concatenate([summed[:rows], summed[2 * rows : 2 * rows + extra]], axis=0)
+    other = jnp.concatenate([summed[rows : 2 * rows], summed[2 * rows + extra :]], axis=0)
+    sent = low(jnp.where(second, first, other))
+    theirs = partner(sent, "fsdp", 0)
+    return in_order(second, jnp.where(second, other, first), theirs.astype(jnp.float32), 1)
+
+
+def device_sum(value):
+    fsdp_size = lax.axis_size("fsdp")
+    tp_size = lax.axis_size("tp")
+    if fsdp_size != 8:
+        return scattered("fsdp", value).astype(jnp.float32)
+    placed = lax.axis_index("fsdp")
+    rows, width = value.shape[1:]
+    value = value.reshape(4, 2, tp_size * rows, width)
+    mine = lax.dynamic_index_in_dim(value, placed % 2, 1, keepdims=False)
+    got = partner(
+        lax.dynamic_index_in_dim(value, 1 - placed % 2, 1, keepdims=False), "fsdp", 0
+    )
+    chip_sums = low(mine.astype(jnp.float32) + got.astype(jnp.float32))
+    pieces = [
+        lax.dynamic_index_in_dim(chip_sums, (placed // 2) ^ at, 0, keepdims=False)
+        for at in range(4)
+    ]
+    return chip_scatter(pieces).reshape(tp_size, rows, width)
 
 
 def shards(
@@ -279,18 +319,24 @@
     common.add(key_value_shared_weight)
     common.add(attention_delta_input)
     common.add(key_value_delta_output)
-    common.add(output_delta_output)
-    common.add(feedforward_delta_input)
-    common.add(down_delta_output)
-    (
-        gains,
-        key_value_complete,
-        delta_attention,
-        key_value_delta_product,
-        output_delta_product,
-        delta_feedforward,
-        down_delta_product,
-    ) = common.gather(both)
+    (gains, key_value_complete, delta_attention, key_value_delta_product) = common.gather(both)
+    extra = output_delta_output.shape[0]
+    lanes = [
+        feedforward_delta_input[at * extra : (at + 1) * extra] for at in range(model_width // rank)
+    ]
+    extra_own = jnp.concatenate(
+        [output_delta_output, down_delta_output, jnp.concatenate(lanes, axis=1)], axis=0
+    )
+    extra_stack = lax.all_gather(extra_own, both, axis=0)
+    output_delta_product = extra_stack[:, :extra].reshape(rank, model_width)
+    down_delta_product = extra_stack[:, extra : 2 * extra].reshape(rank, model_width)
+    delta_feedforward = jnp.concatenate(
+        [
+            extra_stack[:, 2 * extra :, at : at + rank]
+            for at in range(0, model_width, rank)
+        ],
+        axis=1,
+    ).reshape(model_width, rank)
     gains = gains.reshape(parts, 8, rank)[:, :2, : gain_rows.shape[1]].astype(jnp.float32)
     gain_attn = gains[:, 0].reshape(-1)
     gain_mlp = gains[:, 1].reshape(-1)
@@ -321,7 +367,7 @@
         + matrix_multiply(delta_attention, key_value_delta_product)
     )
 
-    grad_span = joined("tp", cotangent)
+    grad_span = tp_rows(cotangent)
     down_delta_relative = chip_relative(down_delta_product, 0)
     grad_wide = both_cores(
         jnp.concatenate(
@@ -389,9 +435,8 @@
     attn_result = scattered("tp", mixed_out)
     hidden = inputs + attn_result.astype(jnp.float32)
     normed_own = low(normalize(hidden, gain_mlp))
-    normed_wide = jnp.concatenate(
-        [chip_relative(normed_own, 1), low(matrix_multiply(normed_own, delta_relative))], axis=1
-    )
+    normed_delta = low(matrix_multiply(normed_own, delta_relative))
+    normed_wide = jnp.concatenate([chip_relative(normed_own, 1), normed_delta], axis=1)
     normed_wide = joined("tp", normed_wide)
     normed_wide = both_cores(normed_wide)
 
@@ -546,17 +591,17 @@
         ],
         axis=1,
     )
-    early_sum = scattered("fsdp", early)
-    late_sum = scattered("fsdp", late)
+    early_sum = device_sum(early)
+    late_sum = device_sum(late)
     head_blocks = head_cols // rank
     keyval_blocks = keyval_eff.shape[1] // rank
     model_blocks = model_width // rank
     split_rows = head_blocks * (main + extra)
     second_sum = scattered(
-        "tp", jnp.concatenate([early_sum[:, split_rows:], late_sum[:, split_rows:]], axis=1)
+        "tp", low(jnp.concatenate([early_sum[:, split_rows:], late_sum[:, split_rows:]], axis=1))
     )[0].astype(jnp.float32)
-    out_split = early_sum[:, :split_rows].astype(jnp.float32)
-    query_split = late_sum[:, :split_rows].astype(jnp.float32)
+    out_split = early_sum[:, :split_rows]
+    query_split = late_sum[:, :split_rows]
     sizes = [
         main,
         model_blocks * extra,

time: 1190 us -> 1180 us (level)
  local copies, waits for them, and re-layouts: 234 us -> 188 us
  starting transfers between devices: 42.6 us -> 64.1 us
  other arithmetic: 117 us -> 134 us
    unnamed x439 -> x420, local copies, waits for them, and re-layouts: 153 us -> 111 us
    ppermute x42 -> x56, waiting for transfers between devices: 354 us -> 385 us  [partner(): return lax.ppermute(value, axis, pairs)]
    all_gather x3 -> x2, waiting for transfers between devices: 58.2 us -> 34 us  [joined(): return lax.all_gather(value, axis_names, axis=axis, tiled=True)]
    ppermute x42 -> x56, starting transfers between devices: 35.4 us -> 50.7 us  [partner(): return lax.ppermute(value, axis, pairs)]
    convert_element_type x16 -> x22, other arithmetic: 27.7 us -> 36.9 us  [low(): return value.astype(jnp.bfloat16)]
    reduce_scatter x7 -> x5, waiting for transfers between devices: 69.3 us -> 61.9 us  [scattered(): return lax.psum_scatter(value, axis_names, scatter_dimension=0, tiled=True)]
    ppermute x3 -> x6, waiting for transfers between devices: 59.4 us -> 64.7 us  [tp_rows(): lax.ppermute(value, 'tp', [(at, (at + shift) % size) for at in range(size)])]
  transfers between devices with their start and end apart: 57 -> 72, of which waited for: 22 -> 25; matrix products, arithmetic and copies ran while one was open for 33% -> 31% of each run, Pallas kernels for 0% -> 0%
where the time goes in v4:
time: 1180 us; the launch traced here: 1170 us
  waiting for transfers between devices  546 us (46%)
  matrix products  215 us (18%)
  local copies, waits for them, and re-layouts  188 us (16%)
  other arithmetic  134 us (11%)
  starting transfers between devices  64.1 us (5%)
  between operations  18 us (2%)
    ppermute x56, waiting for transfers between devices, partner(): return lax.ppermute(value, axis, pairs)  385 us
    unnamed x420, local copies, waits for them, and re-layouts  111 us
    dot_general x17, matrix products, times_transposed(): lax.dot_general(left_mat, right_mat, (((1,), (1,)), ((), ())), preferred_...  76.7 us
    dot_general x15, matrix products, matrix_multiply(): return jnp.dot(left_mat, right_mat, preferred_element_type=jnp.float32)  75.7 us
    ppermute x6, waiting for transfers between devices, tp_rows(): lax.ppermute(value, 'tp', [(at, (at + shift) % size) for at in range(size)])  64.7 us
    dot_general x13, matrix products, transposed_times(): lax.dot_general(left_mat, right_mat, (((0,), (0,)), ((), ())), preferred_...  63 us
    reduce_scatter x5, waiting for transfers between devices, scattered(): return lax.psum_scatter(value, axis_names, scatter_dimension=0, tiled=True)  61.9 us
    ppermute x56, starting transfers between devices, partner(): return lax.ppermute(value, axis, pairs)  50.7 us
  transfers between devices with their start and end apart: 72, of which 25 were waited for; matrix products, arithmetic and copies ran while one was open for 31% of the time, Pallas kernels for 0%

profile of v4, /device:TPU:0, one launch (start us, length us, event | category | flops | bytes accessed | tf_op | source)
XLA Modules:
  0.0 1174.4 jit_solution(16568747954673761075)
XLA Ops:
  58.4 37.8 %collective-permute-done.1 = bf16[128,2048]{1,0:T(8,128)(2,1)} collective-permute-done((bf16[128,2048]{1,0:T(8,128)(2,1)S(1)}, bf16[128,2048]{1,0:T(8,128)(2,1)}, u32[]{:S(2)}, u32[]{:S(2)}) %collective-permute-start.1) | collective-permute-done | bytes 524320 | tf_op jit(solution)/shard_map/ppermute | solution.py:187
  100.2 26.9 %collective-permute-done.22 = bf16[128,2048]{1,0:T(8,128)(2,1)} collective-permute-done((bf16[128,2048]{1,0:T(8,128)(2,1)S(1)}, bf16[128,2048]{1,0:T(8,128)(2,1)}, u32[]{:S(2)}, u32[]{:S(2)}) %collective-permute-start.22) | collective-permute-done | bytes 524320 | tf_op jit(solution)/shard_map/ppermute | solution.py:187
  153.2 55.1 %collective-permute-done.6 = bf16[576,2048]{1,0:T(8,128)(2,1)S(1)} collective-permute-done((bf16[576,2048]{1,0:T(8,128)(2,1)S(1)}, bf16[576,2048]{1,0:T(8,128)(2,1)S(1)}, u32[]{:S(2)}, u32[]{:S(2)}) %collective-permute-start.6) | collective-permute-done | bytes 2359328 | tf_op jit(solution)/shard_map/ppermute | solution.py:17
  212.2 54.4 %collective-permute-done.11 = bf16[576,2048]{1,0:T(8,128)(2,1)S(1)} collective-permute-done((bf16[576,2048]{1,0:T(8,128)(2,1)S(1)}, bf16[576,2048]{1,0:T(8,128)(2,1)S(1)}, u32[]{:S(2)}, u32[]{:S(2)}) %collective-permute-start.11) | collective-permute-done | bytes 2359328 | tf_op jit(solution)/shard_map/ppermute | solution.py:17
  271.9 45.2 %collective-permute-done.16 = bf16[576,2048]{1,0:T(8,128)(2,1)S(1)} collective-permute-done((bf16[576,2048]{1,0:T(8,128)(2,1)S(1)}, bf16[576,2048]{1,0:T(8,128)(2,1)S(1)}, u32[]{:S(2)}, u32[]{:S(2)}) %collective-permute-start.16) | collective-permute-done | bytes 2359328 | tf_op jit(solution)/shard_map/ppermute | solution.py:17
  323.5 19.0 %collective-permute-done.8 = bf16[288,2048]{1,0:T(8,128)(2,1)S(1)} collective-permute-done((bf16[288,2048]{1,0:T(8,128)(2,1)S(1)}, bf16[288,2048]{1,0:T(8,128)(2,1)S(1)}, u32[]{:S(2)}, u32[]{:S(2)}) %collective-permute-start.8) | collective-permute-done | bytes 1179680 | tf_op jit(solution)/shard_map/ppermute | solution.py:17
  344.2 23.6 %collective-permute-done.13 = bf16[288,2048]{1,0:T(8,128)(2,1)S(1)} collective-permute-done((bf16[288,2048]{1,0:T(8,128)(2,1)S(1)}, bf16[288,2048]{1,0:T(8,128)(2,1)S(1)}, u32[]{:S(2)}, u32[]{:S(2)}) %collective-permute-start.13) | collective-permute-done | bytes 1179680 | tf_op jit(solution)/shard_map/ppermute | solution.py:17
  369.7 21.1 %collective-permute-done.18 = bf16[288,2048]{1,0:T(8,128)(2,1)S(1)} collective-permute-done((bf16[288,2048]{1,0:T(8,128)(2,1)S(1)}, bf16[288,2048]{1,0:T(8,128)(2,1)S(1)}, u32[]{:S(2)}, u32[]{:S(2)}) %collective-permute-start.18) | collective-permute-done | bytes 1179680 | tf_op jit(solution)/shard_map/ppermute | solution.py:17
  424.3 17.1 %while.36 = (s32[]{:T(128)}, bf16[2,512,256]{1,2,0:T(8,128)(2,1)}, f32[2,512]{1,0:T(2,128)S(1)}, s32[]{:T(128)}, s32[]{:T(128)}, /*index=5*/s32[]{:T(128)}, s32[...) while((s32[]{:T(128)}, bf16[2,512,256]{1,2,0:T(8,128)(2,1)}, ...), condition=%wide.region_4.5_spmd.clone.clone.clone, body=%wide.region_1.4_spmd.clone.clone.sunk.clone | while | flops 542118912 | bytes 8154803 | solution.py:428
  463.7 27.2 %reduce-scatter.6.cloned.1.call-done = bf16[128,2048]{1,0:T(8,128)(2,1)} async-done(((bf16[512,2048]{1,0:T(8,128)(2,1)}), bf16[128,2048]{1,0:T(8,128)(2,1)}) %reduce-scatter.6.cloned.1.call-update) | async-done | bytes 524304 | tf_op jit(solution)/shard_map/reduce_scatter | solution.py:67
  510.7 34.0 %all-gather.9.cloned.1.call-done = bf16[512,2304]{1,0:T(8,128)(2,1)} async-done(((bf16[128,2304]{1,0:T(8,128)(2,1)}), bf16[512,2304]{1,0:T(8,128)(2,1)}) %all-gather.9.cloned.1.call-update) | async-done | bytes 2359312 | tf_op jit(solution)/shard_map/all_gather | solution.py:63
  544.8 15.5 %fusion.51 = f32[1024,2048]{1,0:T(8,128)} fusion(bf16[2304,2048]{1,0:T(8,128)(2,1)} %slice_dynamic-update-slice_fusion.12, bf16[512,2304]{1,0:T(8,128)(2,1)} %collective-permute-done.24, bf16[512,2304]{1,0:T(8,128)(2,1)S(1)} %copy-done.124), kind=kOutput, calls=%fused_computation.118 | convolution fusion | flops 9673113600 | bytes 22544384 | tf_op jit(solution)/shard_map/dot_general | solution.py:21
  560.6 16.3 %fusion.200 = f32[1024,2048]{1,0:T(8,128)} fusion(bf16[1024,2304]{1,0:T(8,128)(2,1)S(1)} %constant_dynamic-update-slice_fusion.33, bf16[2304,2048]{1,0:T(8,128)(2,1)} %slice_dynamic-update-slice_fusion.16), kind=kOutput, calls=%fused_computation.690 | convolution fusion | flops 9663676416 | bytes 22544384 | tf_op jit(solution)/shard_map/dot_general | solution.py:21
  576.9 23.9 %fusion.35 = (bf16[1024,2048]{1,0:T(8,128)(2,1)}, bf16[1024,2048]{1,0:T(8,128)(2,1)}, bf16[1024,2048]{1,0:T(8,128)(2,1)}) fusion(f32[1024,2048]{1,0:T(8,128)} %fusion.51, f32[1024,2048]{1,0:T(8,128)} %fusion.200, bf16[1024,2304]{1,0:T(8,128)(2,1)S(1)} %constant_dynamic-update-slice_fusion.33, bf16[2304,2048]{1,0:T(8,128)(2,1)} %slice_dynamic-update-slice_fusion.20), kind=kOutput, calls=%fused_computation.60 | convolution fusion | flops 9718202368 | bytes 43515904 | tf_op jit(solution)/shard_map/dot_general | solution.py:21
  600.9 15.6 %fusion.201 = f32[1024,2304]{1,0:T(8,128)} fusion(bf16[1024,2048]{1,0:T(8,128)(2,1)} %get-tuple-element.607, bf16[2304,2048]{1,0:T(8,128)(2,1)} %slice_dynamic-update-slice_fusion.12), kind=kOutput, calls=%fused_computation.691 | convolution fusion | flops 9663676416 | bytes 23068672 | tf_op jit(solution)/shard_map/dot_general | solution.py:25
  616.4 11.7 convolution_convert_fusion
  633.1 14.1 %fusion.202 = f32[1024,2304]{1,0:T(8,128)} fusion(bf16[1024,2048]{1,0:T(8,128)(2,1)S(1)} %copy-done.152, bf16[2304,2048]{1,0:T(8,128)(2,1)} %slice_dynamic-update-slice_fusion.16), kind=kOutput, calls=%fused_computation.692 | convolution fusion | flops 9663676416 | bytes 23068672 | tf_op jit(solution)/shard_map/dot_general | solution.py:25
  647.2 11.2 convolution_convert_fusion.1
  662.2 18.1 %convolution_add_fusion.2 = f32[1024,2304]{1,0:T(8,128)} fusion(f32[1024,2304]{1,0:T(8,128)} %fusion.202, bf16[1024,2048]{1,0:T(8,128)(2,1)} %get-tuple-element.605, bf16[2304,2048]{1,0:T(8,128)(2,1)} %slice_dynamic-update-slice_fusion.20), kind=kOutput, calls=%fused_computation.84 | convolution fusion | flops 9666035712 | bytes 32505856 | tf_op jit(solution)/shard_map/dot_general | solution.py:25
  720.1 12.1 %convolution_convert_fusion.2 = bf16[2304,2048]{1,0:T(8,128)(2,1)S(1)} fusion(bf16[1024,2304]{1,0:T(8,128)(2,1)} %copy-done.87, bf16[1024,2048]{1,0:T(8,128)(2,1)S(1)} %copy-done.154), kind=kOutput, calls=%fused_computation.52 | convolution fusion | flops 9668395008 | bytes 18350080 | tf_op jit(solution)/shard_map/dot_general | solution.py:31
  736.8 21.0 %reduce-scatter.10.cloned.1.call-done = bf16[128,2048]{1,0:T(8,128)(2,1)} async-done(((bf16[512,2048]{1,0:T(8,128)(2,1)}), bf16[128,2048]{1,0:T(8,128)(2,1)}) %reduce-scatter.10.cloned.1.call-update) | async-done | bytes 524304 | tf_op jit(solution)/shard_map/reduce_scatter | solution.py:67
  787.3 11.8 %collective-permute-done.42 = bf16[576,1024]{1,0:T(8,128)(2,1)S(1)} collective-permute-done((bf16[576,1024]{1,0:T(8,128)(2,1)S(1)}, bf16[576,1024]{1,0:T(8,128)(2,1)S(1)}, u32[]{:S(2)}, u32[]{:S(2)}) %collective-permute-start.42) | collective-permute-done | bytes 1179680 | tf_op jit(solution)/shard_map/ppermute | solution.py:17
  809.9 14.6 %collective-permute-done.55 = bf16[576,1024]{1,0:T(8,128)(2,1)} collective-permute-done((bf16[576,1024]{1,0:T(8,128)(2,1)}, bf16[576,1024]{1,0:T(8,128)(2,1)}, u32[]{:S(2)}, u32[]{:S(2)}) %collective-permute-start.55) | collective-permute-done | bytes 1179680 | tf_op jit(solution)/shard_map/ppermute | solution.py:17
  827.5 23.8 %collective-permute-done.57 = bf16[576,1024]{1,0:T(8,128)(2,1)} collective-permute-done((bf16[576,1024]{1,0:T(8,128)(2,1)}, bf16[576,1024]{1,0:T(8,128)(2,1)}, u32[]{:S(2)}, u32[]{:S(2)}) %collective-permute-start.57) | collective-permute-done | bytes 1179680 | tf_op jit(solution)/shard_map/ppermute | solution.py:17
  859.3 15.7 %collective-permute-done.48 = bf16[576,1024]{1,0:T(8,128)(2,1)S(1)} collective-permute-done((bf16[576,1024]{1,0:T(8,128)(2,1)}, bf16[576,1024]{1,0:T(8,128)(2,1)S(1)}, u32[]{:S(2)}, u32[]{:S(2)}) %collective-permute-start.48) | collective-permute-done | bytes 1179680 | tf_op jit(solution)/shard_map/ppermute | solution.py:17
  878.0 23.8 %collective-permute-done.50 = bf16[576,1024]{1,0:T(8,128)(2,1)S(1)} collective-permute-done((bf16[576,1024]{1,0:T(8,128)(2,1)}, bf16[576,1024]{1,0:T(8,128)(2,1)S(1)}, u32[]{:S(2)}, u32[]{:S(2)}) %collective-permute-start.50) | collective-permute-done | bytes 1179680 | tf_op jit(solution)/shard_map/ppermute | solution.py:17
  902.3 23.2 %collective-permute-done.53 = bf16[576,1024]{1,0:T(8,128)(2,1)S(1)} collective-permute-done((bf16[576,1024]{1,0:T(8,128)(2,1)}, bf16[576,1024]{1,0:T(8,128)(2,1)S(1)}, u32[]{:S(2)}, u32[]{:S(2)}) %collective-permute-start.53) | collective-permute-done | bytes 1179680 | tf_op jit(solution)/shard_map/ppermute | solution.py:17
  929.6 20.9 %collective-permute-done.43 = bf16[576,1024]{1,0:T(8,128)(2,1)S(1)} collective-permute-done((bf16[576,1024]{1,0:T(8,128)(2,1)}, bf16[576,1024]{1,0:T(8,128)(2,1)S(1)}, u32[]{:S(2)}, u32[]{:S(2)}) %collective-permute-start.43) | collective-permute-done | bytes 1179680 | tf_op jit(solution)/shard_map/ppermute | solution.py:17
  1003.0 31.7 %while.37 = (s32[]{:T(128)}, f32[1024,256]{1,0:T(8,128)}, f32[1024,256]{1,0:T(8,128)}, f32[2,512,256]{1,2,0:T(8,128)}, s32[]{:T(128)}, /*index=5*/s32[]{:T(128)}...) while((s32[]{:T(128)}, f32[1024,256]{1,0:T(8,128)}, ...), condition=%wide.region_12.13_spmd.clone.clone.clone, body=%wide.region_10.12_spmd.clone.clone.sunk.clone | while | flops 1348998144 | bytes 33572160 | solution.py:508
  1118.0 7.3 collective-permute-done.36
  1126.8 6.5 collective-permute-done.35
  1149.9 13.7 %reduce-scatter.14.cloned.1.call-done = bf16[1,416,256]{2,1,0:T(8,128)(2,1)} async-done(((bf16[4,416,256]{2,1,0:T(8,128)(2,1)}), bf16[1,416,256]{2,1,0:T(8,128)(2,1)}) %reduce-scatter.14.cloned.1.call-update) | async-done | bytes 213008 | tf_op jit(solution)/shard_map/reduce_scatter | solution.py:67
  (841 shorter events, 482.8 us)
Async XLA Ops:
  7.2 390.8 %all-gather.13.cloned.1.call-start = ((), (), s32[]{:S(2)}) async-start(), calls=%async_computation.12 | async-start | bytes 3649536 | tf_op jit(solution)/shard_map/all_gather | solution.py:90
  12.4 402.2 %all-gather.15.cloned.1.call-start = ((), (), s32[]{:S(2)}) async-start(), calls=%async_computation.13 | async-start | bytes 5308416 | tf_op jit(solution)/shard_map/all_gather | solution.py:353
  15.4 426.0 %all-gather.17.cloned.1.call-start = ((), (), s32[]{:S(2)}) async-start(), calls=%async_computation.14 | async-start | bytes 3244032 | tf_op jit(solution)/shard_map/all_gather | solution.py:330
  20.6 75.6 %collective-permute-start.1 = (bf16[128,2048]{1,0:T(8,128)(2,1)S(1)}, bf16[128,2048]{1,0:T(8,128)(2,1)}, u32[]{:S(2)}, u32[]{:S(2)}) collective-permute-start(bf16[128,2048]{1,0:T(8,128)(2,1)S(1)} %copy-done.1), channel_id=1, source_target_pairs={{0,2},{1,3},{2,0},{3,1},{4,6},{5,7},{6,4},{7,5},{8,10},{9,11},{10,... | collective-permute-start | bytes 1572872 | tf_op jit(solution)/shard_map/ppermute | solution.py:187
  20.6 76.7 %collective-permute-start.2 = (bf16[128,2048]{1,0:T(8,128)(2,1)S(1)}, bf16[128,2048]{1,0:T(8,128)(2,1)}, u32[]{:S(2)}, u32[]{:S(2)}) collective-permute-start(bf16[128,2048]{1,0:T(8,128)(2,1)S(1)} %copy-done.1), channel_id=1, source_target_pairs={{0,1},{1,2},{2,3},{3,0},{4,5},{5,6},{6,7},{7,4},{8,9},{9,10},{10,1... | collective-permute-start | bytes 1572872 | tf_op jit(solution)/shard_map/ppermute | solution.py:187
  21.6 77.4 %collective-permute-start.21 = (bf16[128,2048]{1,0:T(8,128)(2,1)S(1)}, bf16[128,2048]{1,0:T(8,128)(2,1)}, u32[]{:S(2)}, u32[]{:S(2)}) collective-permute-start(bf16[128,2048]{1,0:T(8,128)(2,1)S(1)} %copy-done.37), channel_id=1, source_target_pairs={{0,3},{1,0},{2,1},{3,2},{4,7},{5,4},{6,5},{7,6},{8,11},{9,8},{10,9... | collective-permute-start | bytes 1572872 | tf_op jit(solution)/shard_map/ppermute | solution.py:187
  24.4 102.6 %collective-permute-start.22 = (bf16[128,2048]{1,0:T(8,128)(2,1)S(1)}, bf16[128,2048]{1,0:T(8,128)(2,1)}, u32[]{:S(2)}, u32[]{:S(2)}) collective-permute-start(bf16[128,2048]{1,0:T(8,128)(2,1)S(1)} %copy-done.37), channel_id=1, source_target_pairs={{0,2},{1,3},{2,0},{3,1},{4,6},{5,7},{6,4},{7,5},{8,10},{9,11},{10,... | collective-permute-start | bytes 1572872 | tf_op jit(solution)/shard_map/ppermute | solution.py:187
  26.3 464.5 %reduce-scatter.6.cloned.1.call-start = ((), (), s32[]{:S(2)}) async-start(), calls=%async_computation.5 | async-start | bytes 2621440 | tf_op jit(solution)/shard_map/reduce_scatter | solution.py:67
  54.7 73.4 %collective-permute-start.23 = (bf16[128,2048]{1,0:T(8,128)(2,1)S(1)}, bf16[128,2048]{1,0:T(8,128)(2,1)S(1)}, u32[]{:S(2)}, u32[]{:S(2)}) collective-permute-start(bf16[128,2048]{1,0:T(8,128)(2,1)S(1)} %copy-done.37), channel_id=1, source_target_pairs={{0,1},{1,2},{2,3},{3,0},{4,5},{5,6},{6,7},{7,4},{8,9},{9,10},{10,1... | collective-permute-start | bytes 1572872 | tf_op jit(solution)/shard_map/ppermute | solution.py:187
  144.7 121.9 %collective-permute-start.11 = (bf16[576,2048]{1,0:T(8,128)(2,1)S(1)}, bf16[576,2048]{1,0:T(8,128)(2,1)S(1)}, u32[]{:S(2)}, u32[]{:S(2)}) collective-permute-start(bf16[576,2048]{1,0:T(8,128)(2,1)S(1)} %maximum_select_fusion.4), channel_id=1, source_target_pairs={{0,8},{4,12},{8,0},{12,4},{16,24},{20,28},{24,16},{28,20},{1,9},{5... | collective-permute-start | bytes 7077896 | tf_op jit(solution)/shard_map/ppermute | solution.py:17
  146.7 123.2 %collective-permute-start.12 = (bf16[576,2048]{1,0:T(8,128)(2,1)S(1)}, bf16[576,2048]{1,0:T(8,128)(2,1)S(1)}, u32[]{:S(2)}, u32[]{:S(2)}) collective-permute-start(bf16[576,2048]{1,0:T(8,128)(2,1)S(1)} %maximum_select_fusion.4), channel_id=1, source_target_pairs={{0,16},{4,20},{8,24},{12,28},{16,0},{20,4},{24,8},{28,12},{1,17},{... | collective-permute-start | bytes 7077896 | tf_op jit(solution)/shard_map/ppermute | solution.py:17
  150.1 167.0 %collective-permute-start.16 = (bf16[576,2048]{1,0:T(8,128)(2,1)S(1)}, bf16[576,2048]{1,0:T(8,128)(2,1)S(1)}, u32[]{:S(2)}, u32[]{:S(2)}) collective-permute-start(bf16[576,2048]{1,0:T(8,128)(2,1)S(1)} %maximum_select_fusion.5), channel_id=1, source_target_pairs={{0,8},{4,12},{8,0},{12,4},{16,24},{20,28},{24,16},{28,20},{1,9},{5... | collective-permute-start | bytes 7077896 | tf_op jit(solution)/shard_map/ppermute | solution.py:17
  208.2 112.1 %collective-permute-start.17 = (bf16[576,2048]{1,0:T(8,128)(2,1)S(1)}, bf16[576,2048]{1,0:T(8,128)(2,1)S(1)}, u32[]{:S(2)}, u32[]{:S(2)}) collective-permute-start(bf16[576,2048]{1,0:T(8,128)(2,1)S(1)} %maximum_select_fusion.5), channel_id=1, source_target_pairs={{0,16},{4,20},{8,24},{12,28},{16,0},{20,4},{24,8},{28,12},{1,17},{... | collective-permute-start | bytes 7077896 | tf_op jit(solution)/shard_map/ppermute | solution.py:17
  211.2 131.3 %collective-permute-start.8 = (bf16[288,2048]{1,0:T(8,128)(2,1)S(1)}, bf16[288,2048]{1,0:T(8,128)(2,1)S(1)}, u32[]{:S(2)}, u32[]{:S(2)}) collective-permute-start(bf16[288,2048]{1,0:T(8,128)(2,1)S(1)} %slice.1451), channel_id=1, source_target_pairs={{0,16},{4,20},{8,24},{12,28},{16,0},{20,4},{24,8},{28,12},{1,17},{... | collective-permute-start | bytes 3538952 | tf_op jit(solution)/shard_map/ppermute | solution.py:17
  266.6 101.3 %collective-permute-start.9 = (bf16[288,2048]{1,0:T(8,128)(2,1)S(1)}, bf16[288,2048]{1,0:T(8,128)(2,1)S(1)}, u32[]{:S(2)}, u32[]{:S(2)}) collective-permute-start(bf16[288,2048]{1,0:T(8,128)(2,1)S(1)} %slice.1452), channel_id=1, source_target_pairs={{0,8},{4,12},{8,0},{12,4},{16,24},{20,28},{24,16},{28,20},{1,9},{5... | collective-permute-start | bytes 3538952 | tf_op jit(solution)/shard_map/ppermute | solution.py:17
  269.9 97.9 %collective-permute-start.13 = (bf16[288,2048]{1,0:T(8,128)(2,1)S(1)}, bf16[288,2048]{1,0:T(8,128)(2,1)S(1)}, u32[]{:S(2)}, u32[]{:S(2)}) collective-permute-start(bf16[288,2048]{1,0:T(8,128)(2,1)S(1)} %slice.1467), channel_id=1, source_target_pairs={{0,16},{4,20},{8,24},{12,28},{16,0},{20,4},{24,8},{28,12},{1,17},{... | collective-permute-start | bytes 3538952 | tf_op jit(solution)/shard_map/ppermute | solution.py:17
  317.2 74.8 %collective-permute-start.14 = (bf16[288,2048]{1,0:T(8,128)(2,1)S(1)}, bf16[288,2048]{1,0:T(8,128)(2,1)S(1)}, u32[]{:S(2)}, u32[]{:S(2)}) collective-permute-start(bf16[288,2048]{1,0:T(8,128)(2,1)S(1)} %slice.1468), channel_id=1, source_target_pairs={{0,8},{4,12},{8,0},{12,4},{16,24},{20,28},{24,16},{28,20},{1,9},{5... | collective-permute-start | bytes 3538952 | tf_op jit(solution)/shard_map/ppermute | solution.py:17
  320.3 70.5 %collective-permute-start.18 = (bf16[288,2048]{1,0:T(8,128)(2,1)S(1)}, bf16[288,2048]{1,0:T(8,128)(2,1)S(1)}, u32[]{:S(2)}, u32[]{:S(2)}) collective-permute-start(bf16[288,2048]{1,0:T(8,128)(2,1)S(1)} %slice.1483), channel_id=1, source_target_pairs={{0,16},{4,20},{8,24},{12,28},{16,0},{20,4},{24,8},{28,12},{1,17},{... | collective-permute-start | bytes 3538952 | tf_op jit(solution)/shard_map/ppermute | solution.py:17
  448.3 96.4 %all-gather.9.cloned.1.call-start = ((), (), s32[]{:S(2)}) async-start(), calls=%async_computation.6 | async-start | bytes 2949120 | tf_op jit(solution)/shard_map/all_gather | solution.py:63
  495.4 262.5 %reduce-scatter.10.cloned.1.call-start = ((), (), s32[]{:S(2)}) async-start(), calls=%async_computation.8 | async-start | bytes 2621440 | tf_op jit(solution)/shard_map/reduce_scatter | solution.py:67
  689.0 81.2 %collective-permute-start.56 = (bf16[576,1024]{1,0:T(8,128)(2,1)}, bf16[576,1024]{1,0:T(8,128)(2,1)}, u32[]{:S(2)}, u32[]{:S(2)}) collective-permute-start(bf16[576,1024]{1,0:T(8,128)(2,1)} %get-tuple-element.665), channel_id=1, source_target_pairs={{0,8},{4,12},{8,0},{12,4},{16,24},{20,28},{24,16},{28,20},{1,9},{5... | collective-permute-start | bytes 3538952 | tf_op jit(solution)/shard_map/ppermute | solution.py:17
  690.5 81.3 %collective-permute-start.59 = (bf16[576,1024]{1,0:T(8,128)(2,1)}, bf16[576,1024]{1,0:T(8,128)(2,1)}, u32[]{:S(2)}, u32[]{:S(2)}) collective-permute-start(bf16[576,1024]{1,0:T(8,128)(2,1)} %get-tuple-element.664), channel_id=1, source_target_pairs={{0,16},{4,20},{8,24},{12,28},{16,0},{20,4},{24,8},{28,12},{1,17},{... | collective-permute-start | bytes 3538952 | tf_op jit(solution)/shard_map/ppermute | solution.py:17
  693.6 86.6 %collective-permute-start.49 = (bf16[576,1024]{1,0:T(8,128)(2,1)}, bf16[576,1024]{1,0:T(8,128)(2,1)}, u32[]{:S(2)}, u32[]{:S(2)}) collective-permute-start(bf16[576,1024]{1,0:T(8,128)(2,1)} %get-tuple-element.669), channel_id=1, source_target_pairs={{0,8},{4,12},{8,0},{12,4},{16,24},{20,28},{24,16},{28,20},{1,9},{5... | collective-permute-start | bytes 3538952 | tf_op jit(solution)/shard_map/ppermute | solution.py:17
  694.2 89.6 %collective-permute-start.52 = (bf16[576,1024]{1,0:T(8,128)(2,1)}, bf16[576,1024]{1,0:T(8,128)(2,1)}, u32[]{:S(2)}, u32[]{:S(2)}) collective-permute-start(bf16[576,1024]{1,0:T(8,128)(2,1)} %get-tuple-element.668), channel_id=1, source_target_pairs={{0,16},{4,20},{8,24},{12,28},{16,0},{20,4},{24,8},{28,12},{1,17},{... | collective-permute-start | bytes 3538952 | tf_op jit(solution)/shard_map/ppermute | solution.py:17
  713.1 92.0 %collective-permute-start.20 = (bf16[512,2048]{1,0:T(8,128)(2,1)}, bf16[512,2048]{1,0:T(8,128)(2,1)}, u32[]{:S(2)}, u32[]{:S(2)}) collective-permute-start(bf16[512,2048]{1,0:T(8,128)(2,1)} %slice.2546), channel_id=1, source_target_pairs={{0,4},{4,0},{8,12},{12,8},{16,20},{20,16},{24,28},{28,24},{1,5},{5... | collective-permute-start | bytes 6291464 | tf_op jit(solution)/shard_map/ppermute | solution.py:17
  715.2 257.5 %all-gather.11.cloned.1.call-start = ((), (), s32[]{:S(2)}) async-start(), calls=%async_computation.9 | async-start | bytes 2621440 | tf_op jit(solution)/shard_map/all_gather | solution.py:63
  762.1 323.9 %reduce-scatter.8.cloned.1.call-start = ((), (), s32[]{:S(2)}) async-start(), calls=%async_computation.7 | async-start | bytes 2621440 | tf_op jit(solution)/shard_map/reduce_scatter | solution.py:67
  809.5 335.8 %reduce-scatter.12.cloned.1.call-start = ((), (), s32[]{:S(2)}) async-start(), calls=%async_computation.10 | async-start | bytes 2621440 | tf_op jit(solution)/shard_map/reduce_scatter | solution.py:67
  826.1 103.0 %collective-permute-start.41 = (bf16[576,1024]{1,0:T(8,128)(2,1)}, bf16[576,1024]{1,0:T(8,128)(2,1)S(1)}, u32[]{:S(2)}, u32[]{:S(2)}) collective-permute-start(bf16[576,1024]{1,0:T(8,128)(2,1)} %fusion.101), channel_id=1, source_target_pairs={{0,8},{4,12},{8,0},{12,4},{16,24},{20,28},{24,16},{28,20},{1,9},{5... | collective-permute-start | bytes 3538952 | tf_op jit(solution)/shard_map/ppermute | solution.py:17
  852.8 72.8 %collective-permute-start.53 = (bf16[576,1024]{1,0:T(8,128)(2,1)}, bf16[576,1024]{1,0:T(8,128)(2,1)S(1)}, u32[]{:S(2)}, u32[]{:S(2)}) collective-permute-start(bf16[576,1024]{1,0:T(8,128)(2,1)} %add_convert_fusion.5), channel_id=1, source_target_pairs={{0,8},{4,12},{8,0},{12,4},{16,24},{20,28},{24,16},{28,20},{1,9},{5... | collective-permute-start | bytes 3538952 | tf_op jit(solution)/shard_map/ppermute | solution.py:17
  876.5 74.0 %collective-permute-start.43 = (bf16[576,1024]{1,0:T(8,128)(2,1)}, bf16[576,1024]{1,0:T(8,128)(2,1)S(1)}, u32[]{:S(2)}, u32[]{:S(2)}) collective-permute-start(bf16[576,1024]{1,0:T(8,128)(2,1)} %add_convert_fusion.8), channel_id=1, source_target_pairs={{0,16},{4,20},{8,24},{12,28},{16,0},{20,4},{24,8},{28,12},{1,17},{... | collective-permute-start | bytes 3538952 | tf_op jit(solution)/shard_map/ppermute | solution.py:17
  1088.1 75.5 %reduce-scatter.14.cloned.1.call-start = ((), (), s32[]{:S(2)}) async-start(), calls=%async_computation.11 | async-start | bytes 1064960 | tf_op jit(solution)/shard_map/reduce_scatter | solution.py:67
  (206 other events, 3685.0 us)
Sparse Core Ops, SparseCore 0:
  12.5 106.8 all-gather.12
  121.3 55.6 all-gather.14
  179.8 65.4 all-gather.16
  448.5 42.3 reduce-scatter.5
  495.5 49.1 all-gather.8
  715.3 42.5 reduce-scatter.9
  762.3 44.8 all-gather.10
  809.6 42.3 reduce-scatter.7
  1088.2 41.7 reduce-scatter.11
  1140.7 22.8 reduce-scatter.13
